TPU v7x, 32 devices: a whole 2x2x4 slice. The times are simulated.
32 devices in a mesh: blk: 8 (over z, y), grid: 4 (over x, core).
Axes of the slice: x: 2, y: 2, z: 4, core: 2. Of those that a mesh axis runs over, the one named last changes fastest.
Arguments:
- orbitals: bfloat16 [32, 64, 4096], P('blk', 'grid'), may hold values from -60 to 60
Outputs:
- rotated: bfloat16 [32, 64, 4096], P(None, 'grid', 'blk')
- intersection: float32 [32, 32], replicated
All inputs are finite; a program needn't handle non-finite values.
Results may differ from a plain program's by a relative error of at most 0.0085.
Values may be sent and summed in bfloat16 or wider, within the bound.
No kernel may reach another device: no remote copies, remote signals or barrier semaphores. Data moves between devices by JAX's collectives and lax.ppermute only.
A program may use at most 128 MiB of HBM per device.

v0:
```python
import functools

import jax
import jax.numpy as jnp
from jax import lax
from jax.experimental import pallas as pl
from jax.experimental.pallas import tpu as pltpu
from jax.sharding import PartitionSpec as P

NX = 64
NY = 64
NZ = 64
STEPS = 2

exchange_fraction = 0.25
screening = 1.0

BF = jnp.bfloat16
F32 = jnp.float32
VMEM = pl.BlockSpec(memory_space=pltpu.VMEM)
SMEM = pl.BlockSpec(memory_space=pltpu.SMEM)
LANES = 128
ROW_PAD = 8
QUAD = 4
UNROLL = 4


def product(a, b):
    return jnp.dot(a, b, preferred_element_type=F32)


def sine_rows(length, index_in):
    modes = jnp.arange(length).astype(F32)
    angle = jnp.pi * (modes[:, None] + 1.0) * (index_in.astype(F32)[None, :] + 1.0) / (length + 1)
    return (jnp.sqrt(2.0 / (length + 1)) * jnp.sin(angle)).astype(BF)


def block_diagonal(table, copies):
    n = table.shape[0]
    eye = jnp.eye(copies, dtype=BF)
    return (eye[:, None, :, None] * table[None, :, None, :]).reshape(copies * n, copies * n)


def eigen_values(length):
    index = jnp.arange(length).astype(F32)
    return 2.0 - 2.0 * jnp.cos(jnp.pi * (index + 1.0) / (length + 1))


def kernel_weights():
    values_x = eigen_values(NX)
    values_y = eigen_values(NY)
    values_z = eigen_values(NZ)
    weights = 1.0 / (
        screening + values_x[:, None, None] + values_y[None, :, None] + values_z[None, None, :]
    )
    return weights.reshape(NX * NY, NZ)


def block_kernel(slabs, final, rest):
    own = rest[:slabs]
    src = rest[slabs:2 * slabs]
    rest = rest[2 * slabs:]
    pos_ref, tz_ref, tx_ref, txb_ref, ty_ref, w_ref = rest[:6]
    rest = rest[6:]
    if final:
        acc_ref, out_ref, grouped_ref, work_ref = rest
    else:
        out_ref, grouped_ref, work_ref = rest
    count = src[0].shape[0]
    rows = src[0].shape[1]
    halves = count * NZ // LANES
    width = QUAD * NZ
    pitch = work_ref.shape[1] // NY

    def tile(refs, lead, off, size):
        parts = [r[lead + (slice(None), pl.ds(off, size))] for r in refs]
        return jnp.concatenate(parts, 0)

    def load_rows(first):
        parts = []
        for q in range(QUAD):
            at = pl.multiple_of((first + q) * pitch, 8)
            parts.append(
                jnp.concatenate([work_ref[h, pl.ds(at, NX), :] for h in range(halves)], 1)
            )
        return jnp.concatenate(parts, 0)

    def forward(t, carry):
        off = pl.multiple_of(t * width, width)
        at = pl.multiple_of(t * QUAD * NX, QUAD * NX)
        mine = tile(own, (), off, width)
        others = [tile(src, (j,), off, width) for j in range(count)]
        pairs = [mine * other for other in others]
        cut = [slice(q * NZ, (q + 1) * NZ) for q in range(QUAD)]
        density = jnp.concatenate(
            [jnp.concatenate([p[:, c] for p in pairs], 1) for c in cut], 0)
        grouped_ref[pl.ds(at, QUAD * NX), :] = jnp.concatenate(
            [jnp.concatenate([o[:, c] for o in others], 1) for c in cut], 0)
        first = product(density, tz_ref[...]).astype(BF)
        modes = product(tx_ref[...], first)
        for q in range(QUAD):
            to = pl.multiple_of((t * QUAD + q) * pitch, 8)
            for h in range(halves):
                work_ref[h, pl.ds(to, NX), :] = modes[q * NX:(q + 1) * NX, h * LANES:(h + 1) * LANES]
        return carry

    def solve(t, carry):
        at = pl.multiple_of(t * QUAD * NY, QUAD * NY)
        modes = jnp.concatenate([
            jnp.concatenate(
                [work_ref[h, pl.ds(t * QUAD + q, NY, stride=pitch), :] for h in range(halves)], 1)
            for q in range(QUAD)], 0).astype(BF)
        weights = jnp.concatenate([w_ref[pl.ds(at, QUAD * NY), :]] * halves, 1)
        scaled = (product(ty_ref[...], modes) * weights).astype(BF)
        back = product(ty_ref[...], scaled)
        for q in range(QUAD):
            for h in range(halves):
                work_ref[h, pl.ds(t * QUAD + q, NY, stride=pitch), :] = (
                    back[q * NY:(q + 1) * NY, h * LANES:(h + 1) * LANES])
        return carry

    lane = lax.broadcasted_iota(jnp.int32, (NX, LANES), 1)
    per_tile = LANES // NZ

    def backward(t, carry):
        at = pl.multiple_of(t * QUAD * NX, QUAD * NX)
        third = product(txb_ref[...], load_rows(t * QUAD).astype(BF)).astype(BF)
        potential = product(third, tz_ref[...])
        terms = potential * grouped_ref[pl.ds(at, QUAD * NX), :].astype(F32)
        total = terms[:, :LANES]
        for h in range(1, halves):
            total = total + terms[:, h * LANES:(h + 1) * LANES]
        total = total + pltpu.roll(total, NZ, 1)
        for q in range(0, QUAD, per_tile):
            exchange = jnp.where(
                lane < NZ, total[q * NX:(q + 1) * NX], total[(q + 1) * NX:(q + 2) * NX])
            off = pl.multiple_of((t * QUAD + q) * NZ, LANES)
            if not final:
                out_ref[:, pl.ds(off, LANES)] = exchange
                continue
            exchange = exchange + acc_ref[:, pl.ds(off, LANES)]
            mine = tile(own, (), off, LANES).astype(F32)
            updated = (mine - exchange_fraction * exchange).astype(BF)
            for r in range(slabs):
                part = updated[r * rows:(r + 1) * rows]
                if len(out_ref.shape) == 4:
                    share = out_ref.shape[3] // LANES
                    index = (t * QUAD + q) * NZ // LANES
                    to = pl.multiple_of((index % share) * LANES, LANES)
                    out_ref[index // share, pos_ref[r], :, pl.ds(to, LANES)] = part
                else:
                    out_ref[pos_ref[r], :, pl.ds(off, LANES)] = part
        return carry

    lax.fori_loop(0, NY // QUAD, forward, 0, unroll=UNROLL)
    lax.fori_loop(0, NX // QUAD, solve, 0, unroll=UNROLL)
    lax.fori_loop(0, NY // QUAD, backward, 0, unroll=UNROLL)


def add_block(own, src, tables, acc, out_shape):
    slabs = len(own)
    count = src[0].shape[0]
    final = acc is not None
    lead = () if acc is None else (acc,)
    flops = 12 * count * NX * NY * NZ * NZ * 4
    return pl.pallas_call(
        lambda *refs: block_kernel(slabs, final, refs),
        out_shape=out_shape,
        in_specs=[VMEM] * (2 * slabs) + [SMEM] + [VMEM] * (5 + len(lead)),
        out_specs=VMEM,
        scratch_shapes=[
            pltpu.VMEM((NY * NX, count * NZ), BF),
            pltpu.VMEM((count * NZ // LANES, NY * (NX + ROW_PAD), LANES), F32),
        ],
        compiler_params=pltpu.CompilerParams(vmem_limit_bytes=40 * 1024 * 1024),
        cost_estimate=pl.CostEstimate(flops=flops, bytes_accessed=8 << 20, transcendentals=0),
    )(*own, *src, *tables, *lead)


def gram_kernel(x_ref, out_ref):
    orbs, rows, lanes = x_ref.shape
    flat = x_ref[...].reshape(orbs * rows, lanes)
    full = lax.dot_general(flat, flat, (((1,), (1,)), ((), ())), preferred_element_type=F32)
    down = lax.broadcasted_iota(jnp.int32, full.shape, 0)
    along = lax.broadcasted_iota(jnp.int32, full.shape, 1)
    full = jnp.where(down % rows == along % rows, full, 0.0)
    half = jnp.sum(full.reshape(orbs, rows, orbs * rows), axis=1)
    out_ref[...] = jnp.sum(half.T.reshape(orbs, rows, orbs), axis=1)


def rotate_kernel(scale, parts_ref, x_ref, out_ref, gram_ref):
    orbs, rows, lanes = x_ref.shape
    gram = jnp.sum(parts_ref[...], axis=0) * scale
    gram_ref[...] = gram
    down = lax.broadcasted_iota(jnp.int32, (orbs, orbs), 0)
    along = lax.broadcasted_iota(jnp.int32, (orbs, orbs), 1)
    eye = jnp.where(down == along, 1.0, 0.0)
    work = jnp.concatenate([gram, eye], 1)
    row = lax.broadcasted_iota(jnp.int32, (orbs, 1), 0)
    pivots = jnp.zeros((orbs, 1), F32)
    for k in range(orbs):
        column = work[:, k:k + 1]
        pivot = work[k:k + 1, k:k + 1]
        pivots = jnp.where(row == k, pivot, pivots)
        factor = jnp.where(row > k, column / pivot, 0.0)
        work = work - factor * work[k:k + 1, :]
    inverse = (work[:, orbs:] * (1.0 / jnp.sqrt(pivots))).astype(BF)
    tall = lax.broadcasted_iota(jnp.int32, (orbs * rows, orbs), 0) // rows
    wide = lax.broadcasted_iota(jnp.int32, (orbs * rows, orbs), 1)
    pick = jnp.where(tall == wide, 1.0, 0.0).astype(BF)
    spread = product(pick, inverse).astype(BF)
    spread = lax.dot_general(spread, pick, (((1,), (1,)), ((), ())), preferred_element_type=F32)
    i = lax.broadcasted_iota(jnp.int32, spread.shape, 0)
    j = lax.broadcasted_iota(jnp.int32, spread.shape, 1)
    spread = jnp.where(i % rows == j % rows, spread, 0.0).astype(BF)
    flat = x_ref[...].reshape(orbs * rows, lanes)
    out_ref[...] = product(spread, flat).astype(BF).reshape(orbs, rows, lanes)


def exchanged(x, axis, by):
    return lax.ppermute(x, axis, [(i, i ^ by) for i in range(lax.axis_size(axis))])


def gathered(slab):
    size = lax.axis_size("grid")
    slabs = {0: slab}
    bit = size // 2
    while bit:
        for r in list(slabs):
            slabs[r | bit] = exchanged(slabs[r], "grid", bit)
        bit //= 2
    return [slabs[r] for r in range(size)]


def body(orbitals):
    orb_count, slab_rows, plane_cells = orbitals.shape
    slabs = lax.axis_size("grid")
    blocks = lax.axis_size("blk")
    assert orb_count == slabs and slab_rows * slabs == NX and blocks % 2 == 0 and STEPS == 2
    grid_index = lax.axis_index("grid")
    order = jnp.arange(slabs) ^ grid_index

    far = lax.ppermute(orbitals, "blk", [(i, (i + 2) % blocks) for i in range(blocks)])
    own = [lax.dynamic_index_in_dim(orbitals, grid_index, 0, keepdims=False)]
    for r in range(1, slabs):
        piece = lax.dynamic_index_in_dim(orbitals, grid_index ^ r, 0, keepdims=False)
        own.append(exchanged(piece, "grid", r))
    near = exchanged(jnp.where(lax.axis_index("blk") % 2 == 0, orbitals, far), "blk", 1)
    far = gathered(far)
    near = gathered(near)

    cells = jnp.arange(NX)
    here = (order[:, None] * slab_rows + jnp.arange(slab_rows)[None, :]).reshape(NX)
    table_x = sine_rows(NX, here)
    table_z = sine_rows(NZ, cells[:NZ])
    weights = jnp.concatenate([kernel_weights()] * (LANES // NZ), 1)
    tables = (
        order.astype(jnp.int32),
        block_diagonal(table_z, orb_count),
        block_diagonal(table_x, QUAD),
        block_diagonal(table_x.T, QUAD),
        block_diagonal(sine_rows(NY, cells[:NY]), QUAD),
        weights,
    )
    acc = add_block(own, far, tables, None, jax.ShapeDtypeStruct((NX, plane_cells), F32))
    chunk = plane_cells // blocks
    if chunk % LANES == 0:
        shape = (blocks, slabs, slab_rows, chunk)
    else:
        shape = (slabs, slab_rows, plane_cells)
    updated = add_block(own, near, tables, acc, jax.ShapeDtypeStruct(shape, BF))
    if chunk % LANES:
        updated = updated.reshape(slabs, slab_rows, blocks, chunk).transpose(2, 0, 1, 3)
    updated = updated.reshape(blocks * slabs, slab_rows, chunk)
    cellwise = lax.all_to_all(updated, ("blk", "grid"), 0, 0, tiled=True)

    devices = blocks * slabs
    cell_count = NX * NY * NZ
    if devices * slab_rows <= 512 and chunk % LANES == 0:
        local = pl.pallas_call(
            gram_kernel,
            out_shape=jax.ShapeDtypeStruct((devices, devices), F32),
            in_specs=[VMEM],
            out_specs=VMEM,
        )(cellwise)
        parts = lax.all_to_all(
            jnp.broadcast_to(local[None], (devices,) + local.shape), ("blk", "grid"), 0, 0)
        return pl.pallas_call(
            functools.partial(rotate_kernel, 1.0 / cell_count),
            out_shape=(
                jax.ShapeDtypeStruct(cellwise.shape, BF),
                jax.ShapeDtypeStruct(local.shape, F32),
            ),
            in_specs=[VMEM, VMEM],
            out_specs=(VMEM, VMEM),
        )(parts, cellwise)
    flat = cellwise.reshape(devices, slab_rows * chunk)
    local = jnp.dot(flat, flat.T, preferred_element_type=F32)
    intersection = lax.psum(local, ("blk", "grid")) / cell_count
    factor = jnp.linalg.cholesky(intersection)
    identity = jnp.eye(devices, dtype=F32)
    inverse = jax.scipy.linalg.solve_triangular(factor, identity, lower=True).astype(BF)
    rotated = product(inverse, flat).astype(BF)
    return (rotated.reshape(cellwise.shape), intersection)


def solution(mesh):
    in_specs = (P("blk", "grid", None),)
    out_specs = (P(None, "grid", "blk"), P())
    return jax.shard_map(body, mesh=mesh, in_specs=in_specs, out_specs=out_specs, check_vma=False)
```

profile of v0, /device:TPU:0, one launch (start us, length us, event | category | flops | bytes accessed | tf_op | source)
XLA Modules:
  0.0 108.5 jit_solution(14714773791636200767)
XLA Ops:
  0.6 0.0 copy-start
  0.6 3.1 %collective-permute-start.3 = (bf16[4,16,4096]{2,1,0:T(8,128)(2,1)}, bf16[4,16,4096]{2,1,0:T(8,128)(2,1)S(1)}, u32[]{:S(2)}, u32[]{:S(2)}) collective-permute-start(bf16[4,16,4096]{2,1,0:T(8,128)(2,1)} %param.1), channel_id=1, source_target_pairs={{0,8},{4,12},{8,16},{12,20},{16,24},{20,28},{24,0},{28,4},{1,9},{5... | collective-permute-start | bytes 1572872 | tf_op jit(solution)/shard_map/ppermute | solution.py:243
  3.7 1.8 %dynamic-slice_bitcast_fusion = (bf16[16,4096]{1,0:T(8,128)(2,1)}, bf16[16,4096]{1,0:T(8,128)(2,1)S(1)}, bf16[16,4096]{1,0:T(8,128)(2,1)S(1)}, bf16[16,4096]{1,0:T(8,128)(2,1)S(1)}) fusion(bf16[4,16,4096]{2,1,0:T(8,128)(2,1)} %param.1, s32[]{:T(128)S(6)} %select_n.31, s32[]{:T(128)S(6)} %select_n.30, s32[]{:T(128)S(6)} %select_n.29, s32[]{:T(128)S(6)} %select_n.28), kind=kLoop, calls=%fused_computation.6 | loop fusion | bytes 1048592 | tf_op jit(solution)/shard_map/jit(dynamic_index_in_dim)/squeeze | solution.py:246
  5.5 0.0 collective-permute-start
  5.5 1.5 %collective-permute-start.1 = (bf16[16,4096]{1,0:T(8,128)(2,1)S(1)}, bf16[16,4096]{1,0:T(8,128)(2,1)S(1)}, u32[]{:S(2)}, u32[]{:S(2)}) collective-permute-start(bf16[16,4096]{1,0:T(8,128)(2,1)S(1)} %get-tuple-element.3), channel_id=1, source_target_pairs={{0,2},{1,3},{2,0},{3,1},{4,6},{5,7},{6,4},{7,5},{8,10},{9,11},{10,... | collective-permute-start | bytes 393224 | tf_op jit(solution)/shard_map/ppermute | solution.py:221
  7.2 0.1 add.172
  7.2 0.1 add.169
  7.3 0.1 add.170
  7.4 0.6 add_divide_fusion
  8.0 9.9 %collective-permute-done.3.refs_4_ = bf16[4,16,4096]{2,1,0:T(8,128)(2,1)S(1)} collective-permute-done((bf16[4,16,4096]{2,1,0:T(8,128)(2,1)}, bf16[4,16,4096]{2,1,0:T(8,128)(2,1)S(1)}, u32[]{:S(2)}, u32[]{:S(2)}) %collective-permute-start.3) | collective-permute-done | bytes 524320 | tf_op jit(solution)/shard_map/ppermute | solution.py:243
  17.9 0.1 broadcast_select_fusion
  18.0 1.6 %collective-permute-start.4 = (bf16[4,16,4096]{2,1,0:T(8,128)(2,1)S(1)}, bf16[4,16,4096]{2,1,0:T(8,128)(2,1)}, u32[]{:S(2)}, u32[]{:S(2)}) collective-permute-start(bf16[4,16,4096]{2,1,0:T(8,128)(2,1)S(1)} %broadcast_select_fusion), channel_id=1, source_target_pairs={{0,4},{4,0},{8,12},{12,8},{16,20},{20,16},{24,28},{28,24},{1,5},{5... | collective-permute-start | bytes 1572872 | tf_op jit(solution)/shard_map/ppermute | solution.py:221
  19.6 1.5 %collective-permute-start.9 = (bf16[4,16,4096]{2,1,0:T(8,128)(2,1)S(1)}, bf16[4,16,4096]{2,1,0:T(8,128)(2,1)}, u32[]{:S(2)}, u32[]{:S(2)}) collective-permute-start(bf16[4,16,4096]{2,1,0:T(8,128)(2,1)S(1)} %collective-permute-done.3.refs_4_), channel_id=1, source_target_pairs={{0,2},{1,3},{2,0},{3,1},{4,6},{5,7},{6,4},{7,5},{8,10},{9,11},{10,... | collective-permute-start | bytes 1572872 | tf_op jit(solution)/shard_map/ppermute | solution.py:221
  21.1 0.6 pad_maximum_fusion.refs_13_
  21.7 9.6 %collective-permute-done.4.refs_4_ = bf16[4,16,4096]{2,1,0:T(8,128)(2,1)} collective-permute-done((bf16[4,16,4096]{2,1,0:T(8,128)(2,1)S(1)}, bf16[4,16,4096]{2,1,0:T(8,128)(2,1)}, u32[]{:S(2)}, u32[]{:S(2)}) %collective-permute-start.4) | collective-permute-done | bytes 524320 | tf_op jit(solution)/shard_map/ppermute | solution.py:221
  31.2 1.3 %collective-permute-start.6 = (bf16[4,16,4096]{2,1,0:T(8,128)(2,1)}, bf16[4,16,4096]{2,1,0:T(8,128)(2,1)}, u32[]{:S(2)}, u32[]{:S(2)}) collective-permute-start(bf16[4,16,4096]{2,1,0:T(8,128)(2,1)} %collective-permute-done.4.refs_4_), channel_id=1, source_target_pairs={{0,2},{1,3},{2,0},{3,1},{4,6},{5,7},{6,4},{7,5},{8,10},{9,11},{10,... | collective-permute-start | bytes 1572872 | tf_op jit(solution)/shard_map/ppermute | solution.py:221
  32.5 0.1 convert_add_fusion
  32.6 0.1 add.166
  32.7 0.0 collective-permute-start.8
  32.7 0.0 collective-permute-done.9.refs_6_
  32.7 0.5 collective-permute-start.10
  33.2 0.4 multiply_convert_fusion
  33.6 0.0 collective-permute-done.refs_1_
  33.6 0.9 collective-permute-start.2
  34.5 0.0 collective-permute-done.1.refs_2_
  34.5 0.1 collective-permute-start.5
  34.6 10.6 %collective-permute-done.6.refs_6_ = bf16[4,16,4096]{2,1,0:T(8,128)(2,1)} collective-permute-done((bf16[4,16,4096]{2,1,0:T(8,128)(2,1)}, bf16[4,16,4096]{2,1,0:T(8,128)(2,1)}, u32[]{:S(2)}, u32[]{:S(2)}) %collective-permute-start.6) | collective-permute-done | bytes 524320 | tf_op jit(solution)/shard_map/ppermute | solution.py:221
  45.2 0.0 collective-permute-start.7
  45.2 1.2 %broadcast_multiply_fusion = (bf16[4,64,4,64]{3,2,1,0:T(4,128)(2,1)}, bf16[4,64,4,64]{3,2,1,0:T(4,128)(2,1)}, bf16[4,64,4,64]{3,2,1,0:T(4,128)(2,1)S(1)}) fusion(bf16[64,64]{1,0:T(8,128)(2,1)S(1)} %get-tuple-element.9, bf16[4,4]{1,0:T(4,128)(2,1)S(1)} %fusion, bf16[64,64]{1,0:T(8,128)(2,1)S(1)} %get-tuple-element.10, bf16[64,64]{1,0:T(8,128)(2,1)S(1)} %get-tuple-element.11), kind=kLoop, calls=%fused_computation.3 | loop fusion | flops 196608 | bytes 417824 | tf_op jit(solution)/shard_map/mul | solution.py:41
  46.3 0.2 mul.241.refs_9_.refs_12_
  46.6 1.2 %mul.248.refs_10_ = bf16[256,256]{1,0:T(8,128)(2,1)S(1)} reshape(bf16[4,64,4,64]{3,2,1,0:T(4,128)(2,1)} %get-tuple-element.7) | data formatting | bytes 262144 | tf_op jit(solution)/shard_map/mul | solution.py:41
  47.7 1.2 %mul.255.refs_11_ = bf16[256,256]{1,0:T(8,128)(2,1)S(1)} reshape(bf16[4,64,4,64]{3,2,1,0:T(4,128)(2,1)} %get-tuple-element.6) | data formatting | bytes 262144 | tf_op jit(solution)/shard_map/mul | solution.py:41
  49.0 0.0 collective-permute-done.2.refs_3_
  49.0 0.0 collective-permute-done.8.refs_5_
  49.0 0.0 collective-permute-done.10.refs_7_
  49.0 8.9 %shard_map.30.refs_14_ = f32[64,4096]{1,0:T(8,128)S(1)} custom-call(bf16[16,4096]{1,0:T(8,128)(2,1)S(1)} %get-tuple-element.5.refs_0_, bf16[16,4096]{1,0:T(8,128)(2,1)S(1)} %collective-permute-done.refs_1_, bf16[16,4096]{1,0:T(8,128)(2,1)S(1)} %collective-permute-done.1.refs_2_, bf16[16,4096]{1,0:T(8,128)(2,1)S(1)} %collective-permute-done.2.refs_3_, ...), custom_call_target="tpu_custom_call" | custom-call | flops 3221225472 | bytes 8388608 | tf_op jit(solution)/shard_map/pallas_call | solution.py:166
  57.9 0.0 collective-permute-done.5.refs_5_
  57.9 0.0 collective-permute-done.7.refs_7_
  58.0 9.1 %shard_map.31 = bf16[8,4,16,512]{3,2,1,0:T(8,128)(2,1)S(1)} custom-call(bf16[16,4096]{1,0:T(8,128)(2,1)S(1)} %get-tuple-element.5.refs_0_, bf16[16,4096]{1,0:T(8,128)(2,1)S(1)} %collective-permute-done.refs_1_, bf16[16,4096]{1,0:T(8,128)(2,1)S(1)} %collective-permute-done.1.refs_2_, bf16[16,4096]{1,0:T(8,128)(2,1)S(1)} %collective-permute-done.2.refs_3_, ...), custom_call_target="tpu_custom_call" | custom-call | flops 3221225472 | bytes 8388608 | tf_op jit(solution)/shard_map/pallas_call | solution.py:166
  67.1 19.1 %all_to_all.10.x_ref = bf16[32,16,512]{2,1,0:T(8,128)(2,1)} all-to-all(bf16[32,16,512]{2,1,0:T(8,128)(2,1)S(1)} %bitcast.9), channel_id=1, replica_groups=mesh['blk'=8,'grid'=4] {'blk','grid'}, dimensions={0} | all-to-all | bytes 1048576 | tf_op jit(solution)/shard_map/all_to_all | solution.py:275
  86.1 2.3 %shard_map.32 = f32[32,32]{1,0:T(8,128)} custom-call(bf16[32,16,512]{2,1,0:T(8,128)(2,1)} %all_to_all.10.x_ref), custom_call_target="tpu_custom_call" | custom-call | tf_op jit(solution)/shard_map/pallas_call | solution.py:280
  88.5 0.8 broadcast_in_dim.2
  89.2 0.3 reshape.226
  89.5 11.0 %all_to_all.11 = f32[32,1,1024]{2,1,0:T(1,128)S(1)} all-to-all(f32[32,1,1024]{2,1,0:T(1,128)S(1)} %reshape.226), channel_id=1, replica_groups=mesh['blk'=8,'grid'=4] {'blk','grid'}, dimensions={0} | all-to-all | bytes 262144 | tf_op jit(solution)/shard_map/all_to_all | solution.py:286
  100.5 0.5 broadcast.269
  101.0 0.9 reduce.4
  102.0 1.0 reshape.227.parts_ref
  102.9 5.5 %shard_map.33 = (bf16[32,16,512]{2,1,0:T(8,128)(2,1)}, f32[32,32]{1,0:T(8,128)}) custom-call(f32[32,32,32]{2,1,0:T(8,128)} %reshape.227.parts_ref, bf16[32,16,512]{2,1,0:T(8,128)(2,1)} %all_to_all.10.x_ref), custom_call_target="tpu_custom_call" | custom-call | tf_op jit(solution)/shard_map/pallas_call | solution.py:288
  (9 shorter events, 0.2 us)
Async XLA Ops:
  0.6 17.3 %copy-start = (bf16[4,16,4096]{2,1,0:T(8,128)(2,1)S(1)}, bf16[4,16,4096]{2,1,0:T(8,128)(2,1)}, u32[]{:S(2)}) copy-start(bf16[4,16,4096]{2,1,0:T(8,128)(2,1)} %param.1) | copy-start | bytes 1572868
  0.6 17.3 %collective-permute-start.3 = (bf16[4,16,4096]{2,1,0:T(8,128)(2,1)}, bf16[4,16,4096]{2,1,0:T(8,128)(2,1)S(1)}, u32[]{:S(2)}, u32[]{:S(2)}) collective-permute-start(bf16[4,16,4096]{2,1,0:T(8,128)(2,1)} %param.1), channel_id=1, source_target_pairs={{0,8},{4,12},{8,16},{12,20},{16,24},{20,28},{24,0},{28,4},{1,9},{5... | collective-permute-start | bytes 1572872 | tf_op jit(solution)/shard_map/ppermute | solution.py:243
  5.5 28.1 %collective-permute-start = (bf16[16,4096]{1,0:T(8,128)(2,1)S(1)}, bf16[16,4096]{1,0:T(8,128)(2,1)S(1)}, u32[]{:S(2)}, u32[]{:S(2)}) collective-permute-start(bf16[16,4096]{1,0:T(8,128)(2,1)S(1)} %get-tuple-element.4), channel_id=1, source_target_pairs={{0,1},{1,0},{2,3},{3,2},{4,5},{5,4},{6,7},{7,6},{8,9},{9,8},{10,11... | collective-permute-start | bytes 393224 | tf_op jit(solution)/shard_map/ppermute | solution.py:221
  5.5 29.0 %collective-permute-start.1 = (bf16[16,4096]{1,0:T(8,128)(2,1)S(1)}, bf16[16,4096]{1,0:T(8,128)(2,1)S(1)}, u32[]{:S(2)}, u32[]{:S(2)}) collective-permute-start(bf16[16,4096]{1,0:T(8,128)(2,1)S(1)} %get-tuple-element.3), channel_id=1, source_target_pairs={{0,2},{1,3},{2,0},{3,1},{4,6},{5,7},{6,4},{7,5},{8,10},{9,11},{10,... | collective-permute-start | bytes 393224 | tf_op jit(solution)/shard_map/ppermute | solution.py:221
  18.0 13.3 %collective-permute-start.4 = (bf16[4,16,4096]{2,1,0:T(8,128)(2,1)S(1)}, bf16[4,16,4096]{2,1,0:T(8,128)(2,1)}, u32[]{:S(2)}, u32[]{:S(2)}) collective-permute-start(bf16[4,16,4096]{2,1,0:T(8,128)(2,1)S(1)} %broadcast_select_fusion), channel_id=1, source_target_pairs={{0,4},{4,0},{8,12},{12,8},{16,20},{20,16},{24,28},{28,24},{1,5},{5... | collective-permute-start | bytes 1572872 | tf_op jit(solution)/shard_map/ppermute | solution.py:221
  19.6 13.1 %collective-permute-start.9 = (bf16[4,16,4096]{2,1,0:T(8,128)(2,1)S(1)}, bf16[4,16,4096]{2,1,0:T(8,128)(2,1)}, u32[]{:S(2)}, u32[]{:S(2)}) collective-permute-start(bf16[4,16,4096]{2,1,0:T(8,128)(2,1)S(1)} %collective-permute-done.3.refs_4_), channel_id=1, source_target_pairs={{0,2},{1,3},{2,0},{3,1},{4,6},{5,7},{6,4},{7,5},{8,10},{9,11},{10,... | collective-permute-start | bytes 1572872 | tf_op jit(solution)/shard_map/ppermute | solution.py:221
  31.2 14.0 %collective-permute-start.6 = (bf16[4,16,4096]{2,1,0:T(8,128)(2,1)}, bf16[4,16,4096]{2,1,0:T(8,128)(2,1)}, u32[]{:S(2)}, u32[]{:S(2)}) collective-permute-start(bf16[4,16,4096]{2,1,0:T(8,128)(2,1)} %collective-permute-done.4.refs_4_), channel_id=1, source_target_pairs={{0,2},{1,3},{2,0},{3,1},{4,6},{5,7},{6,4},{7,5},{8,10},{9,11},{10,... | collective-permute-start | bytes 1572872 | tf_op jit(solution)/shard_map/ppermute | solution.py:221
  32.7 16.3 %collective-permute-start.8 = (bf16[4,16,4096]{2,1,0:T(8,128)(2,1)S(1)}, bf16[4,16,4096]{2,1,0:T(8,128)(2,1)}, u32[]{:S(2)}, u32[]{:S(2)}) collective-permute-start(bf16[4,16,4096]{2,1,0:T(8,128)(2,1)S(1)} %collective-permute-done.3.refs_4_), channel_id=1, source_target_pairs={{0,1},{1,0},{2,3},{3,2},{4,5},{5,4},{6,7},{7,6},{8,9},{9,8},{10,11... | collective-permute-start | bytes 1572872 | tf_op jit(solution)/shard_map/ppermute | solution.py:221
  32.7 16.3 %collective-permute-start.10 = (bf16[4,16,4096]{2,1,0:T(8,128)(2,1)}, bf16[4,16,4096]{2,1,0:T(8,128)(2,1)}, u32[]{:S(2)}, u32[]{:S(2)}) collective-permute-start(bf16[4,16,4096]{2,1,0:T(8,128)(2,1)} %collective-permute-done.9.refs_6_), channel_id=1, source_target_pairs={{0,1},{1,0},{2,3},{3,2},{4,5},{5,4},{6,7},{7,6},{8,9},{9,8},{10,11... | collective-permute-start | bytes 1572872 | tf_op jit(solution)/shard_map/ppermute | solution.py:221
  33.6 15.3 %collective-permute-start.2 = (bf16[16,4096]{1,0:T(8,128)(2,1)}, bf16[16,4096]{1,0:T(8,128)(2,1)S(1)}, u32[]{:S(2)}, u32[]{:S(2)}) collective-permute-start(bf16[16,4096]{1,0:T(8,128)(2,1)} %get-tuple-element.2), channel_id=1, source_target_pairs={{0,3},{1,2},{2,1},{3,0},{4,7},{5,6},{6,5},{7,4},{8,11},{9,10},{10,... | collective-permute-start | bytes 393224 | tf_op jit(solution)/shard_map/ppermute | solution.py:221
  34.5 23.4 %collective-permute-start.5 = (bf16[4,16,4096]{2,1,0:T(8,128)(2,1)}, bf16[4,16,4096]{2,1,0:T(8,128)(2,1)}, u32[]{:S(2)}, u32[]{:S(2)}) collective-permute-start(bf16[4,16,4096]{2,1,0:T(8,128)(2,1)} %collective-permute-done.4.refs_4_), channel_id=1, source_target_pairs={{0,1},{1,0},{2,3},{3,2},{4,5},{5,4},{6,7},{7,6},{8,9},{9,8},{10,11... | collective-permute-start | bytes 1572872 | tf_op jit(solution)/shard_map/ppermute | solution.py:221
  45.2 12.8 %collective-permute-start.7 = (bf16[4,16,4096]{2,1,0:T(8,128)(2,1)}, bf16[4,16,4096]{2,1,0:T(8,128)(2,1)}, u32[]{:S(2)}, u32[]{:S(2)}) collective-permute-start(bf16[4,16,4096]{2,1,0:T(8,128)(2,1)} %collective-permute-done.6.refs_6_), channel_id=1, source_target_pairs={{0,1},{1,0},{2,3},{3,2},{4,5},{5,4},{6,7},{7,6},{8,9},{9,8},{10,11... | collective-permute-start | bytes 1572872 | tf_op jit(solution)/shard_map/ppermute | solution.py:221
where the time goes:
time: 109 us; the launch traced here: 108 us
  waiting for transfers between devices  30.1 us (28%)
  blocking collectives  30 us (28%)
  Pallas kernels  25.9 us (24%)
  starting transfers between devices  10.4 us (10%)
  local copies, waits for them, and re-layouts  7.19 us (7%)
  other arithmetic  3.98 us (4%)
    ppermute x10, waiting for transfers between devices, exchanged(): lax.ppermute(x, axis, [(i, i ^ by) for i in range(lax.axis_size(axis))])  20.2 us
    all_to_all x1, blocking collectives, body(): cellwise = lax.all_to_all(updated, ('blk', 'grid'), 0, 0, tiled=True)  19.1 us
    pallas_call x2, Pallas kernels, add_block(): pl.pallas_call(lambda *refs: block_kernel(slabs, final, refs), out_shape=...  18.1 us
    all_to_all x1, blocking collectives, body(): lax.all_to_all(jnp.broadcast_to(local[None], (devices,) + local.shape), (...  11 us
    ppermute x1, waiting for transfers between devices, body(): lax.ppermute(orbitals, 'blk', [(i, (i + 2) % blocks) for i in range(block...  9.89 us
    ppermute x10, starting transfers between devices, exchanged(): lax.ppermute(x, axis, [(i, i ^ by) for i in range(lax.axis_size(axis))])  7.28 us
    pallas_call x1, Pallas kernels, body(): pl.pallas_call(functools.partial(rotate_kernel, 1.0 / cell_count), out_sh...  5.55 us
    ppermute x1, starting transfers between devices, body(): lax.ppermute(orbitals, 'blk', [(i, (i + 2) % blocks) for i in range(block...  3.1 us
  transfers between devices with their start and end apart: 11, of which 3 were waited for; matrix products, arithmetic and copies ran while one was open for 7% of the time, Pallas kernels for 8%

commit v1 on v0

--- a/solution.py
+++ b/solution.py
@@ -23,22 +23,16 @@
 ROW_PAD = 8
 QUAD = 4
 UNROLL = 4
+PANEL = 8
 
 
 def product(a, b):
     return jnp.dot(a, b, preferred_element_type=F32)
 
 
-def sine_rows(length, index_in):
-    modes = jnp.arange(length).astype(F32)
-    angle = jnp.pi * (modes[:, None] + 1.0) * (index_in.astype(F32)[None, :] + 1.0) / (length + 1)
-    return (jnp.sqrt(2.0 / (length + 1)) * jnp.sin(angle)).astype(BF)
-
-
-def block_diagonal(table, copies):
-    n = table.shape[0]
-    eye = jnp.eye(copies, dtype=BF)
-    return (eye[:, None, :, None] * table[None, :, None, :]).reshape(copies * n, copies * n)
+def sine_tables(rows, columns):
+    angle = jnp.pi * (rows[:, :, None] + 1.0) * (columns[:, None, :] + 1.0) / (NX + 1)
+    return (jnp.sqrt(2.0 / (NX + 1)) * jnp.sin(angle)).astype(BF)
 
 
 def eigen_values(length):
@@ -46,22 +40,48 @@
     return 2.0 - 2.0 * jnp.cos(jnp.pi * (index + 1.0) / (length + 1))
 
 
-def kernel_weights():
-    values_x = eigen_values(NX)
-    values_y = eigen_values(NY)
-    values_z = eigen_values(NZ)
-    weights = 1.0 / (
-        screening + values_x[:, None, None] + values_y[None, :, None] + values_z[None, None, :]
-    )
-    return weights.reshape(NX * NY, NZ)
+def table_kernel(sine_ref, lam_ref, lanes_ref, diag_ref, weight_ref):
+    count, n, _ = sine_ref.shape
+    size = diag_ref.shape[1]
+    down = lax.broadcasted_iota(jnp.int32, (size, size), 0) // n
+    along = lax.broadcasted_iota(jnp.int32, (size, size), 1) // n
+    for i in range(count):
+        table = sine_ref[i].astype(F32)
+        table = jnp.concatenate([table] * (size // n), 1)
+        table = jnp.concatenate([table] * (size // n), 0)
+        diag_ref[i] = jnp.where(down == along, table, 0.0).astype(BF)
+    columns = lam_ref[...]
+    lanes = lanes_ref[...]
+    for k in range(n):
+        total = screening + columns[k:k + 1, :] + columns + lanes
+        weight_ref[k * n:(k + 1) * n, :] = 1.0 / total
+
+
+def make_tables(here):
+    cells = jnp.arange(NX).astype(F32)
+    here = here.astype(F32)
+    sine = sine_tables(jnp.stack([cells, cells, here]), jnp.stack([cells, here, cells]))
+    lam = eigen_values(NX)
+    size = QUAD * NX
+    return pl.pallas_call(
+        table_kernel,
+        out_shape=(
+            jax.ShapeDtypeStruct((3, size, size), BF),
+            jax.ShapeDtypeStruct((NX * NY, LANES), F32),
+        ),
+        in_specs=[VMEM] * 3,
+        out_specs=(VMEM, VMEM),
+        cost_estimate=pl.CostEstimate(flops=1 << 26, bytes_accessed=3 << 20, transcendentals=0),
+    )(sine, jnp.broadcast_to(lam[:, None], (NX, LANES)),
+      jnp.concatenate([lam] * (LANES // NZ))[None, :])
 
 
 def block_kernel(slabs, final, rest):
     own = rest[:slabs]
     src = rest[slabs:2 * slabs]
     rest = rest[2 * slabs:]
-    pos_ref, tz_ref, tx_ref, txb_ref, ty_ref, w_ref = rest[:6]
-    rest = rest[6:]
+    pos_ref, tab_ref, w_ref = rest[:3]
+    rest = rest[3:]
     if final:
         acc_ref, out_ref, grouped_ref, work_ref = rest
     else:
@@ -96,8 +116,8 @@
             [jnp.concatenate([p[:, c] for p in pairs], 1) for c in cut], 0)
         grouped_ref[pl.ds(at, QUAD * NX), :] = jnp.concatenate(
             [jnp.concatenate([o[:, c] for o in others], 1) for c in cut], 0)
-        first = product(density, tz_ref[...]).astype(BF)
-        modes = product(tx_ref[...], first)
+        first = product(density, tab_ref[0]).astype(BF)
+        modes = product(tab_ref[1], first)
         for q in range(QUAD):
             to = pl.multiple_of((t * QUAD + q) * pitch, 8)
             for h in range(halves):
@@ -111,8 +131,8 @@
                 [work_ref[h, pl.ds(t * QUAD + q, NY, stride=pitch), :] for h in range(halves)], 1)
             for q in range(QUAD)], 0).astype(BF)
         weights = jnp.concatenate([w_ref[pl.ds(at, QUAD * NY), :]] * halves, 1)
-        scaled = (product(ty_ref[...], modes) * weights).astype(BF)
-        back = product(ty_ref[...], scaled)
+        scaled = (product(tab_ref[0], modes) * weights).astype(BF)
+        back = product(tab_ref[0], scaled)
         for q in range(QUAD):
             for h in range(halves):
                 work_ref[h, pl.ds(t * QUAD + q, NY, stride=pitch), :] = (
@@ -124,8 +144,8 @@
 
     def backward(t, carry):
         at = pl.multiple_of(t * QUAD * NX, QUAD * NX)
-        third = product(txb_ref[...], load_rows(t * QUAD).astype(BF)).astype(BF)
-        potential = product(third, tz_ref[...])
+        third = product(tab_ref[2], load_rows(t * QUAD).astype(BF)).astype(BF)
+        potential = product(third, tab_ref[0])
         terms = potential * grouped_ref[pl.ds(at, QUAD * NX), :].astype(F32)
         total = terms[:, :LANES]
         for h in range(1, halves):
@@ -166,7 +186,7 @@
     return pl.pallas_call(
         lambda *refs: block_kernel(slabs, final, refs),
         out_shape=out_shape,
-        in_specs=[VMEM] * (2 * slabs) + [SMEM] + [VMEM] * (5 + len(lead)),
+        in_specs=[VMEM] * (2 * slabs) + [SMEM] + [VMEM] * (2 + len(lead)),
         out_specs=VMEM,
         scratch_shapes=[
             pltpu.VMEM((NY * NX, count * NZ), BF),
@@ -181,38 +201,56 @@
     orbs, rows, lanes = x_ref.shape
     flat = x_ref[...].reshape(orbs * rows, lanes)
     full = lax.dot_general(flat, flat, (((1,), (1,)), ((), ())), preferred_element_type=F32)
-    down = lax.broadcasted_iota(jnp.int32, full.shape, 0)
-    along = lax.broadcasted_iota(jnp.int32, full.shape, 1)
-    full = jnp.where(down % rows == along % rows, full, 0.0)
-    half = jnp.sum(full.reshape(orbs, rows, orbs * rows), axis=1)
-    out_ref[...] = jnp.sum(half.T.reshape(orbs, rows, orbs), axis=1)
+    down = lax.broadcasted_iota(jnp.int32, (rows, orbs * rows), 0)
+    along = lax.broadcasted_iota(jnp.int32, (rows, orbs * rows), 1)
+    same = down == along % rows
+    half = [
+        jnp.sum(jnp.where(same, full[o * rows:(o + 1) * rows], 0.0), axis=0, keepdims=True)
+        for o in range(orbs)
+    ]
+    half = jnp.concatenate(half, 0)
+    gram = jnp.sum(half.T.reshape(orbs, rows, orbs), axis=1)
+    deep = orbs * orbs // LANES
+    packed = jnp.concatenate([gram[q * deep:(q + 1) * deep] for q in range(orbs // deep)], 1)
+    out_ref[...] = jnp.broadcast_to(packed[None], out_ref.shape)
 
 
 def rotate_kernel(scale, parts_ref, x_ref, out_ref, gram_ref):
     orbs, rows, lanes = x_ref.shape
-    gram = jnp.sum(parts_ref[...], axis=0) * scale
+    packed = jnp.sum(parts_ref[...], axis=0) * scale
+    deep = packed.shape[0]
+    gram = jnp.concatenate(
+        [packed[:, q * orbs:(q + 1) * orbs] for q in range(LANES // orbs)], 0)
     gram_ref[...] = gram
     down = lax.broadcasted_iota(jnp.int32, (orbs, orbs), 0)
     along = lax.broadcasted_iota(jnp.int32, (orbs, orbs), 1)
     eye = jnp.where(down == along, 1.0, 0.0)
-    work = jnp.concatenate([gram, eye], 1)
-    row = lax.broadcasted_iota(jnp.int32, (orbs, 1), 0)
-    pivots = jnp.zeros((orbs, 1), F32)
-    for k in range(orbs):
-        column = work[:, k:k + 1]
-        pivot = work[k:k + 1, k:k + 1]
-        pivots = jnp.where(row == k, pivot, pivots)
-        factor = jnp.where(row > k, column / pivot, 0.0)
-        work = work - factor * work[k:k + 1, :]
-    inverse = (work[:, orbs:] * (1.0 / jnp.sqrt(pivots))).astype(BF)
+    zero = jnp.zeros((orbs, LANES - 2 * orbs), F32)
+    work = jnp.concatenate([gram, eye, zero], 1)
+    row = lax.broadcasted_iota(jnp.int32, (orbs, LANES), 0)
+    pivots = jnp.zeros((orbs, LANES), F32)
+    for first in range(0, orbs, PANEL):
+        columns = [
+            jnp.broadcast_to(work[:, c:c + 1], (orbs, LANES)) for c in range(first, first + PANEL)
+        ]
+        for k in range(first, first + PANEL):
+            column = columns[k - first]
+            pivot = column[k:k + 1, :]
+            pivots = jnp.where(row == k, pivot, pivots)
+            factor = jnp.where(row > k, column * (1.0 / pivot), 0.0)
+            work = work - factor * work[k:k + 1, :]
+            for c in range(k - first + 1, PANEL):
+                columns[c] = columns[c] - factor * columns[c][k:k + 1, :]
+    work = work * (1.0 / jnp.sqrt(pivots))
+    inverse = work[:, orbs:2 * orbs].astype(BF)
     tall = lax.broadcasted_iota(jnp.int32, (orbs * rows, orbs), 0) // rows
     wide = lax.broadcasted_iota(jnp.int32, (orbs * rows, orbs), 1)
     pick = jnp.where(tall == wide, 1.0, 0.0).astype(BF)
     spread = product(pick, inverse).astype(BF)
     spread = lax.dot_general(spread, pick, (((1,), (1,)), ((), ())), preferred_element_type=F32)
-    i = lax.broadcasted_iota(jnp.int32, spread.shape, 0)
-    j = lax.broadcasted_iota(jnp.int32, spread.shape, 1)
-    spread = jnp.where(i % rows == j % rows, spread, 0.0).astype(BF)
+    i = lax.broadcasted_iota(jnp.int32, (orbs * rows, 1), 0) % rows
+    j = lax.broadcasted_iota(jnp.int32, (1, orbs * rows), 1) % rows
+    spread = jnp.where(i == j, spread, 0.0).astype(BF)
     flat = x_ref[...].reshape(orbs * rows, lanes)
     out_ref[...] = product(spread, flat).astype(BF).reshape(orbs, rows, lanes)
 
@@ -221,15 +259,20 @@
     return lax.ppermute(x, axis, [(i, i ^ by) for i in range(lax.axis_size(axis))])
 
 
-def gathered(slab):
+def gathered(slab, after=None):
     size = lax.axis_size("grid")
     slabs = {0: slab}
     bit = size // 2
     while bit:
         for r in list(slabs):
-            slabs[r | bit] = exchanged(slabs[r], "grid", bit)
+            source = slabs[r]
+            if after is not None and bit == 1 and r == size - 2:
+                source, after = lax.optimization_barrier((source, after))
+                slabs[r] = source
+            slabs[r | bit] = exchanged(source, "grid", bit)
         bit //= 2
-    return [slabs[r] for r in range(size)]
+    slabs = [slabs[r] for r in range(size)]
+    return slabs if after is None else (slabs, after)
 
 
 def body(orbitals):
@@ -240,29 +283,21 @@
     grid_index = lax.axis_index("grid")
     order = jnp.arange(slabs) ^ grid_index
 
+    here = (order[:, None] * slab_rows + jnp.arange(slab_rows)[None, :]).reshape(NX)
+    diagonals, weights = make_tables(here)
+
     far = lax.ppermute(orbitals, "blk", [(i, (i + 2) % blocks) for i in range(blocks)])
     own = [lax.dynamic_index_in_dim(orbitals, grid_index, 0, keepdims=False)]
     for r in range(1, slabs):
         piece = lax.dynamic_index_in_dim(orbitals, grid_index ^ r, 0, keepdims=False)
         own.append(exchanged(piece, "grid", r))
-    near = exchanged(jnp.where(lax.axis_index("blk") % 2 == 0, orbitals, far), "blk", 1)
+    relay = jnp.where(lax.axis_index("blk") % 2 == 0, orbitals, far)
+    relay, diagonals, weights, own = lax.optimization_barrier((relay, diagonals, weights, own))
+    tables = (order.astype(jnp.int32), diagonals, weights)
+    near = exchanged(relay, "blk", 1)
     far = gathered(far)
-    near = gathered(near)
-
-    cells = jnp.arange(NX)
-    here = (order[:, None] * slab_rows + jnp.arange(slab_rows)[None, :]).reshape(NX)
-    table_x = sine_rows(NX, here)
-    table_z = sine_rows(NZ, cells[:NZ])
-    weights = jnp.concatenate([kernel_weights()] * (LANES // NZ), 1)
-    tables = (
-        order.astype(jnp.int32),
-        block_diagonal(table_z, orb_count),
-        block_diagonal(table_x, QUAD),
-        block_diagonal(table_x.T, QUAD),
-        block_diagonal(sine_rows(NY, cells[:NY]), QUAD),
-        weights,
-    )
     acc = add_block(own, far, tables, None, jax.ShapeDtypeStruct((NX, plane_cells), F32))
+    near, acc = gathered(near, acc)
     chunk = plane_cells // blocks
     if chunk % LANES == 0:
         shape = (blocks, slabs, slab_rows, chunk)
@@ -276,20 +311,19 @@
 
     devices = blocks * slabs
     cell_count = NX * NY * NZ
-    if devices * slab_rows <= 512 and chunk % LANES == 0:
+    if devices * slab_rows <= 512 and devices % PANEL == 0 and chunk % LANES == 0:
         local = pl.pallas_call(
             gram_kernel,
-            out_shape=jax.ShapeDtypeStruct((devices, devices), F32),
+            out_shape=jax.ShapeDtypeStruct((devices, devices * devices // LANES, LANES), F32),
             in_specs=[VMEM],
             out_specs=VMEM,
         )(cellwise)
-        parts = lax.all_to_all(
-            jnp.broadcast_to(local[None], (devices,) + local.shape), ("blk", "grid"), 0, 0)
+        parts = lax.all_to_all(local, ("blk", "grid"), 0, 0, tiled=True)
         return pl.pallas_call(
             functools.partial(rotate_kernel, 1.0 / cell_count),
             out_shape=(
                 jax.ShapeDtypeStruct(cellwise.shape, BF),
-                jax.ShapeDtypeStruct(local.shape, F32),
+                jax.ShapeDtypeStruct((devices, devices), F32),
             ),
             in_specs=[VMEM, VMEM],
             out_specs=(VMEM, VMEM),

time: 109 us -> 92.5 us (0.85)
  waiting for transfers between devices: 30.1 us -> 20.4 us
  local copies, waits for them, and re-layouts: 7.19 us -> 4.47 us
  starting transfers between devices: 10.4 us -> 8.11 us
  other arithmetic: 3.98 us -> 2.85 us
  Pallas kernels: 25.9 us -> 24.8 us
    ppermute x10, waiting for transfers between devices: 20.2 us -> 14.7 us  [exchanged(): lax.ppermute(x, axis, [(i, i ^ by) for i in range(lax.axis_size(axis))])]
    ppermute x1, waiting for transfers between devices: 9.89 us -> 5.72 us  [body(): lax.ppermute(orbitals, 'blk', [(i, (i + 2) % blocks) for i in range(block...]
    mul x3 -> x0, local copies, waits for them, and re-layouts: 2.58 us -> none  [block_diagonal(): eye[:, None, :, None] * table[None, :, None, :]]
    pallas_call x0 -> x1, Pallas kernels: none -> 2.57 us  [make_tables(): pl.pallas_call(table_kernel, out_shape=(jax.ShapeDtypeStruct((3, size, si...]
    ppermute x10, starting transfers between devices: 7.28 us -> 5 us  [exchanged(): lax.ppermute(x, axis, [(i, i ^ by) for i in range(lax.axis_size(axis))])]
    pallas_call x1, Pallas kernels: 5.55 us -> 3.49 us  [body(): pl.pallas_call(functools.partial(rotate_kernel, 1.0 / cell_count), out_sh...]
    pallas_call x2, Pallas kernels: 18.1 us -> 16.3 us  [add_block(): pl.pallas_call(lambda *refs: block_kernel(slabs, final, refs), out_shape=...]
    unnamed x4, local copies, waits for them, and re-layouts: 1.21 us -> 2.58 us
  transfers between devices with their start and end apart: 11 -> 11, of which waited for: 3 -> 5; matrix products, arithmetic and copies ran while one was open for 7% -> 5% of each run, Pallas kernels for 8% -> 12%
where the time goes in v1:
time: 92.5 us; the launch traced here: 92 us
  blocking collectives  30.7 us (33%)
  Pallas kernels  24.8 us (27%)
  waiting for transfers between devices  20.4 us (22%)
  starting transfers between devices  8.11 us (9%)
  local copies, waits for them, and re-layouts  4.47 us (5%)
  other arithmetic  2.85 us (3%)
    all_to_all x1, blocking collectives, body(): cellwise = lax.all_to_all(updated, ('blk', 'grid'), 0, 0, tiled=True)  19.2 us
    pallas_call x2, Pallas kernels, add_block(): pl.pallas_call(lambda *refs: block_kernel(slabs, final, refs), out_shape=...  16.3 us
    ppermute x10, waiting for transfers between devices, exchanged(): lax.ppermute(x, axis, [(i, i ^ by) for i in range(lax.axis_size(axis))])  14.7 us
    all_to_all x1, blocking collectives, body(): parts = lax.all_to_all(local, ('blk', 'grid'), 0, 0, tiled=True)  11.5 us
    ppermute x1, waiting for transfers between devices, body(): lax.ppermute(orbitals, 'blk', [(i, (i + 2) % blocks) for i in range(block...  5.72 us
    ppermute x10, starting transfers between devices, exchanged(): lax.ppermute(x, axis, [(i, i ^ by) for i in range(lax.axis_size(axis))])  5 us
    pallas_call x1, Pallas kernels, body(): pl.pallas_call(functools.partial(rotate_kernel, 1.0 / cell_count), out_sh...  3.49 us
    ppermute x1, starting transfers between devices, body(): lax.ppermute(orbitals, 'blk', [(i, (i + 2) % blocks) for i in range(block...  3.1 us
  transfers between devices with their start and end apart: 11, of which 5 were waited for; matrix products, arithmetic and copies ran while one was open for 5% of the time, Pallas kernels for 12%

profile of v1, /device:TPU:0, one launch (start us, length us, event | category | flops | bytes accessed | tf_op | source)
XLA Modules:
  0.0 92.0 jit_solution(4740476561099999749)
XLA Ops:
  0.6 3.1 %collective-permute-start = (bf16[4,16,4096]{2,1,0:T(8,128)(2,1)}, bf16[4,16,4096]{2,1,0:T(8,128)(2,1)S(1)}, u32[]{:S(2)}, u32[]{:S(2)}) collective-permute-start(bf16[4,16,4096]{2,1,0:T(8,128)(2,1)} %param.1), channel_id=1, source_target_pairs={{0,8},{4,12},{8,16},{12,20},{16,24},{20,28},{24,0},{28,4},{1,9},{5... | collective-permute-start | bytes 1572872 | tf_op jit(solution)/shard_map/ppermute | solution.py:289
  3.7 1.1 %dynamic-slice_bitcast_fusion = (bf16[16,4096]{1,0:T(8,128)(2,1)S(1)}, bf16[16,4096]{1,0:T(8,128)(2,1)S(1)}, bf16[16,4096]{1,0:T(8,128)(2,1)S(1)}, bf16[16,4096]{1,0:T(8,128)(2,1)S(1)}) fusion(bf16[4,16,4096]{2,1,0:T(8,128)(2,1)} %param.1, s32[]{:T(128)S(6)} %select_n.34, s32[]{:T(128)S(6)} %select_n.32, s32[]{:T(128)S(6)} %select_n.31, s32[]{:T(128)S(6)} %select_n.33), kind=kLoop, calls=%fused_computation.1 | loop fusion | bytes 1048592 | tf_op jit(solution)/shard_map/jit(dynamic_index_in_dim)/squeeze | solution.py:292
  4.9 0.7 collective-permute-start.3
  5.6 1.0 %collective-permute-start.1 = (bf16[16,4096]{1,0:T(8,128)(2,1)S(1)}, bf16[16,4096]{1,0:T(8,128)(2,1)S(1)}, u32[]{:S(2)}, u32[]{:S(2)}) collective-permute-start(bf16[16,4096]{1,0:T(8,128)(2,1)S(1)} %get-tuple-element.25), channel_id=1, source_target_pairs={{0,1},{1,0},{2,3},{3,2},{4,5},{5,4},{6,7},{7,6},{8,9},{9,8},{10,11... | collective-permute-start | bytes 393224 | tf_op jit(solution)/shard_map/ppermute | solution.py:259
  6.5 0.5 collective-permute-start.2
  7.1 0.1 add_convert_fusion
  7.2 0.1 convert_element_type.55
  7.3 0.6 maximum_bitcast_fusion.lanes_ref
  7.9 1.0 %multiply_convert_fusion.sine_ref = bf16[3,64,64]{2,1,0:T(8,128)(2,1)} fusion(f32[3,64]{1,0:T(4,128)S(1)} %get-tuple-element.29, f32[3,64]{1,0:T(4,128)S(1)} %get-tuple-element.28), kind=kLoop, calls=%fused_computation.5 | loop fusion | flops 49152 | bytes 26112 | tf_op jit(solution)/shard_map/convert_element_type | solution.py:35
  8.9 0.7 broadcast_in_dim.4.lam_ref
  9.6 2.6 %shard_map.30 = (bf16[3,256,256]{2,1,0:T(8,128)(2,1)}, f32[4096,128]{1,0:T(8,128)}) custom-call(bf16[3,64,64]{2,1,0:T(8,128)(2,1)} %multiply_convert_fusion.sine_ref, f32[64,128]{1,0:T(8,128)} %broadcast_in_dim.4.lam_ref, f32[1,128]{1,0:T(1,128)} %maximum_bitcast_fusion.lanes_ref), custom_call_target="tpu_custom_call" | custom-call | flops 67108864 | bytes 3145728 | tf_op jit(solution)/shard_map/pallas_call | solution.py:66
  12.2 5.7 %collective-permute-done.refs_4_ = bf16[4,16,4096]{2,1,0:T(8,128)(2,1)S(1)} collective-permute-done((bf16[4,16,4096]{2,1,0:T(8,128)(2,1)}, bf16[4,16,4096]{2,1,0:T(8,128)(2,1)S(1)}, u32[]{:S(2)}, u32[]{:S(2)}) %collective-permute-start) | collective-permute-done | bytes 524320 | tf_op jit(solution)/shard_map/ppermute | solution.py:289
  17.9 1.5 %collective-permute-start.8 = (bf16[4,16,4096]{2,1,0:T(8,128)(2,1)S(1)}, bf16[4,16,4096]{2,1,0:T(8,128)(2,1)S(1)}, u32[]{:S(2)}, u32[]{:S(2)}) collective-permute-start(bf16[4,16,4096]{2,1,0:T(8,128)(2,1)S(1)} %collective-permute-done.refs_4_), channel_id=1, source_target_pairs={{0,2},{1,3},{2,0},{3,1},{4,6},{5,7},{6,4},{7,5},{8,10},{9,11},{10,... | collective-permute-start | bytes 1572872 | tf_op jit(solution)/shard_map/ppermute | solution.py:259
  19.4 1.1 %broadcast_select_fusion = bf16[4,16,4096]{2,1,0:T(8,128)(2,1)S(1)} fusion(bf16[4,16,4096]{2,1,0:T(8,128)(2,1)} %param.1, bf16[4,16,4096]{2,1,0:T(8,128)(2,1)S(1)} %collective-permute-done.refs_4_, pred[]{:T(512)S(6)} %eq.5), kind=kLoop, calls=%fused_computation | loop fusion | flops 262144 | bytes 1572865 | tf_op jit(solution)/shard_map/jit(_where)/select_n | solution.py:294
  20.5 0.0 collective-permute-done.3.refs_3_
  20.5 0.0 collective-permute-done.1.refs_1_
  20.5 0.0 collective-permute-done.2.refs_2_
  20.5 0.5 collective-permute-start.4
  21.1 0.0 collective-permute-start.7
  21.1 9.9 %collective-permute-done.8.refs_6_ = bf16[4,16,4096]{2,1,0:T(8,128)(2,1)S(1)} collective-permute-done((bf16[4,16,4096]{2,1,0:T(8,128)(2,1)S(1)}, bf16[4,16,4096]{2,1,0:T(8,128)(2,1)S(1)}, u32[]{:S(2)}, u32[]{:S(2)}) %collective-permute-start.8) | collective-permute-done | bytes 524320 | tf_op jit(solution)/shard_map/ppermute | solution.py:259
  31.0 0.0 collective-permute-start.9
  31.0 2.2 %collective-permute-done.4.refs_4_ = bf16[4,16,4096]{2,1,0:T(8,128)(2,1)S(1)} collective-permute-done((bf16[4,16,4096]{2,1,0:T(8,128)(2,1)S(1)}, bf16[4,16,4096]{2,1,0:T(8,128)(2,1)S(1)}, u32[]{:S(2)}, u32[]{:S(2)}) %collective-permute-start.4) | collective-permute-done | bytes 524320 | tf_op jit(solution)/shard_map/ppermute | solution.py:259
  33.2 0.7 collective-permute-start.6
  33.9 0.0 collective-permute-start.5
  33.9 0.0 collective-permute-done.7.refs_5_
  33.9 0.0 collective-permute-done.9.refs_7_
  34.0 0.0 copy-start
  34.0 1.6 %copy-done = f32[4096,128]{1,0:T(8,128)S(1)} copy-done((f32[4096,128]{1,0:T(8,128)S(1)}, f32[4096,128]{1,0:T(8,128)}, u32[]{:S(2)}) %copy-start) | copy-done | bytes 2097176
  35.5 0.0 copy-start.1
  35.5 1.0 %copy-done.1 = bf16[3,256,256]{2,1,0:T(8,128)(2,1)S(1)} copy-done((bf16[3,256,256]{2,1,0:T(8,128)(2,1)S(1)}, bf16[3,256,256]{2,1,0:T(8,128)(2,1)}, u32[]{:S(2)}) %copy-start.1) | copy-done | bytes 393240
  36.5 8.1 %shard_map.31.refs_11_ = f32[64,4096]{1,0:T(8,128)S(1)} custom-call(bf16[16,4096]{1,0:T(8,128)(2,1)S(1)} %get-tuple-element.15.refs_0_, bf16[16,4096]{1,0:T(8,128)(2,1)S(1)} %collective-permute-done.1.refs_1_, bf16[16,4096]{1,0:T(8,128)(2,1)S(1)} %collective-permute-done.2.refs_2_, bf16[16,4096]{1,0:T(8,128)(2,1)S(1)} %collective-permute-done.3.refs_3_, ...), custom_call_target="tpu_custom_call" | custom-call | flops 3221225472 | bytes 8388608 | tf_op jit(solution)/shard_map/pallas_call | solution.py:186
  44.7 0.6 collective-permute-done.6.refs_6_
  45.3 0.0 collective-permute-start.10
  45.3 0.0 collective-permute-done.5.refs_5_
  45.3 1.9 %collective-permute-done.10.refs_7_ = bf16[4,16,4096]{2,1,0:T(8,128)(2,1)S(1)} collective-permute-done((bf16[4,16,4096]{2,1,0:T(8,128)(2,1)S(1)}, bf16[4,16,4096]{2,1,0:T(8,128)(2,1)S(1)}, u32[]{:S(2)}, u32[]{:S(2)}) %collective-permute-start.10) | collective-permute-done | bytes 524320 | tf_op jit(solution)/shard_map/ppermute | solution.py:259
  47.2 8.2 %shard_map.32 = bf16[8,4,16,512]{3,2,1,0:T(8,128)(2,1)S(1)} custom-call(bf16[16,4096]{1,0:T(8,128)(2,1)S(1)} %get-tuple-element.15.refs_0_, bf16[16,4096]{1,0:T(8,128)(2,1)S(1)} %collective-permute-done.1.refs_1_, bf16[16,4096]{1,0:T(8,128)(2,1)S(1)} %collective-permute-done.2.refs_2_, bf16[16,4096]{1,0:T(8,128)(2,1)S(1)} %collective-permute-done.3.refs_3_, ...), custom_call_target="tpu_custom_call" | custom-call | flops 3221225472 | bytes 8388608 | tf_op jit(solution)/shard_map/pallas_call | solution.py:186
  55.4 19.2 %all_to_all.10.x_ref = bf16[32,16,512]{2,1,0:T(8,128)(2,1)} all-to-all(bf16[32,16,512]{2,1,0:T(8,128)(2,1)S(1)} %bitcast.11), channel_id=1, replica_groups=mesh['blk'=8,'grid'=4] {'blk','grid'}, dimensions={0} | all-to-all | bytes 1048576 | tf_op jit(solution)/shard_map/all_to_all | solution.py:310
  74.6 2.4 %shard_map.33 = f32[32,8,128]{2,1,0:T(8,128)} custom-call(bf16[32,16,512]{2,1,0:T(8,128)(2,1)} %all_to_all.10.x_ref), custom_call_target="tpu_custom_call" | custom-call | tf_op jit(solution)/shard_map/pallas_call | solution.py:315
  77.1 11.5 %all_to_all.11.parts_ref = f32[32,8,128]{2,1,0:T(8,128)} all-to-all(f32[32,8,128]{2,1,0:T(8,128)} %shard_map.33), channel_id=1, replica_groups=mesh['blk'=8,'grid'=4] {'blk','grid'}, dimensions={0} | all-to-all | bytes 262144 | tf_op jit(solution)/shard_map/all_to_all | solution.py:321
  88.5 3.5 %shard_map.34 = (bf16[32,16,512]{2,1,0:T(8,128)(2,1)}, f32[32,32]{1,0:T(8,128)}) custom-call(f32[32,8,128]{2,1,0:T(8,128)} %all_to_all.11.parts_ref, bf16[32,16,512]{2,1,0:T(8,128)(2,1)} %all_to_all.10.x_ref), custom_call_target="tpu_custom_call" | custom-call | tf_op jit(solution)/shard_map/pallas_call | solution.py:322
  (5 shorter events, 0.1 us)
Async XLA Ops:
  0.6 17.3 %collective-permute-start = (bf16[4,16,4096]{2,1,0:T(8,128)(2,1)}, bf16[4,16,4096]{2,1,0:T(8,128)(2,1)S(1)}, u32[]{:S(2)}, u32[]{:S(2)}) collective-permute-start(bf16[4,16,4096]{2,1,0:T(8,128)(2,1)} %param.1), channel_id=1, source_target_pairs={{0,8},{4,12},{8,16},{12,20},{16,24},{20,28},{24,0},{28,4},{1,9},{5... | collective-permute-start | bytes 1572872 | tf_op jit(solution)/shard_map/ppermute | solution.py:289
  4.9 15.6 %collective-permute-start.3 = (bf16[16,4096]{1,0:T(8,128)(2,1)S(1)}, bf16[16,4096]{1,0:T(8,128)(2,1)S(1)}, u32[]{:S(2)}, u32[]{:S(2)}) collective-permute-start(bf16[16,4096]{1,0:T(8,128)(2,1)S(1)} %get-tuple-element.24), channel_id=1, source_target_pairs={{0,3},{1,2},{2,1},{3,0},{4,7},{5,6},{6,5},{7,4},{8,11},{9,10},{10,... | collective-permute-start | bytes 393224 | tf_op jit(solution)/shard_map/ppermute | solution.py:259
  5.6 14.9 %collective-permute-start.1 = (bf16[16,4096]{1,0:T(8,128)(2,1)S(1)}, bf16[16,4096]{1,0:T(8,128)(2,1)S(1)}, u32[]{:S(2)}, u32[]{:S(2)}) collective-permute-start(bf16[16,4096]{1,0:T(8,128)(2,1)S(1)} %get-tuple-element.25), channel_id=1, source_target_pairs={{0,1},{1,0},{2,3},{3,2},{4,5},{5,4},{6,7},{7,6},{8,9},{9,8},{10,11... | collective-permute-start | bytes 393224 | tf_op jit(solution)/shard_map/ppermute | solution.py:259
  6.5 14.0 %collective-permute-start.2 = (bf16[16,4096]{1,0:T(8,128)(2,1)S(1)}, bf16[16,4096]{1,0:T(8,128)(2,1)S(1)}, u32[]{:S(2)}, u32[]{:S(2)}) collective-permute-start(bf16[16,4096]{1,0:T(8,128)(2,1)S(1)} %get-tuple-element.27), channel_id=1, source_target_pairs={{0,2},{1,3},{2,0},{3,1},{4,6},{5,7},{6,4},{7,5},{8,10},{9,11},{10,... | collective-permute-start | bytes 393224 | tf_op jit(solution)/shard_map/ppermute | solution.py:259
  17.9 13.1 %collective-permute-start.8 = (bf16[4,16,4096]{2,1,0:T(8,128)(2,1)S(1)}, bf16[4,16,4096]{2,1,0:T(8,128)(2,1)S(1)}, u32[]{:S(2)}, u32[]{:S(2)}) collective-permute-start(bf16[4,16,4096]{2,1,0:T(8,128)(2,1)S(1)} %collective-permute-done.refs_4_), channel_id=1, source_target_pairs={{0,2},{1,3},{2,0},{3,1},{4,6},{5,7},{6,4},{7,5},{8,10},{9,11},{10,... | collective-permute-start | bytes 1572872 | tf_op jit(solution)/shard_map/ppermute | solution.py:259
  20.5 12.7 %collective-permute-start.4 = (bf16[4,16,4096]{2,1,0:T(8,128)(2,1)S(1)}, bf16[4,16,4096]{2,1,0:T(8,128)(2,1)S(1)}, u32[]{:S(2)}, u32[]{:S(2)}) collective-permute-start(bf16[4,16,4096]{2,1,0:T(8,128)(2,1)S(1)} %broadcast_select_fusion), channel_id=1, source_target_pairs={{0,4},{4,0},{8,12},{12,8},{16,20},{20,16},{24,28},{28,24},{1,5},{5... | collective-permute-start | bytes 1572872 | tf_op jit(solution)/shard_map/ppermute | solution.py:259
  21.1 12.9 %collective-permute-start.7 = (bf16[4,16,4096]{2,1,0:T(8,128)(2,1)S(1)}, bf16[4,16,4096]{2,1,0:T(8,128)(2,1)S(1)}, u32[]{:S(2)}, u32[]{:S(2)}) collective-permute-start(bf16[4,16,4096]{2,1,0:T(8,128)(2,1)S(1)} %collective-permute-done.refs_4_), channel_id=1, source_target_pairs={{0,1},{1,0},{2,3},{3,2},{4,5},{5,4},{6,7},{7,6},{8,9},{9,8},{10,11... | collective-permute-start | bytes 1572872 | tf_op jit(solution)/shard_map/ppermute | solution.py:259
  31.0 3.0 %collective-permute-start.9 = (bf16[4,16,4096]{2,1,0:T(8,128)(2,1)S(1)}, bf16[4,16,4096]{2,1,0:T(8,128)(2,1)S(1)}, u32[]{:S(2)}, u32[]{:S(2)}) collective-permute-start(bf16[4,16,4096]{2,1,0:T(8,128)(2,1)S(1)} %collective-permute-done.8.refs_6_), channel_id=1, source_target_pairs={{0,1},{1,0},{2,3},{3,2},{4,5},{5,4},{6,7},{7,6},{8,9},{9,8},{10,11... | collective-permute-start | bytes 1572872 | tf_op jit(solution)/shard_map/ppermute | solution.py:259
  33.2 12.1 %collective-permute-start.6 = (bf16[4,16,4096]{2,1,0:T(8,128)(2,1)S(1)}, bf16[4,16,4096]{2,1,0:T(8,128)(2,1)S(1)}, u32[]{:S(2)}, u32[]{:S(2)}) collective-permute-start(bf16[4,16,4096]{2,1,0:T(8,128)(2,1)S(1)} %collective-permute-done.4.refs_4_), channel_id=1, source_target_pairs={{0,2},{1,3},{2,0},{3,1},{4,6},{5,7},{6,4},{7,5},{8,10},{9,11},{10,... | collective-permute-start | bytes 1572872 | tf_op jit(solution)/shard_map/ppermute | solution.py:259
  33.9 11.4 %collective-permute-start.5 = (bf16[4,16,4096]{2,1,0:T(8,128)(2,1)S(1)}, bf16[4,16,4096]{2,1,0:T(8,128)(2,1)S(1)}, u32[]{:S(2)}, u32[]{:S(2)}) collective-permute-start(bf16[4,16,4096]{2,1,0:T(8,128)(2,1)S(1)} %collective-permute-done.4.refs_4_), channel_id=1, source_target_pairs={{0,1},{1,0},{2,3},{3,2},{4,5},{5,4},{6,7},{7,6},{8,9},{9,8},{10,11... | collective-permute-start | bytes 1572872 | tf_op jit(solution)/shard_map/ppermute | solution.py:259
  34.0 1.6 %copy-start = (f32[4096,128]{1,0:T(8,128)S(1)}, f32[4096,128]{1,0:T(8,128)}, u32[]{:S(2)}) copy-start(f32[4096,128]{1,0:T(8,128)} %get-tuple-element.21.refs_10_) | copy-start | bytes 6291460
  35.5 1.0 %copy-start.1 = (bf16[3,256,256]{2,1,0:T(8,128)(2,1)S(1)}, bf16[3,256,256]{2,1,0:T(8,128)(2,1)}, u32[]{:S(2)}) copy-start(bf16[3,256,256]{2,1,0:T(8,128)(2,1)} %get-tuple-element.20.refs_9_) | copy-start | bytes 1179652
  45.3 1.9 %collective-permute-start.10 = (bf16[4,16,4096]{2,1,0:T(8,128)(2,1)S(1)}, bf16[4,16,4096]{2,1,0:T(8,128)(2,1)S(1)}, u32[]{:S(2)}, u32[]{:S(2)}) collective-permute-start(bf16[4,16,4096]{2,1,0:T(8,128)(2,1)S(1)} %collective-permute-done.6.refs_6_), channel_id=1, source_target_pairs={{0,1},{1,0},{2,3},{3,2},{4,5},{5,4},{6,7},{7,6},{8,9},{9,8},{10,11... | collective-permute-start | bytes 1572872 | tf_op jit(solution)/shard_map/ppermute | solution.py:259

commit v2 on v1

--- a/solution.py
+++ b/solution.py
@@ -6,6 +6,7 @@
 from jax.experimental import pallas as pl
 from jax.experimental.pallas import tpu as pltpu
 from jax.sharding import PartitionSpec as P
+
 
 NX = 64
 NY = 64
@@ -76,18 +77,19 @@
       jnp.concatenate([lam] * (LANES // NZ))[None, :])
 
 
-def block_kernel(slabs, final, rest):
+def block_kernel(slabs, parts, final, rest):
     own = rest[:slabs]
-    src = rest[slabs:2 * slabs]
-    rest = rest[2 * slabs:]
+    src = [rest[slabs + p * slabs:slabs + (p + 1) * slabs] for p in range(parts)]
+    rest = rest[slabs * (parts + 1):]
     pos_ref, tab_ref, w_ref = rest[:3]
     rest = rest[3:]
     if final:
         acc_ref, out_ref, grouped_ref, work_ref = rest
     else:
         out_ref, grouped_ref, work_ref = rest
-    count = src[0].shape[0]
-    rows = src[0].shape[1]
+    each = src[0][0].shape[0]
+    count = each * parts
+    rows = src[0][0].shape[1]
     halves = count * NZ // LANES
     width = QUAD * NZ
     pitch = work_ref.shape[1] // NY
@@ -109,7 +111,7 @@
         off = pl.multiple_of(t * width, width)
         at = pl.multiple_of(t * QUAD * NX, QUAD * NX)
         mine = tile(own, (), off, width)
-        others = [tile(src, (j,), off, width) for j in range(count)]
+        others = [tile(src[j // each], (j % each,), off, width) for j in range(count)]
         pairs = [mine * other for other in others]
         cut = [slice(q * NZ, (q + 1) * NZ) for q in range(QUAD)]
         density = jnp.concatenate(
@@ -179,14 +181,14 @@
 
 def add_block(own, src, tables, acc, out_shape):
     slabs = len(own)
-    count = src[0].shape[0]
+    count = sum(part[0].shape[0] for part in src)
     final = acc is not None
     lead = () if acc is None else (acc,)
     flops = 12 * count * NX * NY * NZ * NZ * 4
     return pl.pallas_call(
-        lambda *refs: block_kernel(slabs, final, refs),
+        lambda *refs: block_kernel(slabs, len(src), final, refs),
         out_shape=out_shape,
-        in_specs=[VMEM] * (2 * slabs) + [SMEM] + [VMEM] * (2 + len(lead)),
+        in_specs=[VMEM] * ((1 + len(src)) * slabs) + [SMEM] + [VMEM] * (2 + len(lead)),
         out_specs=VMEM,
         scratch_shapes=[
             pltpu.VMEM((NY * NX, count * NZ), BF),
@@ -194,7 +196,7 @@
         ],
         compiler_params=pltpu.CompilerParams(vmem_limit_bytes=40 * 1024 * 1024),
         cost_estimate=pl.CostEstimate(flops=flops, bytes_accessed=8 << 20, transcendentals=0),
-    )(*own, *src, *tables, *lead)
+    )(*own, *[slab for part in src for slab in part], *tables, *lead)
 
 
 def gram_kernel(x_ref, out_ref):
@@ -218,7 +220,6 @@
 def rotate_kernel(scale, parts_ref, x_ref, out_ref, gram_ref):
     orbs, rows, lanes = x_ref.shape
     packed = jnp.sum(parts_ref[...], axis=0) * scale
-    deep = packed.shape[0]
     gram = jnp.concatenate(
         [packed[:, q * orbs:(q + 1) * orbs] for q in range(LANES // orbs)], 0)
     gram_ref[...] = gram
@@ -259,20 +260,15 @@
     return lax.ppermute(x, axis, [(i, i ^ by) for i in range(lax.axis_size(axis))])
 
 
-def gathered(slab, after=None):
-    size = lax.axis_size("grid")
-    slabs = {0: slab}
-    bit = size // 2
+def completed(slab, other):
+    top = lax.axis_size("grid") // 2
+    slabs = {0: slab, top: other}
+    bit = top // 2
     while bit:
         for r in list(slabs):
-            source = slabs[r]
-            if after is not None and bit == 1 and r == size - 2:
-                source, after = lax.optimization_barrier((source, after))
-                slabs[r] = source
-            slabs[r | bit] = exchanged(source, "grid", bit)
+            slabs[r | bit] = exchanged(slabs[r], "grid", bit)
         bit //= 2
-    slabs = [slabs[r] for r in range(size)]
-    return slabs if after is None else (slabs, after)
+    return [slabs[r] for r in range(2 * top)]
 
 
 def body(orbitals):
@@ -286,18 +282,37 @@
     here = (order[:, None] * slab_rows + jnp.arange(slab_rows)[None, :]).reshape(NX)
     diagonals, weights = make_tables(here)
 
-    far = lax.ppermute(orbitals, "blk", [(i, (i + 2) % blocks) for i in range(blocks)])
-    own = [lax.dynamic_index_in_dim(orbitals, grid_index, 0, keepdims=False)]
-    for r in range(1, slabs):
-        piece = lax.dynamic_index_in_dim(orbitals, grid_index ^ r, 0, keepdims=False)
-        own.append(exchanged(piece, "grid", r))
-    relay = jnp.where(lax.axis_index("blk") % 2 == 0, orbitals, far)
-    relay, diagonals, weights, own = lax.optimization_barrier((relay, diagonals, weights, own))
+    top = slabs // 2
+    half = orb_count // 2
+    even = lax.axis_index("blk") % 2 == 0
+
+    def shifted(x):
+        return lax.ppermute(x, "blk", [(i, (i + 2) % blocks) for i in range(blocks)])
+
+    def relayed(mine, received):
+        return exchanged(jnp.where(even, mine, received), "blk", 1)
+
+    mine = lax.optimization_barrier([orbitals[:half], orbitals[half:]])
+    far = [shifted(mine[i]) for i in range(2)]
+    across = exchanged(orbitals, "grid", top)
+    across_half = lax.optimization_barrier(across[:half])
+    first, diagonals, weights = lax.optimization_barrier((far[0], diagonals, weights))
     tables = (order.astype(jnp.int32), diagonals, weights)
-    near = exchanged(relay, "blk", 1)
-    far = gathered(far)
+    near = [relayed(mine[0], first), relayed(mine[1], far[1])]
+    far_other = [shifted(across_half), exchanged(far[1], "grid", top)]
+    near_other = [relayed(across_half, far_other[0]), exchanged(near[1], "grid", top)]
+
+    own = {}
+    for r in range(top):
+        for held, block in ((0, orbitals), (top, across)):
+            piece = lax.dynamic_index_in_dim(block, grid_index ^ r, 0, keepdims=False)
+            own[r | held] = exchanged(piece, "grid", r) if r else piece
+    own = [own[r] for r in range(slabs)]
+
+    far = [completed(far[i], far_other[i]) for i in range(2)]
     acc = add_block(own, far, tables, None, jax.ShapeDtypeStruct((NX, plane_cells), F32))
-    near, acc = gathered(near, acc)
+    near_other, acc = lax.optimization_barrier((near_other, acc))
+    near = [completed(near[i], near_other[i]) for i in range(2)]
     chunk = plane_cells // blocks
     if chunk % LANES == 0:
         shape = (blocks, slabs, slab_rows, chunk)

time: 92.5 us -> 95.6 us (1.034)
  starting transfers between devices: 8.11 us -> 15.2 us
  waiting for transfers between devices: 20.4 us -> 18 us
  local copies, waits for them, and re-layouts: 4.47 us -> 2.88 us
  blocking collectives: 30.7 us -> 31.8 us
  other arithmetic: 2.85 us -> 1.86 us
    ppermute x10 -> x16, starting transfers between devices: 5 us -> 11.9 us  [exchanged(): lax.ppermute(x, axis, [(i, i ^ by) for i in range(lax.axis_size(axis))])]
    ppermute x10 -> x16, waiting for transfers between devices: 14.7 us -> 8.86 us  [exchanged(): lax.ppermute(x, axis, [(i, i ^ by) for i in range(lax.axis_size(axis))])]
    ppermute x1 -> x3, waiting for transfers between devices: 5.72 us -> 9.09 us  [shifted(): lax.ppermute(x, 'blk', [(i, (i + 2) % blocks) for i in range(blocks)])]
    unnamed x4, local copies, waits for them, and re-layouts: 2.58 us -> 0.01 us
    all_to_all x1, blocking collectives: 19.2 us -> 20.3 us  [body(): cellwise = lax.all_to_all(updated, ('blk', 'grid'), 0, 0, tiled=True)]
    slice x0 -> x2, local copies, waits for them, and re-layouts: none -> 1.09 us  [the longest x1 1.07 us: body(): mine = lax.optimization_barrier([orbitals[:half], orbitals[half:]])]
    select_n x1 -> x3, other arithmetic: 1.1 us -> 0.09 us  [relayed(): return exchanged(jnp.where(even, mine, received), 'blk', 1)]
    ppermute x1 -> x3, starting transfers between devices: 3.1 us -> 3.26 us  [shifted(): lax.ppermute(x, 'blk', [(i, (i + 2) % blocks) for i in range(blocks)])]
  transfers between devices with their start and end apart: 11 -> 19, of which waited for: 5 -> 7; matrix products, arithmetic and copies ran while one was open for 5% -> 5% of each run, Pallas kernels for 12% -> 11%
where the time goes in v2:
time: 95.6 us; the launch traced here: 95.2 us
  blocking collectives  31.8 us (33%)
  Pallas kernels  24.7 us (26%)
  waiting for transfers between devices  18 us (19%)
  starting transfers between devices  15.2 us (16%)
  local copies, waits for them, and re-layouts  2.88 us (3%)
  other arithmetic  1.86 us (2%)
    all_to_all x1, blocking collectives, body(): cellwise = lax.all_to_all(updated, ('blk', 'grid'), 0, 0, tiled=True)  20.3 us
    pallas_call x2, Pallas kernels, add_block(): pl.pallas_call(lambda *refs: block_kernel(slabs, len(src), final, refs),...  16.3 us
    ppermute x16, starting transfers between devices, exchanged(): lax.ppermute(x, axis, [(i, i ^ by) for i in range(lax.axis_size(axis))])  11.9 us
    all_to_all x1, blocking collectives, body(): parts = lax.all_to_all(local, ('blk', 'grid'), 0, 0, tiled=True)  11.5 us
    ppermute x3, waiting for transfers between devices, shifted(): lax.ppermute(x, 'blk', [(i, (i + 2) % blocks) for i in range(blocks)])  9.09 us
    ppermute x16, waiting for transfers between devices, exchanged(): lax.ppermute(x, axis, [(i, i ^ by) for i in range(lax.axis_size(axis))])  8.86 us
    pallas_call x1, Pallas kernels, body(): pl.pallas_call(functools.partial(rotate_kernel, 1.0 / cell_count), out_sh...  3.49 us
    ppermute x3, starting transfers between devices, shifted(): lax.ppermute(x, 'blk', [(i, (i + 2) % blocks) for i in range(blocks)])  3.26 us
  transfers between devices with their start and end apart: 19, of which 7 were waited for; matrix products, arithmetic and copies ran while one was open for 5% of the time, Pallas kernels for 11%

profile of v2, /device:TPU:0, one launch (start us, length us, event | category | flops | bytes accessed | tf_op | source)
XLA Modules:
  0.0 95.2 jit_solution(16921691986126117783)
XLA Ops:
  0.6 3.0 %collective-permute-start.1 = (bf16[4,16,4096]{2,1,0:T(8,128)(2,1)}, bf16[4,16,4096]{2,1,0:T(8,128)(2,1)S(1)}, u32[]{:S(2)}, u32[]{:S(2)}) collective-permute-start(bf16[4,16,4096]{2,1,0:T(8,128)(2,1)} %param.1), channel_id=1, source_target_pairs={{0,2},{1,3},{2,0},{3,1},{4,6},{5,7},{6,4},{7,5},{8,10},{9,11},{10,... | collective-permute-start | bytes 1572872 | tf_op jit(solution)/shard_map/ppermute | solution.py:260
  3.7 1.0 %dynamic-slice_bitcast_fusion.2 = (bf16[16,4096]{1,0:T(8,128)(2,1)S(1)}, bf16[16,4096]{1,0:T(8,128)(2,1)S(1)}) fusion(bf16[4,16,4096]{2,1,0:T(8,128)(2,1)} %param.1, s32[]{:T(128)S(6)} %select_n.33, s32[]{:T(128)S(6)} %select_n.32), kind=kLoop, calls=%fused_computation.5 | loop fusion | bytes 524296 | tf_op jit(solution)/shard_map/jit(dynamic_index_in_dim)/squeeze | solution.py:308
  4.7 0.1 collective-permute-start
  4.7 1.1 %fusion.5 = (bf16[2,16,4096]{2,1,0:T(8,128)(2,1)S(1)}, bf16[2,16,4096]{2,1,0:T(8,128)(2,1)S(1)}) fusion(bf16[4,16,4096]{2,1,0:T(8,128)(2,1)} %param.1), kind=kLoop, calls=%fused_computation.21 | loop fusion | bytes 1048576 | tf_op jit(solution)/shard_map/slice | solution.py:295
  5.8 1.6 %collective-permute-start.3 = (bf16[2,16,4096]{2,1,0:T(8,128)(2,1)S(1)}, bf16[2,16,4096]{2,1,0:T(8,128)(2,1)S(1)}, u32[]{:S(2)}, u32[]{:S(2)}) collective-permute-start(bf16[2,16,4096]{2,1,0:T(8,128)(2,1)S(1)} %get-tuple-element.12), channel_id=1, source_target_pairs={{0,8},{4,12},{8,16},{12,20},{16,24},{20,28},{24,0},{28,4},{1,9},{5... | collective-permute-start | bytes 786440 | tf_op jit(solution)/shard_map/ppermute | solution.py:290
  7.4 1.6 %collective-permute-start.8 = (bf16[2,16,4096]{2,1,0:T(8,128)(2,1)S(1)}, bf16[2,16,4096]{2,1,0:T(8,128)(2,1)S(1)}, u32[]{:S(2)}, u32[]{:S(2)}) collective-permute-start(bf16[2,16,4096]{2,1,0:T(8,128)(2,1)S(1)} %get-tuple-element.16), channel_id=1, source_target_pairs={{0,8},{4,12},{8,16},{12,20},{16,24},{20,28},{24,0},{28,4},{1,9},{5... | collective-permute-start | bytes 786440 | tf_op jit(solution)/shard_map/ppermute | solution.py:290
  9.0 0.1 add_convert_fusion
  9.1 0.1 convert_element_type.55
  9.2 1.0 %multiply_convert_fusion.sine_ref = bf16[3,64,64]{2,1,0:T(8,128)(2,1)} fusion(f32[3,64]{1,0:T(4,128)S(1)} %get-tuple-element.29, f32[3,64]{1,0:T(4,128)S(1)} %get-tuple-element.28), kind=kLoop, calls=%fused_computation.7 | loop fusion | flops 49152 | bytes 26112 | tf_op jit(solution)/shard_map/convert_element_type | solution.py:36
  10.3 0.6 maximum_bitcast_fusion.lanes_ref
  10.9 0.7 broadcast_in_dim.4.lam_ref
  11.6 2.6 %shard_map.30 = (bf16[3,256,256]{2,1,0:T(8,128)(2,1)}, f32[4096,128]{1,0:T(8,128)}) custom-call(bf16[3,64,64]{2,1,0:T(8,128)(2,1)} %multiply_convert_fusion.sine_ref, f32[64,128]{1,0:T(8,128)} %broadcast_in_dim.4.lam_ref, f32[1,128]{1,0:T(1,128)} %maximum_bitcast_fusion.lanes_ref), custom_call_target="tpu_custom_call" | custom-call | flops 67108864 | bytes 3145728 | tf_op jit(solution)/shard_map/pallas_call | solution.py:67
  14.2 2.7 %collective-permute-done.3.refs_4_ = bf16[2,16,4096]{2,1,0:T(8,128)(2,1)S(1)} collective-permute-done((bf16[2,16,4096]{2,1,0:T(8,128)(2,1)S(1)}, bf16[2,16,4096]{2,1,0:T(8,128)(2,1)S(1)}, u32[]{:S(2)}, u32[]{:S(2)}) %collective-permute-start.3) | collective-permute-done | bytes 262176 | tf_op jit(solution)/shard_map/ppermute | solution.py:290
  16.9 5.2 %collective-permute-done.8.refs_8_ = bf16[2,16,4096]{2,1,0:T(8,128)(2,1)S(1)} collective-permute-done((bf16[2,16,4096]{2,1,0:T(8,128)(2,1)S(1)}, bf16[2,16,4096]{2,1,0:T(8,128)(2,1)S(1)}, u32[]{:S(2)}, u32[]{:S(2)}) %collective-permute-start.8) | collective-permute-done | bytes 262176 | tf_op jit(solution)/shard_map/ppermute | solution.py:290
  22.0 0.5 collective-permute-start.14
  22.6 0.0 collective-permute-start.13
  22.6 0.5 collective-permute-start.11
  23.1 0.0 collective-permute-done.1
  23.2 0.1 collective-permute-start.6
  23.3 0.0 collective-permute-done.refs_1_
  23.3 1.6 %collective-permute-start.9 = (bf16[2,16,4096]{2,1,0:T(8,128)(2,1)S(1)}, bf16[2,16,4096]{2,1,0:T(8,128)(2,1)S(1)}, u32[]{:S(2)}, u32[]{:S(2)}) collective-permute-start(bf16[2,16,4096]{2,1,0:T(8,128)(2,1)S(1)} %broadcast_select_fusion), channel_id=1, source_target_pairs={{0,4},{4,0},{8,12},{12,8},{16,20},{20,16},{24,28},{28,24},{1,5},{5... | collective-permute-start | bytes 786440 | tf_op jit(solution)/shard_map/ppermute | solution.py:260
  24.9 5.1 %collective-permute-done.14.refs_10_ = bf16[2,16,4096]{2,1,0:T(8,128)(2,1)S(1)} collective-permute-done((bf16[2,16,4096]{2,1,0:T(8,128)(2,1)S(1)}, bf16[2,16,4096]{2,1,0:T(8,128)(2,1)S(1)}, u32[]{:S(2)}, u32[]{:S(2)}) %collective-permute-start.14) | collective-permute-done | bytes 262176 | tf_op jit(solution)/shard_map/ppermute | solution.py:260
  30.0 1.5 %collective-permute-start.4 = (bf16[2,16,4096]{2,1,0:T(8,128)(2,1)S(1)}, bf16[2,16,4096]{2,1,0:T(8,128)(2,1)S(1)}, u32[]{:S(2)}, u32[]{:S(2)}) collective-permute-start(bf16[2,16,4096]{2,1,0:T(8,128)(2,1)S(1)} %broadcast_select_fusion.2), channel_id=1, source_target_pairs={{0,4},{4,0},{8,12},{12,8},{16,20},{20,16},{24,28},{28,24},{1,5},{5... | collective-permute-start | bytes 786440 | tf_op jit(solution)/shard_map/ppermute | solution.py:260
  31.5 0.0 collective-permute-done.13.refs_9_
  31.5 0.0 collective-permute-start.2
  31.5 0.0 collective-permute-done.11.refs_5_
  31.5 0.5 collective-permute-start.15
  32.0 1.2 %collective-permute-done.6.refs_6_ = bf16[2,16,4096]{2,1,0:T(8,128)(2,1)S(1)} collective-permute-done((bf16[2,16,4096]{2,1,0:T(8,128)(2,1)S(1)}, bf16[2,16,4096]{2,1,0:T(8,128)(2,1)S(1)}, u32[]{:S(2)}, u32[]{:S(2)}) %collective-permute-start.6) | collective-permute-done | bytes 262176 | tf_op jit(solution)/shard_map/ppermute | solution.py:290
  33.2 0.0 collective-permute-start.12
  33.3 1.6 %collective-permute-start.10 = (bf16[2,16,4096]{2,1,0:T(8,128)(2,1)S(1)}, bf16[2,16,4096]{2,1,0:T(8,128)(2,1)S(1)}, u32[]{:S(2)}, u32[]{:S(2)}) collective-permute-start(bf16[2,16,4096]{2,1,0:T(8,128)(2,1)S(1)} %collective-permute-done.9.refs_8_), channel_id=1, source_target_pairs={{0,2},{1,3},{2,0},{3,1},{4,6},{5,7},{6,4},{7,5},{8,10},{9,11},{10,... | collective-permute-start | bytes 786440 | tf_op jit(solution)/shard_map/ppermute | solution.py:260
  34.8 2.3 %collective-permute-done.4.refs_4_ = bf16[2,16,4096]{2,1,0:T(8,128)(2,1)S(1)} collective-permute-done((bf16[2,16,4096]{2,1,0:T(8,128)(2,1)S(1)}, bf16[2,16,4096]{2,1,0:T(8,128)(2,1)S(1)}, u32[]{:S(2)}, u32[]{:S(2)}) %collective-permute-start.4) | collective-permute-done | bytes 262176 | tf_op jit(solution)/shard_map/ppermute | solution.py:260
  37.2 0.0 collective-permute-done.2.refs_3_
  37.2 0.5 collective-permute-start.5
  37.7 0.0 collective-permute-done.15.refs_11_
  37.7 1.5 %collective-permute-start.7 = (bf16[2,16,4096]{2,1,0:T(8,128)(2,1)S(1)}, bf16[2,16,4096]{2,1,0:T(8,128)(2,1)S(1)}, u32[]{:S(2)}, u32[]{:S(2)}) collective-permute-start(bf16[2,16,4096]{2,1,0:T(8,128)(2,1)S(1)} %broadcast_select_fusion.1), channel_id=1, source_target_pairs={{0,4},{4,0},{8,12},{12,8},{16,20},{20,16},{24,28},{28,24},{1,5},{5... | collective-permute-start | bytes 786440 | tf_op jit(solution)/shard_map/ppermute | solution.py:260
  39.2 8.1 %shard_map.31.refs_15_ = f32[64,4096]{1,0:T(8,128)S(1)} custom-call(bf16[16,4096]{1,0:T(8,128)(2,1)S(1)} %get-tuple-element.27.refs_0_, bf16[16,4096]{1,0:T(8,128)(2,1)S(1)} %collective-permute-done.refs_1_, bf16[16,4096]{1,0:T(8,128)(2,1)S(1)} %get-tuple-element.25.refs_2_, bf16[16,4096]{1,0:T(8,128)(2,1)S(1)} %collective-permute-done.2.refs_3_, ...), custom_call_target="tpu_custom_call" | custom-call | flops 3221225472 | bytes 8388608 | tf_op jit(solution)/shard_map/pallas_call | solution.py:188
  47.4 0.0 collective-permute-done.7.refs_6_
  47.4 0.1 collective-permute-start.16
  47.5 0.5 collective-permute-start.18
  48.0 0.0 collective-permute-done.5.refs_5_
  48.0 0.0 collective-permute-done.17.refs_9_
  48.0 1.0 %collective-permute-done.16.refs_7_ = bf16[2,16,4096]{2,1,0:T(8,128)(2,1)S(1)} collective-permute-done((bf16[2,16,4096]{2,1,0:T(8,128)(2,1)S(1)}, bf16[2,16,4096]{2,1,0:T(8,128)(2,1)S(1)}, u32[]{:S(2)}, u32[]{:S(2)}) %collective-permute-start.16) | collective-permute-done | bytes 262176 | tf_op jit(solution)/shard_map/ppermute | solution.py:260
  49.0 0.4 collective-permute-done.18.refs_11_
  49.4 8.1 %shard_map.32 = bf16[8,4,16,512]{3,2,1,0:T(8,128)(2,1)S(1)} custom-call(bf16[16,4096]{1,0:T(8,128)(2,1)S(1)} %get-tuple-element.27.refs_0_, bf16[16,4096]{1,0:T(8,128)(2,1)S(1)} %collective-permute-done.refs_1_, bf16[16,4096]{1,0:T(8,128)(2,1)S(1)} %get-tuple-element.25.refs_2_, bf16[16,4096]{1,0:T(8,128)(2,1)S(1)} %collective-permute-done.2.refs_3_, ...), custom_call_target="tpu_custom_call" | custom-call | flops 3221225472 | bytes 8388608 | tf_op jit(solution)/shard_map/pallas_call | solution.py:188
  57.5 20.3 %all_to_all.10.x_ref = bf16[32,16,512]{2,1,0:T(8,128)(2,1)} all-to-all(bf16[32,16,512]{2,1,0:T(8,128)(2,1)S(1)} %bitcast.11), channel_id=1, replica_groups=mesh['blk'=8,'grid'=4] {'blk','grid'}, dimensions={0} | all-to-all | bytes 1048576 | tf_op jit(solution)/shard_map/all_to_all | solution.py:325
  77.8 2.4 %shard_map.33 = f32[32,8,128]{2,1,0:T(8,128)} custom-call(bf16[32,16,512]{2,1,0:T(8,128)(2,1)} %all_to_all.10.x_ref), custom_call_target="tpu_custom_call" | custom-call | tf_op jit(solution)/shard_map/pallas_call | solution.py:330
  80.2 11.5 %all_to_all.11.parts_ref = f32[32,8,128]{2,1,0:T(8,128)} all-to-all(f32[32,8,128]{2,1,0:T(8,128)} %shard_map.33), channel_id=1, replica_groups=mesh['blk'=8,'grid'=4] {'blk','grid'}, dimensions={0} | all-to-all | bytes 262144 | tf_op jit(solution)/shard_map/all_to_all | solution.py:336
  91.7 3.5 %shard_map.34 = (bf16[32,16,512]{2,1,0:T(8,128)(2,1)}, f32[32,32]{1,0:T(8,128)}) custom-call(f32[32,8,128]{2,1,0:T(8,128)} %all_to_all.11.parts_ref, bf16[32,16,512]{2,1,0:T(8,128)(2,1)} %all_to_all.10.x_ref), custom_call_target="tpu_custom_call" | custom-call | tf_op jit(solution)/shard_map/pallas_call | solution.py:337
  (18 shorter events, 0.2 us)
Async XLA Ops:
  0.6 22.5 %collective-permute-start.1 = (bf16[4,16,4096]{2,1,0:T(8,128)(2,1)}, bf16[4,16,4096]{2,1,0:T(8,128)(2,1)S(1)}, u32[]{:S(2)}, u32[]{:S(2)}) collective-permute-start(bf16[4,16,4096]{2,1,0:T(8,128)(2,1)} %param.1), channel_id=1, source_target_pairs={{0,2},{1,3},{2,0},{3,1},{4,6},{5,7},{6,4},{7,5},{8,10},{9,11},{10,... | collective-permute-start | bytes 1572872 | tf_op jit(solution)/shard_map/ppermute | solution.py:260
  4.7 18.6 %collective-permute-start = (bf16[16,4096]{1,0:T(8,128)(2,1)S(1)}, bf16[16,4096]{1,0:T(8,128)(2,1)S(1)}, u32[]{:S(2)}, u32[]{:S(2)}) collective-permute-start(bf16[16,4096]{1,0:T(8,128)(2,1)S(1)} %get-tuple-element.26), channel_id=1, source_target_pairs={{0,1},{1,0},{2,3},{3,2},{4,5},{5,4},{6,7},{7,6},{8,9},{9,8},{10,11... | collective-permute-start | bytes 393224 | tf_op jit(solution)/shard_map/ppermute | solution.py:260
  5.8 11.0 %collective-permute-start.3 = (bf16[2,16,4096]{2,1,0:T(8,128)(2,1)S(1)}, bf16[2,16,4096]{2,1,0:T(8,128)(2,1)S(1)}, u32[]{:S(2)}, u32[]{:S(2)}) collective-permute-start(bf16[2,16,4096]{2,1,0:T(8,128)(2,1)S(1)} %get-tuple-element.12), channel_id=1, source_target_pairs={{0,8},{4,12},{8,16},{12,20},{16,24},{20,28},{24,0},{28,4},{1,9},{5... | collective-permute-start | bytes 786440 | tf_op jit(solution)/shard_map/ppermute | solution.py:290
  7.4 14.6 %collective-permute-start.8 = (bf16[2,16,4096]{2,1,0:T(8,128)(2,1)S(1)}, bf16[2,16,4096]{2,1,0:T(8,128)(2,1)S(1)}, u32[]{:S(2)}, u32[]{:S(2)}) collective-permute-start(bf16[2,16,4096]{2,1,0:T(8,128)(2,1)S(1)} %get-tuple-element.16), channel_id=1, source_target_pairs={{0,8},{4,12},{8,16},{12,20},{16,24},{20,28},{24,0},{28,4},{1,9},{5... | collective-permute-start | bytes 786440 | tf_op jit(solution)/shard_map/ppermute | solution.py:290
  14.1 25.1 %copy-start = (f32[4096,128]{1,0:T(8,128)S(1)}, f32[4096,128]{1,0:T(8,128)}, u32[]{:S(2)}) copy-start(f32[4096,128]{1,0:T(8,128)} %get-tuple-element.18.refs_14_) | copy-start | bytes 6291460
  14.1 25.1 %copy-start.1 = (bf16[3,256,256]{2,1,0:T(8,128)(2,1)S(1)}, bf16[3,256,256]{2,1,0:T(8,128)(2,1)}, u32[]{:S(2)}) copy-start(bf16[3,256,256]{2,1,0:T(8,128)(2,1)} %get-tuple-element.17.refs_13_) | copy-start | bytes 1179652
  22.0 7.9 %collective-permute-start.14 = (bf16[2,16,4096]{2,1,0:T(8,128)(2,1)S(1)}, bf16[2,16,4096]{2,1,0:T(8,128)(2,1)S(1)}, u32[]{:S(2)}, u32[]{:S(2)}) collective-permute-start(bf16[2,16,4096]{2,1,0:T(8,128)(2,1)S(1)} %collective-permute-done.8.refs_8_), channel_id=1, source_target_pairs={{0,2},{1,3},{2,0},{3,1},{4,6},{5,7},{6,4},{7,5},{8,10},{9,11},{10,... | collective-permute-start | bytes 786440 | tf_op jit(solution)/shard_map/ppermute | solution.py:260
  22.6 8.9 %collective-permute-start.13 = (bf16[2,16,4096]{2,1,0:T(8,128)(2,1)S(1)}, bf16[2,16,4096]{2,1,0:T(8,128)(2,1)S(1)}, u32[]{:S(2)}, u32[]{:S(2)}) collective-permute-start(bf16[2,16,4096]{2,1,0:T(8,128)(2,1)S(1)} %collective-permute-done.8.refs_8_), channel_id=1, source_target_pairs={{0,1},{1,0},{2,3},{3,2},{4,5},{5,4},{6,7},{7,6},{8,9},{9,8},{10,11... | collective-permute-start | bytes 786440 | tf_op jit(solution)/shard_map/ppermute | solution.py:260
  22.6 8.9 %collective-permute-start.11 = (bf16[2,16,4096]{2,1,0:T(8,128)(2,1)S(1)}, bf16[2,16,4096]{2,1,0:T(8,128)(2,1)S(1)}, u32[]{:S(2)}, u32[]{:S(2)}) collective-permute-start(bf16[2,16,4096]{2,1,0:T(8,128)(2,1)S(1)} %collective-permute-done.3.refs_4_), channel_id=1, source_target_pairs={{0,1},{1,0},{2,3},{3,2},{4,5},{5,4},{6,7},{7,6},{8,9},{9,8},{10,11... | collective-permute-start | bytes 786440 | tf_op jit(solution)/shard_map/ppermute | solution.py:260
  23.2 10.1 %collective-permute-start.6 = (bf16[2,16,4096]{2,1,0:T(8,128)(2,1)S(1)}, bf16[2,16,4096]{2,1,0:T(8,128)(2,1)S(1)}, u32[]{:S(2)}, u32[]{:S(2)}) collective-permute-start(bf16[2,16,4096]{2,1,0:T(8,128)(2,1)S(1)} %slice.12), channel_id=1, source_target_pairs={{0,8},{4,12},{8,16},{12,20},{16,24},{20,28},{24,0},{28,4},{1,9},{5... | collective-permute-start | bytes 786440 | tf_op jit(solution)/shard_map/ppermute | solution.py:290
  23.3 10.0 %collective-permute-start.9 = (bf16[2,16,4096]{2,1,0:T(8,128)(2,1)S(1)}, bf16[2,16,4096]{2,1,0:T(8,128)(2,1)S(1)}, u32[]{:S(2)}, u32[]{:S(2)}) collective-permute-start(bf16[2,16,4096]{2,1,0:T(8,128)(2,1)S(1)} %broadcast_select_fusion), channel_id=1, source_target_pairs={{0,4},{4,0},{8,12},{12,8},{16,20},{20,16},{24,28},{28,24},{1,5},{5... | collective-permute-start | bytes 786440 | tf_op jit(solution)/shard_map/ppermute | solution.py:260
  30.0 7.2 %collective-permute-start.4 = (bf16[2,16,4096]{2,1,0:T(8,128)(2,1)S(1)}, bf16[2,16,4096]{2,1,0:T(8,128)(2,1)S(1)}, u32[]{:S(2)}, u32[]{:S(2)}) collective-permute-start(bf16[2,16,4096]{2,1,0:T(8,128)(2,1)S(1)} %broadcast_select_fusion.2), channel_id=1, source_target_pairs={{0,4},{4,0},{8,12},{12,8},{16,20},{20,16},{24,28},{28,24},{1,5},{5... | collective-permute-start | bytes 786440 | tf_op jit(solution)/shard_map/ppermute | solution.py:260
  31.5 5.7 %collective-permute-start.2 = (bf16[16,4096]{1,0:T(8,128)(2,1)S(1)}, bf16[16,4096]{1,0:T(8,128)(2,1)S(1)}, u32[]{:S(2)}, u32[]{:S(2)}) collective-permute-start(bf16[16,4096]{1,0:T(8,128)(2,1)S(1)} %get-tuple-element.24), channel_id=1, source_target_pairs={{0,1},{1,0},{2,3},{3,2},{4,5},{5,4},{6,7},{7,6},{8,9},{9,8},{10,11... | collective-permute-start | bytes 393224 | tf_op jit(solution)/shard_map/ppermute | solution.py:260
  31.5 6.2 %collective-permute-start.15 = (bf16[2,16,4096]{2,1,0:T(8,128)(2,1)S(1)}, bf16[2,16,4096]{2,1,0:T(8,128)(2,1)S(1)}, u32[]{:S(2)}, u32[]{:S(2)}) collective-permute-start(bf16[2,16,4096]{2,1,0:T(8,128)(2,1)S(1)} %collective-permute-done.14.refs_10_), channel_id=1, source_target_pairs={{0,1},{1,0},{2,3},{3,2},{4,5},{5,4},{6,7},{7,6},{8,9},{9,8},{10,11... | collective-permute-start | bytes 786440 | tf_op jit(solution)/shard_map/ppermute | solution.py:260
  33.2 6.0 %collective-permute-start.12 = (bf16[2,16,4096]{2,1,0:T(8,128)(2,1)S(1)}, bf16[2,16,4096]{2,1,0:T(8,128)(2,1)S(1)}, u32[]{:S(2)}, u32[]{:S(2)}) collective-permute-start(bf16[2,16,4096]{2,1,0:T(8,128)(2,1)S(1)} %collective-permute-done.6.refs_6_), channel_id=1, source_target_pairs={{0,1},{1,0},{2,3},{3,2},{4,5},{5,4},{6,7},{7,6},{8,9},{9,8},{10,11... | collective-permute-start | bytes 786440 | tf_op jit(solution)/shard_map/ppermute | solution.py:260
  33.3 14.1 %collective-permute-start.10 = (bf16[2,16,4096]{2,1,0:T(8,128)(2,1)S(1)}, bf16[2,16,4096]{2,1,0:T(8,128)(2,1)S(1)}, u32[]{:S(2)}, u32[]{:S(2)}) collective-permute-start(bf16[2,16,4096]{2,1,0:T(8,128)(2,1)S(1)} %collective-permute-done.9.refs_8_), channel_id=1, source_target_pairs={{0,2},{1,3},{2,0},{3,1},{4,6},{5,7},{6,4},{7,5},{8,10},{9,11},{10,... | collective-permute-start | bytes 786440 | tf_op jit(solution)/shard_map/ppermute | solution.py:260
  37.2 10.8 %collective-permute-start.17 = (bf16[2,16,4096]{2,1,0:T(8,128)(2,1)S(1)}, bf16[2,16,4096]{2,1,0:T(8,128)(2,1)S(1)}, u32[]{:S(2)}, u32[]{:S(2)}) collective-permute-start(bf16[2,16,4096]{2,1,0:T(8,128)(2,1)S(1)} %collective-permute-done.9.refs_8_), channel_id=1, source_target_pairs={{0,1},{1,0},{2,3},{3,2},{4,5},{5,4},{6,7},{7,6},{8,9},{9,8},{10,11... | collective-permute-start | bytes 786440 | tf_op jit(solution)/shard_map/ppermute | solution.py:260
  37.2 10.8 %collective-permute-start.5 = (bf16[2,16,4096]{2,1,0:T(8,128)(2,1)S(1)}, bf16[2,16,4096]{2,1,0:T(8,128)(2,1)S(1)}, u32[]{:S(2)}, u32[]{:S(2)}) collective-permute-start(bf16[2,16,4096]{2,1,0:T(8,128)(2,1)S(1)} %collective-permute-done.4.refs_4_), channel_id=1, source_target_pairs={{0,1},{1,0},{2,3},{3,2},{4,5},{5,4},{6,7},{7,6},{8,9},{9,8},{10,11... | collective-permute-start | bytes 786440 | tf_op jit(solution)/shard_map/ppermute | solution.py:260
  37.7 9.7 %collective-permute-start.7 = (bf16[2,16,4096]{2,1,0:T(8,128)(2,1)S(1)}, bf16[2,16,4096]{2,1,0:T(8,128)(2,1)S(1)}, u32[]{:S(2)}, u32[]{:S(2)}) collective-permute-start(bf16[2,16,4096]{2,1,0:T(8,128)(2,1)S(1)} %broadcast_select_fusion.1), channel_id=1, source_target_pairs={{0,4},{4,0},{8,12},{12,8},{16,20},{20,16},{24,28},{28,24},{1,5},{5... | collective-permute-start | bytes 786440 | tf_op jit(solution)/shard_map/ppermute | solution.py:260
  47.4 1.6 %collective-permute-start.16 = (bf16[2,16,4096]{2,1,0:T(8,128)(2,1)S(1)}, bf16[2,16,4096]{2,1,0:T(8,128)(2,1)S(1)}, u32[]{:S(2)}, u32[]{:S(2)}) collective-permute-start(bf16[2,16,4096]{2,1,0:T(8,128)(2,1)S(1)} %collective-permute-done.7.refs_6_), channel_id=1, source_target_pairs={{0,1},{1,0},{2,3},{3,2},{4,5},{5,4},{6,7},{7,6},{8,9},{9,8},{10,11... | collective-permute-start | bytes 786440 | tf_op jit(solution)/shard_map/ppermute | solution.py:260
  47.5 1.9 %collective-permute-start.18 = (bf16[2,16,4096]{2,1,0:T(8,128)(2,1)S(1)}, bf16[2,16,4096]{2,1,0:T(8,128)(2,1)S(1)}, u32[]{:S(2)}, u32[]{:S(2)}) collective-permute-start(bf16[2,16,4096]{2,1,0:T(8,128)(2,1)S(1)} %collective-permute-done.10.refs_10_), channel_id=1, source_target_pairs={{0,1},{1,0},{2,3},{3,2},{4,5},{5,4},{6,7},{7,6},{8,9},{9,8},{10,11... | collective-permute-start | bytes 786440 | tf_op jit(solution)/shard_map/ppermute | solution.py:260

commit v3 on v2

--- a/solution.py
+++ b/solution.py
@@ -21,9 +21,8 @@
 VMEM = pl.BlockSpec(memory_space=pltpu.VMEM)
 SMEM = pl.BlockSpec(memory_space=pltpu.SMEM)
 LANES = 128
-ROW_PAD = 8
+ROW_PAD = 1
 QUAD = 4
-UNROLL = 4
 PANEL = 8
 
 
@@ -31,50 +30,60 @@
     return jnp.dot(a, b, preferred_element_type=F32)
 
 
-def sine_tables(rows, columns):
-    angle = jnp.pi * (rows[:, :, None] + 1.0) * (columns[:, None, :] + 1.0) / (NX + 1)
-    return (jnp.sqrt(2.0 / (NX + 1)) * jnp.sin(angle)).astype(BF)
-
-
-def eigen_values(length):
-    index = jnp.arange(length).astype(F32)
+def sines(rows, columns, length):
+    angle = jnp.pi * (rows + 1.0) * (columns + 1.0) / (length + 1)
+    return jnp.sqrt(2.0 / (length + 1)) * jnp.sin(angle)
+
+
+def eigen_values(index, length):
     return 2.0 - 2.0 * jnp.cos(jnp.pi * (index + 1.0) / (length + 1))
 
 
-def table_kernel(sine_ref, lam_ref, lanes_ref, diag_ref, weight_ref):
-    count, n, _ = sine_ref.shape
+def table_kernel(slab_rows, order_ref, diag_ref, weight_ref):
     size = diag_ref.shape[1]
-    down = lax.broadcasted_iota(jnp.int32, (size, size), 0) // n
-    along = lax.broadcasted_iota(jnp.int32, (size, size), 1) // n
-    for i in range(count):
-        table = sine_ref[i].astype(F32)
-        table = jnp.concatenate([table] * (size // n), 1)
-        table = jnp.concatenate([table] * (size // n), 0)
-        diag_ref[i] = jnp.where(down == along, table, 0.0).astype(BF)
-    columns = lam_ref[...]
-    lanes = lanes_ref[...]
-    for k in range(n):
-        total = screening + columns[k:k + 1, :] + columns + lanes
-        weight_ref[k * n:(k + 1) * n, :] = 1.0 / total
-
-
-def make_tables(here):
-    cells = jnp.arange(NX).astype(F32)
-    here = here.astype(F32)
-    sine = sine_tables(jnp.stack([cells, cells, here]), jnp.stack([cells, here, cells]))
-    lam = eigen_values(NX)
+    copies = size // NX
+
+    def cells_of(position):
+        slab = position // slab_rows
+        start = jnp.zeros_like(position)
+        for r in range(NX // slab_rows):
+            start = jnp.where(slab == r, order_ref[r] * slab_rows, start)
+        return start + position % slab_rows
+
+    shape = (NX, LANES)
+    down = lax.broadcasted_iota(jnp.int32, shape, 0)
+    along = lax.broadcasted_iota(jnp.int32, shape, 1) % NX
+    pairs = (
+        (down, along),
+        (down, cells_of(along)),
+        (cells_of(down), along),
+    )
+    same = (
+        lax.broadcasted_iota(jnp.int32, (NX, size), 1) // NX
+    )
+    for i, (row, column) in enumerate(pairs):
+        table = sines(row.astype(F32), column.astype(F32), NX)
+        table = jnp.concatenate([table] * (size // LANES), 1)
+        for c in range(copies):
+            diag_ref[i, c * NX:(c + 1) * NX, :] = jnp.where(same == c, table, 0.0).astype(BF)
+    lam = eigen_values(down.astype(F32), NX)
+    plane = screening + lam + eigen_values(along.astype(F32), NZ)
+    for k in range(NX):
+        weight_ref[k * NY:(k + 1) * NY, :] = 1.0 / (lam[k:k + 1, :] + plane)
+
+
+def make_tables(order, slab_rows):
     size = QUAD * NX
     return pl.pallas_call(
-        table_kernel,
+        functools.partial(table_kernel, slab_rows),
         out_shape=(
             jax.ShapeDtypeStruct((3, size, size), BF),
             jax.ShapeDtypeStruct((NX * NY, LANES), F32),
         ),
-        in_specs=[VMEM] * 3,
+        in_specs=[SMEM],
         out_specs=(VMEM, VMEM),
-        cost_estimate=pl.CostEstimate(flops=1 << 26, bytes_accessed=3 << 20, transcendentals=0),
-    )(sine, jnp.broadcast_to(lam[:, None], (NX, LANES)),
-      jnp.concatenate([lam] * (LANES // NZ))[None, :])
+        cost_estimate=pl.CostEstimate(flops=1 << 28, bytes_accessed=3 << 20, transcendentals=0),
+    )(order)
 
 
 def block_kernel(slabs, parts, final, rest):
@@ -101,15 +110,15 @@
     def load_rows(first):
         parts = []
         for q in range(QUAD):
-            at = pl.multiple_of((first + q) * pitch, 8)
+            at = (first + q) * pitch
             parts.append(
                 jnp.concatenate([work_ref[h, pl.ds(at, NX), :] for h in range(halves)], 1)
             )
         return jnp.concatenate(parts, 0)
 
-    def forward(t, carry):
-        off = pl.multiple_of(t * width, width)
-        at = pl.multiple_of(t * QUAD * NX, QUAD * NX)
+    def forward(t):
+        off = t * width
+        at = t * QUAD * NX
         mine = tile(own, (), off, width)
         others = [tile(src[j // each], (j % each,), off, width) for j in range(count)]
         pairs = [mine * other for other in others]
@@ -121,13 +130,12 @@
         first = product(density, tab_ref[0]).astype(BF)
         modes = product(tab_ref[1], first)
         for q in range(QUAD):
-            to = pl.multiple_of((t * QUAD + q) * pitch, 8)
+            to = (t * QUAD + q) * pitch
             for h in range(halves):
                 work_ref[h, pl.ds(to, NX), :] = modes[q * NX:(q + 1) * NX, h * LANES:(h + 1) * LANES]
-        return carry
-
-    def solve(t, carry):
-        at = pl.multiple_of(t * QUAD * NY, QUAD * NY)
+
+    def solve(t):
+        at = t * QUAD * NY
         modes = jnp.concatenate([
             jnp.concatenate(
                 [work_ref[h, pl.ds(t * QUAD + q, NY, stride=pitch), :] for h in range(halves)], 1)
@@ -139,13 +147,12 @@
             for h in range(halves):
                 work_ref[h, pl.ds(t * QUAD + q, NY, stride=pitch), :] = (
                     back[q * NY:(q + 1) * NY, h * LANES:(h + 1) * LANES])
-        return carry
 
     lane = lax.broadcasted_iota(jnp.int32, (NX, LANES), 1)
     per_tile = LANES // NZ
 
-    def backward(t, carry):
-        at = pl.multiple_of(t * QUAD * NX, QUAD * NX)
+    def backward(t):
+        at = t * QUAD * NX
         third = product(tab_ref[2], load_rows(t * QUAD).astype(BF)).astype(BF)
         potential = product(third, tab_ref[0])
         terms = potential * grouped_ref[pl.ds(at, QUAD * NX), :].astype(F32)
@@ -156,7 +163,7 @@
         for q in range(0, QUAD, per_tile):
             exchange = jnp.where(
                 lane < NZ, total[q * NX:(q + 1) * NX], total[(q + 1) * NX:(q + 2) * NX])
-            off = pl.multiple_of((t * QUAD + q) * NZ, LANES)
+            off = (t * QUAD + q) * NZ
             if not final:
                 out_ref[:, pl.ds(off, LANES)] = exchange
                 continue
@@ -168,15 +175,14 @@
                 if len(out_ref.shape) == 4:
                     share = out_ref.shape[3] // LANES
                     index = (t * QUAD + q) * NZ // LANES
-                    to = pl.multiple_of((index % share) * LANES, LANES)
+                    to = (index % share) * LANES
                     out_ref[index // share, pos_ref[r], :, pl.ds(to, LANES)] = part
                 else:
                     out_ref[pos_ref[r], :, pl.ds(off, LANES)] = part
-        return carry
-
-    lax.fori_loop(0, NY // QUAD, forward, 0, unroll=UNROLL)
-    lax.fori_loop(0, NX // QUAD, solve, 0, unroll=UNROLL)
-    lax.fori_loop(0, NY // QUAD, backward, 0, unroll=UNROLL)
+
+    for step, trips in ((forward, NY // QUAD), (solve, NX // QUAD), (backward, NY // QUAD)):
+        for t in range(trips):
+            step(t)
 
 
 def add_block(own, src, tables, acc, out_shape):
@@ -277,11 +283,9 @@
     blocks = lax.axis_size("blk")
     assert orb_count == slabs and slab_rows * slabs == NX and blocks % 2 == 0 and STEPS == 2
     grid_index = lax.axis_index("grid")
-    order = jnp.arange(slabs) ^ grid_index
-
-    here = (order[:, None] * slab_rows + jnp.arange(slab_rows)[None, :]).reshape(NX)
-    diagonals, weights = make_tables(here)
-
+    order = (jnp.arange(slabs) ^ grid_index).astype(jnp.int32)
+
+    diagonals, weights = make_tables(order, slab_rows)
     top = slabs // 2
     half = orb_count // 2
     even = lax.axis_index("blk") % 2 == 0
@@ -296,10 +300,11 @@
     far = [shifted(mine[i]) for i in range(2)]
     across = exchanged(orbitals, "grid", top)
     across_half = lax.optimization_barrier(across[:half])
-    first, diagonals, weights = lax.optimization_barrier((far[0], diagonals, weights))
-    tables = (order.astype(jnp.int32), diagonals, weights)
-    near = [relayed(mine[0], first), relayed(mine[1], far[1])]
+    near = [relayed(mine[i], far[i]) for i in range(2)]
     far_other = [shifted(across_half), exchanged(far[1], "grid", top)]
+    across_half, diagonals, weights = lax.optimization_barrier(
+        (across_half, diagonals, weights))
+    tables = (order, diagonals, weights)
     near_other = [relayed(across_half, far_other[0]), exchanged(near[1], "grid", top)]
 
     own = {}

time: 95.6 us -> 88.3 us (0.924)
  Pallas kernels: 24.7 us -> 18.5 us
  waiting for transfers between devices: 18 us -> 20.7 us
  starting transfers between devices: 15.2 us -> 13.4 us
  other arithmetic: 1.86 us -> 0.6 us
    pallas_call x2, Pallas kernels: 16.3 us -> 9.68 us  [add_block(): pl.pallas_call(lambda *refs: block_kernel(slabs, len(src), final, refs),...]
    ppermute x3, waiting for transfers between devices: 9.09 us -> 13.8 us  [shifted(): lax.ppermute(x, 'blk', [(i, (i + 2) % blocks) for i in range(blocks)])]
    ppermute x16, waiting for transfers between devices: 8.86 us -> 6.9 us  [exchanged(): lax.ppermute(x, axis, [(i, i ^ by) for i in range(lax.axis_size(axis))])]
    ppermute x16, starting transfers between devices: 11.9 us -> 10.2 us  [exchanged(): lax.ppermute(x, axis, [(i, i ^ by) for i in range(lax.axis_size(axis))])]
    convert_element_type x3 -> x0, other arithmetic: 1.12 us -> none  [the longest x1 1.04 us: sine_tables(): return (jnp.sqrt(2.0 / (NX + 1)) * jnp.sin(angle)).astype(BF)]
  transfers between devices with their start and end apart: 19 -> 19, of which waited for: 7 -> 8; matrix products, arithmetic and copies ran while one was open for 5% -> 3% of each run, Pallas kernels for 11% -> 9%
where the time goes in v3:
time: 88.3 us; the launch traced here: 87.9 us
  blocking collectives  31.8 us (36%)
  waiting for transfers between devices  20.7 us (23%)
  Pallas kernels  18.5 us (21%)
  starting transfers between devices  13.4 us (15%)
  local copies, waits for them, and re-layouts  2.1 us (2%)
    all_to_all x1, blocking collectives, body(): cellwise = lax.all_to_all(updated, ('blk', 'grid'), 0, 0, tiled=True)  20.4 us
    ppermute x3, waiting for transfers between devices, shifted(): lax.ppermute(x, 'blk', [(i, (i + 2) % blocks) for i in range(blocks)])  13.8 us
    all_to_all x1, blocking collectives, body(): parts = lax.all_to_all(local, ('blk', 'grid'), 0, 0, tiled=True)  11.5 us
    ppermute x16, starting transfers between devices, exchanged(): lax.ppermute(x, axis, [(i, i ^ by) for i in range(lax.axis_size(axis))])  10.2 us
    pallas_call x2, Pallas kernels, add_block(): pl.pallas_call(lambda *refs: block_kernel(slabs, len(src), final, refs),...  9.68 us
    ppermute x16, waiting for transfers between devices, exchanged(): lax.ppermute(x, axis, [(i, i ^ by) for i in range(lax.axis_size(axis))])  6.9 us
    pallas_call x1, Pallas kernels, body(): pl.pallas_call(functools.partial(rotate_kernel, 1.0 / cell_count), out_sh...  3.49 us
    ppermute x3, starting transfers between devices, shifted(): lax.ppermute(x, 'blk', [(i, (i + 2) % blocks) for i in range(blocks)])  3.26 us
  transfers between devices with their start and end apart: 19, of which 8 were waited for; matrix products, arithmetic and copies ran while one was open for 3% of the time, Pallas kernels for 9%

profile of v3, /device:TPU:0, one launch (start us, length us, event | category | flops | bytes accessed | tf_op | source)
XLA Modules:
  0.0 87.9 jit_solution(2332716072853029362)
XLA Ops:
  0.6 3.0 %collective-permute-start.1 = (bf16[4,16,4096]{2,1,0:T(8,128)(2,1)}, bf16[4,16,4096]{2,1,0:T(8,128)(2,1)S(1)}, u32[]{:S(2)}, u32[]{:S(2)}) collective-permute-start(bf16[4,16,4096]{2,1,0:T(8,128)(2,1)} %param.1), channel_id=1, source_target_pairs={{0,2},{1,3},{2,0},{3,1},{4,6},{5,7},{6,4},{7,5},{8,10},{9,11},{10,... | collective-permute-start | bytes 1572872 | tf_op jit(solution)/shard_map/ppermute | solution.py:266
  3.7 1.1 %fusion = (bf16[2,16,4096]{2,1,0:T(8,128)(2,1)S(1)}, bf16[2,16,4096]{2,1,0:T(8,128)(2,1)S(1)}) fusion(bf16[4,16,4096]{2,1,0:T(8,128)(2,1)} %param.1), kind=kLoop, calls=%fused_computation.8 | loop fusion | bytes 1048576 | tf_op jit(solution)/shard_map/slice | solution.py:299
  4.7 1.6 %collective-permute-start.8 = (bf16[2,16,4096]{2,1,0:T(8,128)(2,1)S(1)}, bf16[2,16,4096]{2,1,0:T(8,128)(2,1)S(1)}, u32[]{:S(2)}, u32[]{:S(2)}) collective-permute-start(bf16[2,16,4096]{2,1,0:T(8,128)(2,1)S(1)} %get-tuple-element.16), channel_id=1, source_target_pairs={{0,8},{4,12},{8,16},{12,20},{16,24},{20,28},{24,0},{28,4},{1,9},{5... | collective-permute-start | bytes 786440 | tf_op jit(solution)/shard_map/ppermute | solution.py:294
  6.4 1.6 %collective-permute-start.3 = (bf16[2,16,4096]{2,1,0:T(8,128)(2,1)S(1)}, bf16[2,16,4096]{2,1,0:T(8,128)(2,1)S(1)}, u32[]{:S(2)}, u32[]{:S(2)}) collective-permute-start(bf16[2,16,4096]{2,1,0:T(8,128)(2,1)S(1)} %get-tuple-element.12), channel_id=1, source_target_pairs={{0,8},{4,12},{8,16},{12,20},{16,24},{20,28},{24,0},{28,4},{1,9},{5... | collective-permute-start | bytes 786440 | tf_op jit(solution)/shard_map/ppermute | solution.py:294
  7.9 1.0 %dynamic-slice_bitcast_fusion.2 = (bf16[16,4096]{1,0:T(8,128)(2,1)S(1)}, bf16[16,4096]{1,0:T(8,128)(2,1)S(1)}) fusion(bf16[4,16,4096]{2,1,0:T(8,128)(2,1)} %param.1, s32[]{:T(128)S(6)} %select_n.33, s32[]{:T(128)S(6)} %select_n.32), kind=kLoop, calls=%fused_computation.5 | loop fusion | bytes 524296 | tf_op jit(solution)/shard_map/jit(dynamic_index_in_dim)/squeeze | solution.py:313
  8.9 0.1 collective-permute-start
  9.0 0.5 iota_xor_fusion.order_ref.refs_12_
  9.5 2.9 %shard_map.30 = (bf16[3,256,256]{2,1,0:T(8,128)(2,1)}, f32[4096,128]{1,0:T(8,128)}) custom-call(s32[4]{0:T(128)} %iota_xor_fusion.order_ref.refs_12_), custom_call_target="tpu_custom_call" | custom-call | flops 268435456 | bytes 3145728 | tf_op jit(solution)/shard_map/pallas_call | solution.py:77
  12.4 3.3 %collective-permute-done.8.refs_8_ = bf16[2,16,4096]{2,1,0:T(8,128)(2,1)S(1)} collective-permute-done((bf16[2,16,4096]{2,1,0:T(8,128)(2,1)S(1)}, bf16[2,16,4096]{2,1,0:T(8,128)(2,1)S(1)}, u32[]{:S(2)}, u32[]{:S(2)}) %collective-permute-start.8) | collective-permute-done | bytes 262176 | tf_op jit(solution)/shard_map/ppermute | solution.py:294
  15.8 0.3 collective-permute-start.14
  16.1 0.0 collective-permute-start.13
  16.1 3.9 %collective-permute-done.3.refs_4_ = bf16[2,16,4096]{2,1,0:T(8,128)(2,1)S(1)} collective-permute-done((bf16[2,16,4096]{2,1,0:T(8,128)(2,1)S(1)}, bf16[2,16,4096]{2,1,0:T(8,128)(2,1)S(1)}, u32[]{:S(2)}, u32[]{:S(2)}) %collective-permute-start.3) | collective-permute-done | bytes 262176 | tf_op jit(solution)/shard_map/ppermute | solution.py:294
  20.0 0.0 collective-permute-start.11
  20.1 0.0 collective-permute-done.1
  20.1 0.1 collective-permute-start.6
  20.2 0.0 collective-permute-done.refs_1_
  20.2 1.6 %collective-permute-start.9 = (bf16[2,16,4096]{2,1,0:T(8,128)(2,1)S(1)}, bf16[2,16,4096]{2,1,0:T(8,128)(2,1)S(1)}, u32[]{:S(2)}, u32[]{:S(2)}) collective-permute-start(bf16[2,16,4096]{2,1,0:T(8,128)(2,1)S(1)} %broadcast_select_fusion), channel_id=1, source_target_pairs={{0,4},{4,0},{8,12},{12,8},{16,20},{20,16},{24,28},{28,24},{1,5},{5... | collective-permute-start | bytes 786440 | tf_op jit(solution)/shard_map/ppermute | solution.py:266
  21.8 0.3 collective-permute-done.14.refs_10_
  22.1 1.5 %collective-permute-start.4 = (bf16[2,16,4096]{2,1,0:T(8,128)(2,1)S(1)}, bf16[2,16,4096]{2,1,0:T(8,128)(2,1)S(1)}, u32[]{:S(2)}, u32[]{:S(2)}) collective-permute-start(bf16[2,16,4096]{2,1,0:T(8,128)(2,1)S(1)} %broadcast_select_fusion.2), channel_id=1, source_target_pairs={{0,4},{4,0},{8,12},{12,8},{16,20},{20,16},{24,28},{28,24},{1,5},{5... | collective-permute-start | bytes 786440 | tf_op jit(solution)/shard_map/ppermute | solution.py:266
  23.6 0.0 collective-permute-done.13.refs_9_
  23.7 0.0 collective-permute-start.2
  23.7 0.0 collective-permute-done.11.refs_5_
  23.7 0.5 collective-permute-start.15
  24.2 6.5 %collective-permute-done.6.refs_6_ = bf16[2,16,4096]{2,1,0:T(8,128)(2,1)S(1)} collective-permute-done((bf16[2,16,4096]{2,1,0:T(8,128)(2,1)S(1)}, bf16[2,16,4096]{2,1,0:T(8,128)(2,1)S(1)}, u32[]{:S(2)}, u32[]{:S(2)}) %collective-permute-start.6) | collective-permute-done | bytes 262176 | tf_op jit(solution)/shard_map/ppermute | solution.py:294
  30.7 0.0 collective-permute-start.12
  30.7 0.0 collective-permute-done.9.refs_8_
  30.8 0.6 collective-permute-start.10
  31.4 3.3 %collective-permute-done.4.refs_4_ = bf16[2,16,4096]{2,1,0:T(8,128)(2,1)S(1)} collective-permute-done((bf16[2,16,4096]{2,1,0:T(8,128)(2,1)S(1)}, bf16[2,16,4096]{2,1,0:T(8,128)(2,1)S(1)}, u32[]{:S(2)}, u32[]{:S(2)}) %collective-permute-start.4) | collective-permute-done | bytes 262176 | tf_op jit(solution)/shard_map/ppermute | solution.py:266
  34.7 0.0 collective-permute-start.17
  34.7 0.0 collective-permute-done.2.refs_3_
  34.7 0.5 collective-permute-start.5
  35.2 0.0 collective-permute-done.15.refs_11_
  35.2 1.5 %collective-permute-start.7 = (bf16[2,16,4096]{2,1,0:T(8,128)(2,1)S(1)}, bf16[2,16,4096]{2,1,0:T(8,128)(2,1)S(1)}, u32[]{:S(2)}, u32[]{:S(2)}) collective-permute-start(bf16[2,16,4096]{2,1,0:T(8,128)(2,1)S(1)} %broadcast_select_fusion.1), channel_id=1, source_target_pairs={{0,4},{4,0},{8,12},{12,8},{16,20},{20,16},{24,28},{28,24},{1,5},{5... | collective-permute-start | bytes 786440 | tf_op jit(solution)/shard_map/ppermute | solution.py:266
  36.7 0.0 collective-permute-done.12.refs_7_
  36.7 4.8 %shard_map.31.refs_15_ = f32[64,4096]{1,0:T(8,128)S(1)} custom-call(bf16[16,4096]{1,0:T(8,128)(2,1)S(1)} %get-tuple-element.27.refs_0_, bf16[16,4096]{1,0:T(8,128)(2,1)S(1)} %collective-permute-done.refs_1_, bf16[16,4096]{1,0:T(8,128)(2,1)S(1)} %get-tuple-element.25.refs_2_, bf16[16,4096]{1,0:T(8,128)(2,1)S(1)} %collective-permute-done.2.refs_3_, ...), custom_call_target="tpu_custom_call" | custom-call | flops 3221225472 | bytes 8388608 | tf_op jit(solution)/shard_map/pallas_call | solution.py:194
  41.6 0.0 collective-permute-done.10.refs_10_
  41.6 1.9 %collective-permute-done.7.refs_6_ = bf16[2,16,4096]{2,1,0:T(8,128)(2,1)S(1)} collective-permute-done((bf16[2,16,4096]{2,1,0:T(8,128)(2,1)S(1)}, bf16[2,16,4096]{2,1,0:T(8,128)(2,1)S(1)}, u32[]{:S(2)}, u32[]{:S(2)}) %collective-permute-start.7) | collective-permute-done | bytes 262176 | tf_op jit(solution)/shard_map/ppermute | solution.py:266
  43.5 0.0 collective-permute-start.16
  43.5 0.5 collective-permute-start.18
  44.0 0.0 collective-permute-done.17.refs_9_
  44.0 0.0 collective-permute-done.5.refs_5_
  44.0 1.0 %collective-permute-done.16.refs_7_ = bf16[2,16,4096]{2,1,0:T(8,128)(2,1)S(1)} collective-permute-done((bf16[2,16,4096]{2,1,0:T(8,128)(2,1)S(1)}, bf16[2,16,4096]{2,1,0:T(8,128)(2,1)S(1)}, u32[]{:S(2)}, u32[]{:S(2)}) %collective-permute-start.16) | collective-permute-done | bytes 262176 | tf_op jit(solution)/shard_map/ppermute | solution.py:266
  45.0 0.4 collective-permute-done.18.refs_11_
  45.4 4.8 %shard_map.32 = bf16[8,4,16,512]{3,2,1,0:T(8,128)(2,1)S(1)} custom-call(bf16[16,4096]{1,0:T(8,128)(2,1)S(1)} %get-tuple-element.27.refs_0_, bf16[16,4096]{1,0:T(8,128)(2,1)S(1)} %collective-permute-done.refs_1_, bf16[16,4096]{1,0:T(8,128)(2,1)S(1)} %get-tuple-element.25.refs_2_, bf16[16,4096]{1,0:T(8,128)(2,1)S(1)} %collective-permute-done.2.refs_3_, ...), custom_call_target="tpu_custom_call" | custom-call | flops 3221225472 | bytes 8388608 | tf_op jit(solution)/shard_map/pallas_call | solution.py:194
  50.2 20.4 %all_to_all.10.x_ref = bf16[32,16,512]{2,1,0:T(8,128)(2,1)} all-to-all(bf16[32,16,512]{2,1,0:T(8,128)(2,1)S(1)} %bitcast.9), channel_id=1, replica_groups=mesh['blk'=8,'grid'=4] {'blk','grid'}, dimensions={0} | all-to-all | bytes 1048576 | tf_op jit(solution)/shard_map/all_to_all | solution.py:330
  70.6 2.4 %shard_map.33 = f32[32,8,128]{2,1,0:T(8,128)} custom-call(bf16[32,16,512]{2,1,0:T(8,128)(2,1)} %all_to_all.10.x_ref), custom_call_target="tpu_custom_call" | custom-call | tf_op jit(solution)/shard_map/pallas_call | solution.py:335
  73.0 11.5 %all_to_all.11.parts_ref = f32[32,8,128]{2,1,0:T(8,128)} all-to-all(f32[32,8,128]{2,1,0:T(8,128)} %shard_map.33), channel_id=1, replica_groups=mesh['blk'=8,'grid'=4] {'blk','grid'}, dimensions={0} | all-to-all | bytes 262144 | tf_op jit(solution)/shard_map/all_to_all | solution.py:341
  84.5 3.5 %shard_map.34 = (bf16[32,16,512]{2,1,0:T(8,128)(2,1)}, f32[32,32]{1,0:T(8,128)}) custom-call(f32[32,8,128]{2,1,0:T(8,128)} %all_to_all.11.parts_ref, bf16[32,16,512]{2,1,0:T(8,128)(2,1)} %all_to_all.10.x_ref), custom_call_target="tpu_custom_call" | custom-call | tf_op jit(solution)/shard_map/pallas_call | solution.py:342
  (11 shorter events, 0.1 us)
Async XLA Ops:
  0.6 19.5 %collective-permute-start.1 = (bf16[4,16,4096]{2,1,0:T(8,128)(2,1)}, bf16[4,16,4096]{2,1,0:T(8,128)(2,1)S(1)}, u32[]{:S(2)}, u32[]{:S(2)}) collective-permute-start(bf16[4,16,4096]{2,1,0:T(8,128)(2,1)} %param.1), channel_id=1, source_target_pairs={{0,2},{1,3},{2,0},{3,1},{4,6},{5,7},{6,4},{7,5},{8,10},{9,11},{10,... | collective-permute-start | bytes 1572872 | tf_op jit(solution)/shard_map/ppermute | solution.py:266
  4.7 11.0 %collective-permute-start.8 = (bf16[2,16,4096]{2,1,0:T(8,128)(2,1)S(1)}, bf16[2,16,4096]{2,1,0:T(8,128)(2,1)S(1)}, u32[]{:S(2)}, u32[]{:S(2)}) collective-permute-start(bf16[2,16,4096]{2,1,0:T(8,128)(2,1)S(1)} %get-tuple-element.16), channel_id=1, source_target_pairs={{0,8},{4,12},{8,16},{12,20},{16,24},{20,28},{24,0},{28,4},{1,9},{5... | collective-permute-start | bytes 786440 | tf_op jit(solution)/shard_map/ppermute | solution.py:294
  6.4 13.7 %collective-permute-start.3 = (bf16[2,16,4096]{2,1,0:T(8,128)(2,1)S(1)}, bf16[2,16,4096]{2,1,0:T(8,128)(2,1)S(1)}, u32[]{:S(2)}, u32[]{:S(2)}) collective-permute-start(bf16[2,16,4096]{2,1,0:T(8,128)(2,1)S(1)} %get-tuple-element.12), channel_id=1, source_target_pairs={{0,8},{4,12},{8,16},{12,20},{16,24},{20,28},{24,0},{28,4},{1,9},{5... | collective-permute-start | bytes 786440 | tf_op jit(solution)/shard_map/ppermute | solution.py:294
  8.9 11.3 %collective-permute-start = (bf16[16,4096]{1,0:T(8,128)(2,1)S(1)}, bf16[16,4096]{1,0:T(8,128)(2,1)S(1)}, u32[]{:S(2)}, u32[]{:S(2)}) collective-permute-start(bf16[16,4096]{1,0:T(8,128)(2,1)S(1)} %get-tuple-element.26), channel_id=1, source_target_pairs={{0,1},{1,0},{2,3},{3,2},{4,5},{5,4},{6,7},{7,6},{8,9},{9,8},{10,11... | collective-permute-start | bytes 393224 | tf_op jit(solution)/shard_map/ppermute | solution.py:266
  9.5 27.2 %copy-start = (s32[4]{0:T(128)S(1)}, s32[4]{0:T(128)}, u32[]{:S(2)}) copy-start(s32[4]{0:T(128)} %iota_xor_fusion.order_ref.refs_12_) | copy-start | bytes 52
  12.4 24.3 %copy-start.1 = (f32[4096,128]{1,0:T(8,128)S(1)}, f32[4096,128]{1,0:T(8,128)}, u32[]{:S(2)}) copy-start(f32[4096,128]{1,0:T(8,128)} %get-tuple-element.18.refs_14_) | copy-start | bytes 6291460
  12.4 24.3 %copy-start.2 = (bf16[3,256,256]{2,1,0:T(8,128)(2,1)S(1)}, bf16[3,256,256]{2,1,0:T(8,128)(2,1)}, u32[]{:S(2)}) copy-start(bf16[3,256,256]{2,1,0:T(8,128)(2,1)} %get-tuple-element.17.refs_13_) | copy-start | bytes 1179652
  15.8 6.4 %collective-permute-start.14 = (bf16[2,16,4096]{2,1,0:T(8,128)(2,1)S(1)}, bf16[2,16,4096]{2,1,0:T(8,128)(2,1)S(1)}, u32[]{:S(2)}, u32[]{:S(2)}) collective-permute-start(bf16[2,16,4096]{2,1,0:T(8,128)(2,1)S(1)} %collective-permute-done.8.refs_8_), channel_id=1, source_target_pairs={{0,2},{1,3},{2,0},{3,1},{4,6},{5,7},{6,4},{7,5},{8,10},{9,11},{10,... | collective-permute-start | bytes 786440 | tf_op jit(solution)/shard_map/ppermute | solution.py:266
  16.1 7.6 %collective-permute-start.13 = (bf16[2,16,4096]{2,1,0:T(8,128)(2,1)S(1)}, bf16[2,16,4096]{2,1,0:T(8,128)(2,1)S(1)}, u32[]{:S(2)}, u32[]{:S(2)}) collective-permute-start(bf16[2,16,4096]{2,1,0:T(8,128)(2,1)S(1)} %collective-permute-done.8.refs_8_), channel_id=1, source_target_pairs={{0,1},{1,0},{2,3},{3,2},{4,5},{5,4},{6,7},{7,6},{8,9},{9,8},{10,11... | collective-permute-start | bytes 786440 | tf_op jit(solution)/shard_map/ppermute | solution.py:266
  20.0 3.6 %collective-permute-start.11 = (bf16[2,16,4096]{2,1,0:T(8,128)(2,1)S(1)}, bf16[2,16,4096]{2,1,0:T(8,128)(2,1)S(1)}, u32[]{:S(2)}, u32[]{:S(2)}) collective-permute-start(bf16[2,16,4096]{2,1,0:T(8,128)(2,1)S(1)} %collective-permute-done.3.refs_4_), channel_id=1, source_target_pairs={{0,1},{1,0},{2,3},{3,2},{4,5},{5,4},{6,7},{7,6},{8,9},{9,8},{10,11... | collective-permute-start | bytes 786440 | tf_op jit(solution)/shard_map/ppermute | solution.py:266
  20.1 10.6 %collective-permute-start.6 = (bf16[2,16,4096]{2,1,0:T(8,128)(2,1)S(1)}, bf16[2,16,4096]{2,1,0:T(8,128)(2,1)S(1)}, u32[]{:S(2)}, u32[]{:S(2)}) collective-permute-start(bf16[2,16,4096]{2,1,0:T(8,128)(2,1)S(1)} %slice.12), channel_id=1, source_target_pairs={{0,8},{4,12},{8,16},{12,20},{16,24},{20,28},{24,0},{28,4},{1,9},{5... | collective-permute-start | bytes 786440 | tf_op jit(solution)/shard_map/ppermute | solution.py:294
  20.2 10.5 %collective-permute-start.9 = (bf16[2,16,4096]{2,1,0:T(8,128)(2,1)S(1)}, bf16[2,16,4096]{2,1,0:T(8,128)(2,1)S(1)}, u32[]{:S(2)}, u32[]{:S(2)}) collective-permute-start(bf16[2,16,4096]{2,1,0:T(8,128)(2,1)S(1)} %broadcast_select_fusion), channel_id=1, source_target_pairs={{0,4},{4,0},{8,12},{12,8},{16,20},{20,16},{24,28},{28,24},{1,5},{5... | collective-permute-start | bytes 786440 | tf_op jit(solution)/shard_map/ppermute | solution.py:266
  22.1 12.5 %collective-permute-start.4 = (bf16[2,16,4096]{2,1,0:T(8,128)(2,1)S(1)}, bf16[2,16,4096]{2,1,0:T(8,128)(2,1)S(1)}, u32[]{:S(2)}, u32[]{:S(2)}) collective-permute-start(bf16[2,16,4096]{2,1,0:T(8,128)(2,1)S(1)} %broadcast_select_fusion.2), channel_id=1, source_target_pairs={{0,4},{4,0},{8,12},{12,8},{16,20},{20,16},{24,28},{28,24},{1,5},{5... | collective-permute-start | bytes 786440 | tf_op jit(solution)/shard_map/ppermute | solution.py:266
  23.7 11.0 %collective-permute-start.2 = (bf16[16,4096]{1,0:T(8,128)(2,1)S(1)}, bf16[16,4096]{1,0:T(8,128)(2,1)S(1)}, u32[]{:S(2)}, u32[]{:S(2)}) collective-permute-start(bf16[16,4096]{1,0:T(8,128)(2,1)S(1)} %get-tuple-element.24), channel_id=1, source_target_pairs={{0,1},{1,0},{2,3},{3,2},{4,5},{5,4},{6,7},{7,6},{8,9},{9,8},{10,11... | collective-permute-start | bytes 393224 | tf_op jit(solution)/shard_map/ppermute | solution.py:266
  23.7 11.5 %collective-permute-start.15 = (bf16[2,16,4096]{2,1,0:T(8,128)(2,1)S(1)}, bf16[2,16,4096]{2,1,0:T(8,128)(2,1)S(1)}, u32[]{:S(2)}, u32[]{:S(2)}) collective-permute-start(bf16[2,16,4096]{2,1,0:T(8,128)(2,1)S(1)} %collective-permute-done.14.refs_10_), channel_id=1, source_target_pairs={{0,1},{1,0},{2,3},{3,2},{4,5},{5,4},{6,7},{7,6},{8,9},{9,8},{10,11... | collective-permute-start | bytes 786440 | tf_op jit(solution)/shard_map/ppermute | solution.py:266
  30.7 6.0 %collective-permute-start.12 = (bf16[2,16,4096]{2,1,0:T(8,128)(2,1)S(1)}, bf16[2,16,4096]{2,1,0:T(8,128)(2,1)S(1)}, u32[]{:S(2)}, u32[]{:S(2)}) collective-permute-start(bf16[2,16,4096]{2,1,0:T(8,128)(2,1)S(1)} %collective-permute-done.6.refs_6_), channel_id=1, source_target_pairs={{0,1},{1,0},{2,3},{3,2},{4,5},{5,4},{6,7},{7,6},{8,9},{9,8},{10,11... | collective-permute-start | bytes 786440 | tf_op jit(solution)/shard_map/ppermute | solution.py:266
  30.8 10.8 %collective-permute-start.10 = (bf16[2,16,4096]{2,1,0:T(8,128)(2,1)S(1)}, bf16[2,16,4096]{2,1,0:T(8,128)(2,1)S(1)}, u32[]{:S(2)}, u32[]{:S(2)}) collective-permute-start(bf16[2,16,4096]{2,1,0:T(8,128)(2,1)S(1)} %collective-permute-done.9.refs_8_), channel_id=1, source_target_pairs={{0,2},{1,3},{2,0},{3,1},{4,6},{5,7},{6,4},{7,5},{8,10},{9,11},{10,... | collective-permute-start | bytes 786440 | tf_op jit(solution)/shard_map/ppermute | solution.py:266
  34.7 9.3 %collective-permute-start.17 = (bf16[2,16,4096]{2,1,0:T(8,128)(2,1)S(1)}, bf16[2,16,4096]{2,1,0:T(8,128)(2,1)S(1)}, u32[]{:S(2)}, u32[]{:S(2)}) collective-permute-start(bf16[2,16,4096]{2,1,0:T(8,128)(2,1)S(1)} %collective-permute-done.9.refs_8_), channel_id=1, source_target_pairs={{0,1},{1,0},{2,3},{3,2},{4,5},{5,4},{6,7},{7,6},{8,9},{9,8},{10,11... | collective-permute-start | bytes 786440 | tf_op jit(solution)/shard_map/ppermute | solution.py:266
  34.7 9.3 %collective-permute-start.5 = (bf16[2,16,4096]{2,1,0:T(8,128)(2,1)S(1)}, bf16[2,16,4096]{2,1,0:T(8,128)(2,1)S(1)}, u32[]{:S(2)}, u32[]{:S(2)}) collective-permute-start(bf16[2,16,4096]{2,1,0:T(8,128)(2,1)S(1)} %collective-permute-done.4.refs_4_), channel_id=1, source_target_pairs={{0,1},{1,0},{2,3},{3,2},{4,5},{5,4},{6,7},{7,6},{8,9},{9,8},{10,11... | collective-permute-start | bytes 786440 | tf_op jit(solution)/shard_map/ppermute | solution.py:266
  35.2 8.3 %collective-permute-start.7 = (bf16[2,16,4096]{2,1,0:T(8,128)(2,1)S(1)}, bf16[2,16,4096]{2,1,0:T(8,128)(2,1)S(1)}, u32[]{:S(2)}, u32[]{:S(2)}) collective-permute-start(bf16[2,16,4096]{2,1,0:T(8,128)(2,1)S(1)} %broadcast_select_fusion.1), channel_id=1, source_target_pairs={{0,4},{4,0},{8,12},{12,8},{16,20},{20,16},{24,28},{28,24},{1,5},{5... | collective-permute-start | bytes 786440 | tf_op jit(solution)/shard_map/ppermute | solution.py:266
  43.5 1.5 %collective-permute-start.16 = (bf16[2,16,4096]{2,1,0:T(8,128)(2,1)S(1)}, bf16[2,16,4096]{2,1,0:T(8,128)(2,1)S(1)}, u32[]{:S(2)}, u32[]{:S(2)}) collective-permute-start(bf16[2,16,4096]{2,1,0:T(8,128)(2,1)S(1)} %collective-permute-done.7.refs_6_), channel_id=1, source_target_pairs={{0,1},{1,0},{2,3},{3,2},{4,5},{5,4},{6,7},{7,6},{8,9},{9,8},{10,11... | collective-permute-start | bytes 786440 | tf_op jit(solution)/shard_map/ppermute | solution.py:266
  43.5 1.9 %collective-permute-start.18 = (bf16[2,16,4096]{2,1,0:T(8,128)(2,1)S(1)}, bf16[2,16,4096]{2,1,0:T(8,128)(2,1)S(1)}, u32[]{:S(2)}, u32[]{:S(2)}) collective-permute-start(bf16[2,16,4096]{2,1,0:T(8,128)(2,1)S(1)} %collective-permute-done.10.refs_10_), channel_id=1, source_target_pairs={{0,1},{1,0},{2,3},{3,2},{4,5},{5,4},{6,7},{7,6},{8,9},{9,8},{10,11... | collective-permute-start | bytes 786440 | tf_op jit(solution)/shard_map/ppermute | solution.py:266

commit v4 on v3

--- a/solution.py
+++ b/solution.py
@@ -39,15 +39,16 @@
     return 2.0 - 2.0 * jnp.cos(jnp.pi * (index + 1.0) / (length + 1))
 
 
-def table_kernel(slab_rows, order_ref, diag_ref, weight_ref):
+def table_kernel(slab_rows, diag_ref, weight_ref):
     size = diag_ref.shape[1]
     copies = size // NX
+    grid_index = lax.axis_index("grid")
 
     def cells_of(position):
         slab = position // slab_rows
         start = jnp.zeros_like(position)
         for r in range(NX // slab_rows):
-            start = jnp.where(slab == r, order_ref[r] * slab_rows, start)
+            start = jnp.where(slab == r, (grid_index ^ r) * slab_rows, start)
         return start + position % slab_rows
 
     shape = (NX, LANES)
@@ -72,7 +73,7 @@
         weight_ref[k * NY:(k + 1) * NY, :] = 1.0 / (lam[k:k + 1, :] + plane)
 
 
-def make_tables(order, slab_rows):
+def make_tables(slab_rows):
     size = QUAD * NX
     return pl.pallas_call(
         functools.partial(table_kernel, slab_rows),
@@ -80,48 +81,41 @@
             jax.ShapeDtypeStruct((3, size, size), BF),
             jax.ShapeDtypeStruct((NX * NY, LANES), F32),
         ),
-        in_specs=[SMEM],
         out_specs=(VMEM, VMEM),
         cost_estimate=pl.CostEstimate(flops=1 << 28, bytes_accessed=3 << 20, transcendentals=0),
-    )(order)
-
-
-def block_kernel(slabs, parts, final, rest):
-    own = rest[:slabs]
-    src = [rest[slabs + p * slabs:slabs + (p + 1) * slabs] for p in range(parts)]
-    rest = rest[slabs * (parts + 1):]
-    pos_ref, tab_ref, w_ref = rest[:3]
-    rest = rest[3:]
+    )()
+
+
+def block_kernel(slabs, final, rest):
+    grid_index = lax.axis_index("grid")
+    core, chip = grid_index % 2, grid_index // 2
+    local = rest[:slabs]
+    passed = rest[slabs:2 * slabs]
+    src = rest[2 * slabs:3 * slabs]
+    tab_ref, w_ref = rest[3 * slabs:3 * slabs + 2]
+    rest = rest[3 * slabs + 2:]
     if final:
-        acc_ref, out_ref, grouped_ref, work_ref = rest
+        acc_ref, keep_ref, send_ref, grouped_ref, work_ref = rest
     else:
         out_ref, grouped_ref, work_ref = rest
-    each = src[0][0].shape[0]
-    count = each * parts
-    rows = src[0][0].shape[1]
-    halves = count * NZ // LANES
+    owns = local[0].shape[0]
+    count = src[0].shape[0]
+    halves = owns * count * NZ // LANES
     width = QUAD * NZ
     pitch = work_ref.shape[1] // NY
 
-    def tile(refs, lead, off, size):
-        parts = [r[lead + (slice(None), pl.ds(off, size))] for r in refs]
-        return jnp.concatenate(parts, 0)
-
-    def load_rows(first):
-        parts = []
-        for q in range(QUAD):
-            at = (first + q) * pitch
-            parts.append(
-                jnp.concatenate([work_ref[h, pl.ds(at, NX), :] for h in range(halves)], 1)
-            )
-        return jnp.concatenate(parts, 0)
+    def tile(refs, j, off, size):
+        return jnp.concatenate([r[j, :, pl.ds(off, size)] for r in refs], 0)
+
+    def own_tile(o, off, size):
+        return jnp.where(core == chip, tile(local, o, off, size), tile(passed, o, off, size))
 
     def forward(t):
         off = t * width
         at = t * QUAD * NX
-        mine = tile(own, (), off, width)
-        others = [tile(src[j // each], (j % each,), off, width) for j in range(count)]
-        pairs = [mine * other for other in others]
+        mine = [own_tile(o, off, width) for o in range(owns)]
+        others = [tile(src, j, off, width) for j in range(count)]
+        pairs = [m * other for m in mine for other in others]
         cut = [slice(q * NZ, (q + 1) * NZ) for q in range(QUAD)]
         density = jnp.concatenate(
             [jnp.concatenate([p[:, c] for p in pairs], 1) for c in cut], 0)
@@ -149,60 +143,86 @@
                     back[q * NY:(q + 1) * NY, h * LANES:(h + 1) * LANES])
 
     lane = lax.broadcasted_iota(jnp.int32, (NX, LANES), 1)
-    per_tile = LANES // NZ
 
     def backward(t):
         at = t * QUAD * NX
-        third = product(tab_ref[2], load_rows(t * QUAD).astype(BF)).astype(BF)
+        modes = jnp.concatenate([
+            jnp.concatenate(
+                [work_ref[h, pl.ds((t * QUAD + q) * pitch, NX), :] for h in range(halves)], 1)
+            for q in range(QUAD)], 0).astype(BF)
+        third = product(tab_ref[2], modes).astype(BF)
         potential = product(third, tab_ref[0])
-        terms = potential * grouped_ref[pl.ds(at, QUAD * NX), :].astype(F32)
-        total = terms[:, :LANES]
-        for h in range(1, halves):
-            total = total + terms[:, h * LANES:(h + 1) * LANES]
-        total = total + pltpu.roll(total, NZ, 1)
-        for q in range(0, QUAD, per_tile):
-            exchange = jnp.where(
-                lane < NZ, total[q * NX:(q + 1) * NX], total[(q + 1) * NX:(q + 2) * NX])
+        factor = grouped_ref[pl.ds(at, QUAD * NX), :].astype(F32)
+        totals = []
+        for o in range(owns):
+            terms = potential[:, o * LANES:(o + 1) * LANES] * factor
+            totals.append(terms + pltpu.roll(terms, NZ, 1))
+        for q in range(0, QUAD, LANES // NZ):
             off = (t * QUAD + q) * NZ
+            exchange = [
+                jnp.where(lane < NZ, x[q * NX:(q + 1) * NX], x[(q + 1) * NX:(q + 2) * NX])
+                for x in totals
+            ]
             if not final:
-                out_ref[:, pl.ds(off, LANES)] = exchange
+                for o in range(owns):
+                    out_ref[o, :, pl.ds(off, LANES)] = exchange[o]
                 continue
-            exchange = exchange + acc_ref[:, pl.ds(off, LANES)]
-            mine = tile(own, (), off, LANES).astype(F32)
-            updated = (mine - exchange_fraction * exchange).astype(BF)
-            for r in range(slabs):
-                part = updated[r * rows:(r + 1) * rows]
-                if len(out_ref.shape) == 4:
-                    share = out_ref.shape[3] // LANES
-                    index = (t * QUAD + q) * NZ // LANES
-                    to = (index % share) * LANES
-                    out_ref[index // share, pos_ref[r], :, pl.ds(to, LANES)] = part
-                else:
-                    out_ref[pos_ref[r], :, pl.ds(off, LANES)] = part
+            exchange = [
+                exchange_fraction * (x + acc_ref[o, :, pl.ds(off, LANES)])
+                for o, x in enumerate(exchange)
+            ]
+            own = [own_tile(o, off, LANES) for o in range(owns)]
+            first = core == 0
+            own = jnp.where(first, own[0], own[1]).astype(F32)
+            keep_ref[:, pl.ds(off, LANES)] = own - jnp.where(first, exchange[0], exchange[1])
+            send_ref[:, pl.ds(off, LANES)] = (
+                jnp.where(first, exchange[1], exchange[0]).astype(send_ref.dtype))
 
     for step, trips in ((forward, NY // QUAD), (solve, NX // QUAD), (backward, NY // QUAD)):
         for t in range(trips):
             step(t)
 
 
-def add_block(own, src, tables, acc, out_shape):
-    slabs = len(own)
-    count = sum(part[0].shape[0] for part in src)
+def add_block(local, passed, src, tables, acc):
+    slabs = len(local)
+    owns, _, cells = local[0].shape
+    count = src[0].shape[0]
+    assert count * NZ == LANES and owns == 2
     final = acc is not None
     lead = () if acc is None else (acc,)
-    flops = 12 * count * NX * NY * NZ * NZ * 4
+    flops = 12 * owns * count * NX * NY * NZ * NZ * 4
+    if final:
+        out_shape = (
+            jax.ShapeDtypeStruct((NX, cells), F32), jax.ShapeDtypeStruct((NX, cells), BF))
+    else:
+        out_shape = jax.ShapeDtypeStruct((owns, NX, cells), F32)
     return pl.pallas_call(
-        lambda *refs: block_kernel(slabs, len(src), final, refs),
+        lambda *refs: block_kernel(slabs, final, refs),
         out_shape=out_shape,
-        in_specs=[VMEM] * ((1 + len(src)) * slabs) + [SMEM] + [VMEM] * (2 + len(lead)),
-        out_specs=VMEM,
+        in_specs=[VMEM] * (3 * slabs + 2 + len(lead)),
+        out_specs=(VMEM, VMEM) if final else VMEM,
         scratch_shapes=[
             pltpu.VMEM((NY * NX, count * NZ), BF),
-            pltpu.VMEM((count * NZ // LANES, NY * (NX + ROW_PAD), LANES), F32),
+            pltpu.VMEM((owns * count * NZ // LANES, NY * (NX + ROW_PAD), LANES), F32),
         ],
-        compiler_params=pltpu.CompilerParams(vmem_limit_bytes=40 * 1024 * 1024),
+        compiler_params=pltpu.CompilerParams(vmem_limit_bytes=24 * 1024 * 1024),
         cost_estimate=pl.CostEstimate(flops=flops, bytes_accessed=8 << 20, transcendentals=0),
-    )(*own, *[slab for part in src for slab in part], *tables, *lead)
+    )(*local, *passed, *src, *tables, *lead)
+
+
+def combine_kernel(slabs, keep_ref, part_ref, out_ref):
+    grid_index = lax.axis_index("grid")
+    rows = keep_ref.shape[0] // slabs
+    for r in range(slabs):
+        other = (r ^ 1) * rows
+        updated = keep_ref[r * rows:(r + 1) * rows] - part_ref[other:other + rows].astype(F32)
+        updated = updated.astype(BF)
+        if len(out_ref.shape) == 3:
+            out_ref[grid_index ^ r] = updated
+            continue
+        share = out_ref.shape[3]
+        for b in range(out_ref.shape[0]):
+            out_ref[b, grid_index ^ r] = updated[:, b * share:(b + 1) * share]
 
 
 def gram_kernel(x_ref, out_ref):
@@ -262,33 +282,21 @@
     out_ref[...] = product(spread, flat).astype(BF).reshape(orbs, rows, lanes)
 
 
-def exchanged(x, axis, by):
-    return lax.ppermute(x, axis, [(i, i ^ by) for i in range(lax.axis_size(axis))])
-
-
-def completed(slab, other):
-    top = lax.axis_size("grid") // 2
-    slabs = {0: slab, top: other}
-    bit = top // 2
-    while bit:
-        for r in list(slabs):
-            slabs[r | bit] = exchanged(slabs[r], "grid", bit)
-        bit //= 2
-    return [slabs[r] for r in range(2 * top)]
+def exchanged(x, axis, by, only=None):
+    return lax.ppermute(x, axis, [
+        (i, i ^ by) for i in range(lax.axis_size(axis)) if only is None or only(i)])
 
 
 def body(orbitals):
     orb_count, slab_rows, plane_cells = orbitals.shape
     slabs = lax.axis_size("grid")
     blocks = lax.axis_size("blk")
-    assert orb_count == slabs and slab_rows * slabs == NX and blocks % 2 == 0 and STEPS == 2
-    grid_index = lax.axis_index("grid")
-    order = (jnp.arange(slabs) ^ grid_index).astype(jnp.int32)
-
-    diagonals, weights = make_tables(order, slab_rows)
+    assert orb_count == slabs == 4 and slab_rows * slabs == NX and blocks % 2 == 0 and STEPS == 2
     top = slabs // 2
     half = orb_count // 2
+    core = lax.axis_index("grid") % 2
     even = lax.axis_index("blk") % 2 == 0
+    diagonals, weights = make_tables(slab_rows)
 
     def shifted(x):
         return lax.ppermute(x, "blk", [(i, (i + 2) % blocks) for i in range(blocks)])
@@ -296,34 +304,36 @@
     def relayed(mine, received):
         return exchanged(jnp.where(even, mine, received), "blk", 1)
 
-    mine = lax.optimization_barrier([orbitals[:half], orbitals[half:]])
-    far = [shifted(mine[i]) for i in range(2)]
-    across = exchanged(orbitals, "grid", top)
-    across_half = lax.optimization_barrier(across[:half])
-    near = [relayed(mine[i], far[i]) for i in range(2)]
-    far_other = [shifted(across_half), exchanged(far[1], "grid", top)]
-    across_half, diagonals, weights = lax.optimization_barrier(
-        (across_half, diagonals, weights))
-    tables = (order, diagonals, weights)
-    near_other = [relayed(across_half, far_other[0]), exchanged(near[1], "grid", top)]
-
-    own = {}
-    for r in range(top):
-        for held, block in ((0, orbitals), (top, across)):
-            piece = lax.dynamic_index_in_dim(block, grid_index ^ r, 0, keepdims=False)
-            own[r | held] = exchanged(piece, "grid", r) if r else piece
-    own = [own[r] for r in range(slabs)]
-
-    far = [completed(far[i], far_other[i]) for i in range(2)]
-    acc = add_block(own, far, tables, None, jax.ShapeDtypeStruct((NX, plane_cells), F32))
-    near_other, acc = lax.optimization_barrier((near_other, acc))
-    near = [completed(near[i], near_other[i]) for i in range(2)]
+    def passed_on(x):
+        return exchanged(x, "grid", 1, lambda i: i // 2 == i % 2)
+
+    keep = lax.dynamic_slice_in_dim(orbitals, core * half, half, 0)
+    give = lax.dynamic_slice_in_dim(orbitals, (1 - core) * half, half, 0)
+    keep, give = lax.optimization_barrier((keep, give))
+    held = [keep, exchanged(give, "grid", 1)]
+    far = [shifted(held[i]) for i in range(2)]
+    across = [exchanged(held[i], "grid", top) for i in range(2)]
+    near = [relayed(held[i], far[i]) for i in range(2)]
+    far_other = [shifted(across[0]), exchanged(far[1], "grid", top)]
+    relay, diagonals, weights = lax.optimization_barrier((across[0], diagonals, weights))
+    tables = (diagonals, weights)
+    near_other = [relayed(relay, far_other[0]), exchanged(near[1], "grid", top)]
+    local = held + across
+    passed = [give, passed_on(held[0]), passed_on(across[1]), passed_on(across[0])]
+    acc = add_block(local, passed, far + far_other, tables, None)
+    mine, other = add_block(local, passed, near + near_other, tables, acc)
+    other = exchanged(other, "grid", 1)
     chunk = plane_cells // blocks
     if chunk % LANES == 0:
         shape = (blocks, slabs, slab_rows, chunk)
     else:
         shape = (slabs, slab_rows, plane_cells)
-    updated = add_block(own, near, tables, acc, jax.ShapeDtypeStruct(shape, BF))
+    updated = pl.pallas_call(
+        functools.partial(combine_kernel, slabs),
+        out_shape=jax.ShapeDtypeStruct(shape, BF),
+        in_specs=[VMEM, VMEM],
+        out_specs=VMEM,
+    )(mine, other)
     if chunk % LANES:
         updated = updated.reshape(slabs, slab_rows, blocks, chunk).transpose(2, 0, 1, 3)
     updated = updated.reshape(blocks * slabs, slab_rows, chunk)

time: 88.3 us -> 90.2 us (1.022)
  waiting for transfers between devices: 20.7 us -> 12.9 us
  starting transfers between devices: 13.4 us -> 20.5 us
  local copies, waits for them, and re-layouts: 2.1 us -> 3.85 us
    ppermute x3, waiting for transfers between devices: 13.8 us -> 5.94 us  [shifted(): lax.ppermute(x, 'blk', [(i, (i + 2) % blocks) for i in range(blocks)])]
    ppermute x16 -> x12, starting transfers between devices: 10.2 us -> 15.5 us  [exchanged(): lax.ppermute(x, axis, [(i, i ^ by) for i in range(lax.axis_size(axis)) if...]
    unnamed x6 -> x10, local copies, waits for them, and re-layouts: 0.01 us -> 2.78 us
    ppermute x3, starting transfers between devices: 3.26 us -> 4.98 us  [shifted(): lax.ppermute(x, 'blk', [(i, (i + 2) % blocks) for i in range(blocks)])]
    pallas_call x2 -> x3, Pallas kernels: 9.68 us -> 11.2 us  [the longest x2 8.97 us: add_block(): pl.pallas_call(lambda *refs: block_kernel(slabs, final, refs), out_shape=...]
    slice x2 -> x0, local copies, waits for them, and re-layouts: 1.08 us -> none  [the longest x1 1.06 us: body(): mine = lax.optimization_barrier([orbitals[:half], orbitals[half:]])]
    dynamic_slice x0 -> x1, local copies, waits for them, and re-layouts: none -> 1.07 us  [body(): give = lax.dynamic_slice_in_dim(orbitals, (1 - core) * half, half, 0)]
    squeeze x2 -> x0, local copies, waits for them, and re-layouts: 1.01 us -> none  [body(): piece = lax.dynamic_index_in_dim(block, grid_index ^ r, 0, keepdims=False)]
  transfers between devices with their start and end apart: 19 -> 15, of which waited for: 8 -> 6; matrix products, arithmetic and copies ran while one was open for 3% -> 0% of each run, Pallas kernels for 9% -> 7%
where the time goes in v4:
time: 90.2 us; the launch traced here: 89.7 us
  blocking collectives  32.4 us (36%)
  starting transfers between devices  20.5 us (23%)
  Pallas kernels  19.2 us (21%)
  waiting for transfers between devices  12.9 us (14%)
  local copies, waits for them, and re-layouts  3.85 us (4%)
    all_to_all x1, blocking collectives, body(): cellwise = lax.all_to_all(updated, ('blk', 'grid'), 0, 0, tiled=True)  20.9 us
    ppermute x12, starting transfers between devices, exchanged(): lax.ppermute(x, axis, [(i, i ^ by) for i in range(lax.axis_size(axis)) if...  15.5 us
    all_to_all x1, blocking collectives, body(): parts = lax.all_to_all(local, ('blk', 'grid'), 0, 0, tiled=True)  11.5 us
    pallas_call x2, Pallas kernels, add_block(): pl.pallas_call(lambda *refs: block_kernel(slabs, final, refs), out_shape=...  8.97 us
    ppermute x12, waiting for transfers between devices, exchanged(): lax.ppermute(x, axis, [(i, i ^ by) for i in range(lax.axis_size(axis)) if...  6.92 us
    ppermute x3, waiting for transfers between devices, shifted(): lax.ppermute(x, 'blk', [(i, (i + 2) % blocks) for i in range(blocks)])  5.94 us
    ppermute x3, starting transfers between devices, shifted(): lax.ppermute(x, 'blk', [(i, (i + 2) % blocks) for i in range(blocks)])  4.98 us
    pallas_call x1, Pallas kernels, body(): pl.pallas_call(functools.partial(rotate_kernel, 1.0 / cell_count), out_sh...  3.49 us
  transfers between devices with their start and end apart: 15, of which 6 were waited for; matrix products, arithmetic and copies ran while one was open for 0% of the time, Pallas kernels for 7%

profile of v4, /device:TPU:0, one launch (start us, length us, event | category | flops | bytes accessed | tf_op | source)
XLA Modules:
  0.0 89.7 jit_solution(2642915879184348002)
XLA Ops:
  0.7 1.1 %constant_dynamic-slice_fusion = (bf16[2,16,4096]{2,1,0:T(8,128)(2,1)S(1)}, bf16[2,16,4096]{2,1,0:T(8,128)(2,1)S(1)}) fusion(bf16[4,16,4096]{2,1,0:T(8,128)(2,1)} %param.1, s32[]{:T(128)S(6)} %select_n.35, s32[]{:T(128)S(6)} %select_n.34), kind=kLoop, calls=%fused_computation.3 | loop fusion | bytes 1048584 | tf_op jit(solution)/shard_map/dynamic_slice | solution.py:311
  1.7 3.0 %collective-permute-start.1 = (bf16[2,16,4096]{2,1,0:T(8,128)(2,1)S(1)}, bf16[2,16,4096]{2,1,0:T(8,128)(2,1)S(1)}, u32[]{:S(2)}, u32[]{:S(2)}) collective-permute-start(bf16[2,16,4096]{2,1,0:T(8,128)(2,1)S(1)} %get-tuple-element.11.refs_0_), channel_id=1, source_target_pairs={{0,2},{1,3},{2,0},{3,1},{4,6},{5,7},{6,4},{7,5},{8,10},{9,11},{10,... | collective-permute-start | bytes 786440 | tf_op jit(solution)/shard_map/ppermute | solution.py:286
  4.8 0.0 collective-permute-start
  4.8 1.6 %collective-permute-start.6 = (bf16[2,16,4096]{2,1,0:T(8,128)(2,1)S(1)}, bf16[2,16,4096]{2,1,0:T(8,128)(2,1)S(1)}, u32[]{:S(2)}, u32[]{:S(2)}) collective-permute-start(bf16[2,16,4096]{2,1,0:T(8,128)(2,1)S(1)} %get-tuple-element.11.refs_0_), channel_id=1, source_target_pairs={{0,8},{4,12},{8,16},{12,20},{16,24},{20,28},{24,0},{28,4},{1,9},{5... | collective-permute-start | bytes 786440 | tf_op jit(solution)/shard_map/ppermute | solution.py:302
  6.3 2.1 %collective-permute-start.3 = (bf16[2,16,4096]{2,1,0:T(8,128)(2,1)S(1)}, bf16[2,16,4096]{2,1,0:T(8,128)(2,1)S(1)}, u32[]{:S(2)}, u32[]{:S(2)}) collective-permute-start(bf16[2,16,4096]{2,1,0:T(8,128)(2,1)S(1)} %get-tuple-element.11.refs_0_), channel_id=1, source_target_pairs={{0,1},{3,2},{4,5},{7,6},{8,9},{11,10},{12,13},{15,14},{16,17},{19,... | collective-permute-start | bytes 786440 | tf_op jit(solution)/shard_map/ppermute | solution.py:286
  8.5 2.1 %shard_map.30 = (bf16[3,256,256]{2,1,0:T(8,128)(2,1)}, f32[4096,128]{1,0:T(8,128)}) custom-call(), custom_call_target="tpu_custom_call" | custom-call | flops 268435456 | bytes 3145728 | tf_op jit(solution)/shard_map/pallas_call | solution.py:78
  10.6 0.0 copy-start.1
  10.6 0.5 collective-permute-done.1.refs_2_
  11.1 0.0 collective-permute-done.refs_1_
  11.1 1.8 %collective-permute-start.8 = (bf16[2,16,4096]{2,1,0:T(8,128)(2,1)S(1)}, bf16[2,16,4096]{2,1,0:T(8,128)(2,1)S(1)}, u32[]{:S(2)}, u32[]{:S(2)}) collective-permute-start(bf16[2,16,4096]{2,1,0:T(8,128)(2,1)S(1)} %collective-permute-done.refs_1_), channel_id=1, source_target_pairs={{0,8},{4,12},{8,16},{12,20},{16,24},{20,28},{24,0},{28,4},{1,9},{5... | collective-permute-start | bytes 786440 | tf_op jit(solution)/shard_map/ppermute | solution.py:302
  12.9 1.5 %collective-permute-start.2 = (bf16[2,16,4096]{2,1,0:T(8,128)(2,1)S(1)}, bf16[2,16,4096]{2,1,0:T(8,128)(2,1)S(1)}, u32[]{:S(2)}, u32[]{:S(2)}) collective-permute-start(bf16[2,16,4096]{2,1,0:T(8,128)(2,1)S(1)} %collective-permute-done.refs_1_), channel_id=1, source_target_pairs={{0,2},{1,3},{2,0},{3,1},{4,6},{5,7},{6,4},{7,5},{8,10},{9,11},{10,... | collective-permute-start | bytes 786440 | tf_op jit(solution)/shard_map/ppermute | solution.py:286
  14.4 1.6 %collective-permute-start.10 = (bf16[2,16,4096]{2,1,0:T(8,128)(2,1)S(1)}, bf16[2,16,4096]{2,1,0:T(8,128)(2,1)S(1)}, u32[]{:S(2)}, u32[]{:S(2)}) collective-permute-start(bf16[2,16,4096]{2,1,0:T(8,128)(2,1)S(1)} %collective-permute-done.1.refs_2_), channel_id=1, source_target_pairs={{0,8},{4,12},{8,16},{12,20},{16,24},{20,28},{24,0},{28,4},{1,9},{5... | collective-permute-start | bytes 786440 | tf_op jit(solution)/shard_map/ppermute | solution.py:302
  16.0 0.0 collective-permute-done.6.refs_8_
  16.0 1.3 %collective-permute-start.5 = (bf16[2,16,4096]{2,1,0:T(8,128)(2,1)S(1)}, bf16[2,16,4096]{2,1,0:T(8,128)(2,1)S(1)}, u32[]{:S(2)}, u32[]{:S(2)}) collective-permute-start(bf16[2,16,4096]{2,1,0:T(8,128)(2,1)S(1)} %collective-permute-done.1.refs_2_), channel_id=1, source_target_pairs={{0,1},{3,2},{4,5},{7,6},{8,9},{11,10},{12,13},{15,14},{16,17},{19,... | collective-permute-start | bytes 786440 | tf_op jit(solution)/shard_map/ppermute | solution.py:286
  17.3 4.8 %collective-permute-done.8.refs_9_ = bf16[2,16,4096]{2,1,0:T(8,128)(2,1)S(1)} collective-permute-done((bf16[2,16,4096]{2,1,0:T(8,128)(2,1)S(1)}, bf16[2,16,4096]{2,1,0:T(8,128)(2,1)S(1)}, u32[]{:S(2)}, u32[]{:S(2)}) %collective-permute-start.8) | collective-permute-done | bytes 262176 | tf_op jit(solution)/shard_map/ppermute | solution.py:302
  22.1 1.8 %collective-permute-start.9 = (bf16[2,16,4096]{2,1,0:T(8,128)(2,1)S(1)}, bf16[2,16,4096]{2,1,0:T(8,128)(2,1)S(1)}, u32[]{:S(2)}, u32[]{:S(2)}) collective-permute-start(bf16[2,16,4096]{2,1,0:T(8,128)(2,1)S(1)} %broadcast_select_fusion.1), channel_id=1, source_target_pairs={{0,4},{4,0},{8,12},{12,8},{16,20},{20,16},{24,28},{28,24},{1,5},{5... | collective-permute-start | bytes 786440 | tf_op jit(solution)/shard_map/ppermute | solution.py:286
  23.9 0.0 collective-permute-done.2.refs_3_
  23.9 1.5 %collective-permute-start.13 = (bf16[2,16,4096]{2,1,0:T(8,128)(2,1)S(1)}, bf16[2,16,4096]{2,1,0:T(8,128)(2,1)S(1)}, u32[]{:S(2)}, u32[]{:S(2)}) collective-permute-start(bf16[2,16,4096]{2,1,0:T(8,128)(2,1)S(1)} %collective-permute-done.8.refs_9_), channel_id=1, source_target_pairs={{0,2},{1,3},{2,0},{3,1},{4,6},{5,7},{6,4},{7,5},{8,10},{9,11},{10,... | collective-permute-start | bytes 786440 | tf_op jit(solution)/shard_map/ppermute | solution.py:286
  25.4 1.2 %collective-permute-done.10.refs_10_ = bf16[2,16,4096]{2,1,0:T(8,128)(2,1)S(1)} collective-permute-done((bf16[2,16,4096]{2,1,0:T(8,128)(2,1)S(1)}, bf16[2,16,4096]{2,1,0:T(8,128)(2,1)S(1)}, u32[]{:S(2)}, u32[]{:S(2)}) %collective-permute-start.10) | collective-permute-done | bytes 262176 | tf_op jit(solution)/shard_map/ppermute | solution.py:302
  26.6 1.3 %collective-permute-start.4 = (bf16[2,16,4096]{2,1,0:T(8,128)(2,1)S(1)}, bf16[2,16,4096]{2,1,0:T(8,128)(2,1)S(1)}, u32[]{:S(2)}, u32[]{:S(2)}) collective-permute-start(bf16[2,16,4096]{2,1,0:T(8,128)(2,1)S(1)} %collective-permute-done.2.refs_3_), channel_id=1, source_target_pairs={{0,1},{3,2},{4,5},{7,6},{8,9},{11,10},{12,13},{15,14},{16,17},{19,... | collective-permute-start | bytes 786440 | tf_op jit(solution)/shard_map/ppermute | solution.py:286
  27.9 0.0 collective-permute-done.3.refs_5_
  27.9 1.6 %collective-permute-start.7 = (bf16[2,16,4096]{2,1,0:T(8,128)(2,1)S(1)}, bf16[2,16,4096]{2,1,0:T(8,128)(2,1)S(1)}, u32[]{:S(2)}, u32[]{:S(2)}) collective-permute-start(bf16[2,16,4096]{2,1,0:T(8,128)(2,1)S(1)} %broadcast_select_fusion.2), channel_id=1, source_target_pairs={{0,4},{4,0},{8,12},{12,8},{16,20},{20,16},{24,28},{28,24},{1,5},{5... | collective-permute-start | bytes 786440 | tf_op jit(solution)/shard_map/ppermute | solution.py:286
  29.5 0.0 collective-permute-done.5.refs_7_
  29.5 0.5 collective-permute-start.11
  30.0 0.0 collective-permute-done.9.refs_9_
  30.0 0.9 collective-permute-start.12
  30.9 0.0 collective-permute-done.13.refs_11_
  30.9 0.0 collective-permute-done.4.refs_6_
  30.9 0.0 copy-done.1
  30.9 0.0 copy-start.2
  30.9 1.0 %copy-done.2 = bf16[3,256,256]{2,1,0:T(8,128)(2,1)S(1)} copy-done((bf16[3,256,256]{2,1,0:T(8,128)(2,1)S(1)}, bf16[3,256,256]{2,1,0:T(8,128)(2,1)}, u32[]{:S(2)}) %copy-start.2) | copy-done | bytes 393240
  31.9 0.0 copy-start.3
  31.9 4.3 %shard_map.31.refs_14_ = f32[2,64,4096]{2,1,0:T(8,128)S(1)} custom-call(bf16[2,16,4096]{2,1,0:T(8,128)(2,1)S(1)} %get-tuple-element.11.refs_0_, bf16[2,16,4096]{2,1,0:T(8,128)(2,1)S(1)} %collective-permute-done.refs_1_, bf16[2,16,4096]{2,1,0:T(8,128)(2,1)S(1)} %collective-permute-done.1.refs_2_, bf16[2,16,4096]{2,1,0:T(8,128)(2,1)S(1)} %collective-permute-done.2.refs_3_, ...), custom_call_target="tpu_custom_call" | custom-call | flops 3221225472 | bytes 8388608 | tf_op jit(solution)/shard_map/pallas_call | solution.py:199
  36.3 0.9 %collective-permute-done.7.refs_8_ = bf16[2,16,4096]{2,1,0:T(8,128)(2,1)S(1)} collective-permute-done((bf16[2,16,4096]{2,1,0:T(8,128)(2,1)S(1)}, bf16[2,16,4096]{2,1,0:T(8,128)(2,1)S(1)}, u32[]{:S(2)}, u32[]{:S(2)}) %collective-permute-start.7) | collective-permute-done | bytes 262176 | tf_op jit(solution)/shard_map/ppermute | solution.py:286
  37.2 3.6 %collective-permute-done.11.refs_10_ = bf16[2,16,4096]{2,1,0:T(8,128)(2,1)S(1)} collective-permute-done((bf16[2,16,4096]{2,1,0:T(8,128)(2,1)S(1)}, bf16[2,16,4096]{2,1,0:T(8,128)(2,1)S(1)}, u32[]{:S(2)}, u32[]{:S(2)}) %collective-permute-start.11) | collective-permute-done | bytes 262176 | tf_op jit(solution)/shard_map/ppermute | solution.py:286
  40.8 0.0 collective-permute-done.12.refs_11_
  40.8 0.0 copy-done.3
  40.8 4.6 %shard_map.32 = (f32[64,4096]{1,0:T(8,128)S(1)}, bf16[64,4096]{1,0:T(8,128)(2,1)S(1)}) custom-call(bf16[2,16,4096]{2,1,0:T(8,128)(2,1)S(1)} %get-tuple-element.11.refs_0_, bf16[2,16,4096]{2,1,0:T(8,128)(2,1)S(1)} %collective-permute-done.refs_1_, bf16[2,16,4096]{2,1,0:T(8,128)(2,1)S(1)} %collective-permute-done.1.refs_2_, ...), custom_call_target="tpu_custom_call" | custom-call | flops 3221225472 | bytes 8388608 | tf_op jit(solution)/shard_map/pallas_call | solution.py:199
  45.5 0.0 copy-start
  45.5 1.0 %copy-done = f32[64,4096]{1,0:T(8,128)} copy-done((f32[64,4096]{1,0:T(8,128)}, f32[64,4096]{1,0:T(8,128)S(1)}, u32[]{:S(2)}) %copy-start) | copy-done | bytes 1048600
  46.5 0.0 collective-permute-start.14
  46.5 1.9 %collective-permute-done.14.part_ref = bf16[64,4096]{1,0:T(8,128)(2,1)S(1)} collective-permute-done((bf16[64,4096]{1,0:T(8,128)(2,1)S(1)}, bf16[64,4096]{1,0:T(8,128)(2,1)S(1)}, u32[]{:S(2)}, u32[]{:S(2)}) %collective-permute-start.14) | collective-permute-done | bytes 524320 | tf_op jit(solution)/shard_map/ppermute | solution.py:286
  48.4 0.8 copy-done.4
  49.2 2.2 %shard_map.33 = bf16[8,4,16,512]{3,2,1,0:T(8,128)(2,1)} custom-call(f32[64,4096]{1,0:T(8,128)} %copy-done, bf16[64,4096]{1,0:T(8,128)(2,1)} %copy-done.4), custom_call_target="tpu_custom_call" | custom-call | tf_op jit(solution)/shard_map/pallas_call | solution.py:331
  51.4 20.9 %all_to_all.10.x_ref = bf16[32,16,512]{2,1,0:T(8,128)(2,1)} all-to-all(bf16[32,16,512]{2,1,0:T(8,128)(2,1)} %bitcast.1), channel_id=1, replica_groups=mesh['blk'=8,'grid'=4] {'blk','grid'}, dimensions={0} | all-to-all | bytes 1048576 | tf_op jit(solution)/shard_map/all_to_all | solution.py:340
  72.3 2.4 %shard_map.34 = f32[32,8,128]{2,1,0:T(8,128)} custom-call(bf16[32,16,512]{2,1,0:T(8,128)(2,1)} %all_to_all.10.x_ref), custom_call_target="tpu_custom_call" | custom-call | tf_op jit(solution)/shard_map/pallas_call | solution.py:345
  74.7 11.5 %all_to_all.11.parts_ref = f32[32,8,128]{2,1,0:T(8,128)} all-to-all(f32[32,8,128]{2,1,0:T(8,128)} %shard_map.34), channel_id=1, replica_groups=mesh['blk'=8,'grid'=4] {'blk','grid'}, dimensions={0} | all-to-all | bytes 262144 | tf_op jit(solution)/shard_map/all_to_all | solution.py:351
  86.2 3.5 %shard_map.35 = (bf16[32,16,512]{2,1,0:T(8,128)(2,1)}, f32[32,32]{1,0:T(8,128)}) custom-call(f32[32,8,128]{2,1,0:T(8,128)} %all_to_all.11.parts_ref, bf16[32,16,512]{2,1,0:T(8,128)(2,1)} %all_to_all.10.x_ref), custom_call_target="tpu_custom_call" | custom-call | tf_op jit(solution)/shard_map/pallas_call | solution.py:352
  (4 shorter events, 0.1 us)
Async XLA Ops:
  1.7 9.3 %collective-permute-start.1 = (bf16[2,16,4096]{2,1,0:T(8,128)(2,1)S(1)}, bf16[2,16,4096]{2,1,0:T(8,128)(2,1)S(1)}, u32[]{:S(2)}, u32[]{:S(2)}) collective-permute-start(bf16[2,16,4096]{2,1,0:T(8,128)(2,1)S(1)} %get-tuple-element.11.refs_0_), channel_id=1, source_target_pairs={{0,2},{1,3},{2,0},{3,1},{4,6},{5,7},{6,4},{7,5},{8,10},{9,11},{10,... | collective-permute-start | bytes 786440 | tf_op jit(solution)/shard_map/ppermute | solution.py:286
  4.8 6.3 %collective-permute-start = (bf16[2,16,4096]{2,1,0:T(8,128)(2,1)S(1)}, bf16[2,16,4096]{2,1,0:T(8,128)(2,1)S(1)}, u32[]{:S(2)}, u32[]{:S(2)}) collective-permute-start(bf16[2,16,4096]{2,1,0:T(8,128)(2,1)S(1)} %get-tuple-element.12.refs_4_), channel_id=1, source_target_pairs={{0,1},{1,0},{2,3},{3,2},{4,5},{5,4},{6,7},{7,6},{8,9},{9,8},{10,11... | collective-permute-start | bytes 786440 | tf_op jit(solution)/shard_map/ppermute | solution.py:286
  4.8 11.2 %collective-permute-start.6 = (bf16[2,16,4096]{2,1,0:T(8,128)(2,1)S(1)}, bf16[2,16,4096]{2,1,0:T(8,128)(2,1)S(1)}, u32[]{:S(2)}, u32[]{:S(2)}) collective-permute-start(bf16[2,16,4096]{2,1,0:T(8,128)(2,1)S(1)} %get-tuple-element.11.refs_0_), channel_id=1, source_target_pairs={{0,8},{4,12},{8,16},{12,20},{16,24},{20,28},{24,0},{28,4},{1,9},{5... | collective-permute-start | bytes 786440 | tf_op jit(solution)/shard_map/ppermute | solution.py:302
  6.3 21.6 %collective-permute-start.3 = (bf16[2,16,4096]{2,1,0:T(8,128)(2,1)S(1)}, bf16[2,16,4096]{2,1,0:T(8,128)(2,1)S(1)}, u32[]{:S(2)}, u32[]{:S(2)}) collective-permute-start(bf16[2,16,4096]{2,1,0:T(8,128)(2,1)S(1)} %get-tuple-element.11.refs_0_), channel_id=1, source_target_pairs={{0,1},{3,2},{4,5},{7,6},{8,9},{11,10},{12,13},{15,14},{16,17},{19,... | collective-permute-start | bytes 786440 | tf_op jit(solution)/shard_map/ppermute | solution.py:286
  10.6 20.3 %copy-start.1 = (f32[4096,128]{1,0:T(8,128)S(1)}, f32[4096,128]{1,0:T(8,128)}, u32[]{:S(2)}) copy-start(f32[4096,128]{1,0:T(8,128)} %get-tuple-element.17.refs_13_) | copy-start | bytes 6291460
  11.1 11.0 %collective-permute-start.8 = (bf16[2,16,4096]{2,1,0:T(8,128)(2,1)S(1)}, bf16[2,16,4096]{2,1,0:T(8,128)(2,1)S(1)}, u32[]{:S(2)}, u32[]{:S(2)}) collective-permute-start(bf16[2,16,4096]{2,1,0:T(8,128)(2,1)S(1)} %collective-permute-done.refs_1_), channel_id=1, source_target_pairs={{0,8},{4,12},{8,16},{12,20},{16,24},{20,28},{24,0},{28,4},{1,9},{5... | collective-permute-start | bytes 786440 | tf_op jit(solution)/shard_map/ppermute | solution.py:302
  12.9 11.0 %collective-permute-start.2 = (bf16[2,16,4096]{2,1,0:T(8,128)(2,1)S(1)}, bf16[2,16,4096]{2,1,0:T(8,128)(2,1)S(1)}, u32[]{:S(2)}, u32[]{:S(2)}) collective-permute-start(bf16[2,16,4096]{2,1,0:T(8,128)(2,1)S(1)} %collective-permute-done.refs_1_), channel_id=1, source_target_pairs={{0,2},{1,3},{2,0},{3,1},{4,6},{5,7},{6,4},{7,5},{8,10},{9,11},{10,... | collective-permute-start | bytes 786440 | tf_op jit(solution)/shard_map/ppermute | solution.py:286
  14.4 12.2 %collective-permute-start.10 = (bf16[2,16,4096]{2,1,0:T(8,128)(2,1)S(1)}, bf16[2,16,4096]{2,1,0:T(8,128)(2,1)S(1)}, u32[]{:S(2)}, u32[]{:S(2)}) collective-permute-start(bf16[2,16,4096]{2,1,0:T(8,128)(2,1)S(1)} %collective-permute-done.1.refs_2_), channel_id=1, source_target_pairs={{0,8},{4,12},{8,16},{12,20},{16,24},{20,28},{24,0},{28,4},{1,9},{5... | collective-permute-start | bytes 786440 | tf_op jit(solution)/shard_map/ppermute | solution.py:302
  16.0 13.5 %collective-permute-start.5 = (bf16[2,16,4096]{2,1,0:T(8,128)(2,1)S(1)}, bf16[2,16,4096]{2,1,0:T(8,128)(2,1)S(1)}, u32[]{:S(2)}, u32[]{:S(2)}) collective-permute-start(bf16[2,16,4096]{2,1,0:T(8,128)(2,1)S(1)} %collective-permute-done.1.refs_2_), channel_id=1, source_target_pairs={{0,1},{3,2},{4,5},{7,6},{8,9},{11,10},{12,13},{15,14},{16,17},{19,... | collective-permute-start | bytes 786440 | tf_op jit(solution)/shard_map/ppermute | solution.py:286
  22.1 7.9 %collective-permute-start.9 = (bf16[2,16,4096]{2,1,0:T(8,128)(2,1)S(1)}, bf16[2,16,4096]{2,1,0:T(8,128)(2,1)S(1)}, u32[]{:S(2)}, u32[]{:S(2)}) collective-permute-start(bf16[2,16,4096]{2,1,0:T(8,128)(2,1)S(1)} %broadcast_select_fusion.1), channel_id=1, source_target_pairs={{0,4},{4,0},{8,12},{12,8},{16,20},{20,16},{24,28},{28,24},{1,5},{5... | collective-permute-start | bytes 786440 | tf_op jit(solution)/shard_map/ppermute | solution.py:286
  23.9 7.0 %collective-permute-start.13 = (bf16[2,16,4096]{2,1,0:T(8,128)(2,1)S(1)}, bf16[2,16,4096]{2,1,0:T(8,128)(2,1)S(1)}, u32[]{:S(2)}, u32[]{:S(2)}) collective-permute-start(bf16[2,16,4096]{2,1,0:T(8,128)(2,1)S(1)} %collective-permute-done.8.refs_9_), channel_id=1, source_target_pairs={{0,2},{1,3},{2,0},{3,1},{4,6},{5,7},{6,4},{7,5},{8,10},{9,11},{10,... | collective-permute-start | bytes 786440 | tf_op jit(solution)/shard_map/ppermute | solution.py:286
  26.6 4.3 %collective-permute-start.4 = (bf16[2,16,4096]{2,1,0:T(8,128)(2,1)S(1)}, bf16[2,16,4096]{2,1,0:T(8,128)(2,1)S(1)}, u32[]{:S(2)}, u32[]{:S(2)}) collective-permute-start(bf16[2,16,4096]{2,1,0:T(8,128)(2,1)S(1)} %collective-permute-done.2.refs_3_), channel_id=1, source_target_pairs={{0,1},{3,2},{4,5},{7,6},{8,9},{11,10},{12,13},{15,14},{16,17},{19,... | collective-permute-start | bytes 786440 | tf_op jit(solution)/shard_map/ppermute | solution.py:286
  27.9 9.2 %collective-permute-start.7 = (bf16[2,16,4096]{2,1,0:T(8,128)(2,1)S(1)}, bf16[2,16,4096]{2,1,0:T(8,128)(2,1)S(1)}, u32[]{:S(2)}, u32[]{:S(2)}) collective-permute-start(bf16[2,16,4096]{2,1,0:T(8,128)(2,1)S(1)} %broadcast_select_fusion.2), channel_id=1, source_target_pairs={{0,4},{4,0},{8,12},{12,8},{16,20},{20,16},{24,28},{28,24},{1,5},{5... | collective-permute-start | bytes 786440 | tf_op jit(solution)/shard_map/ppermute | solution.py:286
  29.5 11.3 %collective-permute-start.11 = (bf16[2,16,4096]{2,1,0:T(8,128)(2,1)S(1)}, bf16[2,16,4096]{2,1,0:T(8,128)(2,1)S(1)}, u32[]{:S(2)}, u32[]{:S(2)}) collective-permute-start(bf16[2,16,4096]{2,1,0:T(8,128)(2,1)S(1)} %broadcast_select_fusion), channel_id=1, source_target_pairs={{0,4},{4,0},{8,12},{12,8},{16,20},{20,16},{24,28},{28,24},{1,5},{5... | collective-permute-start | bytes 786440 | tf_op jit(solution)/shard_map/ppermute | solution.py:286
  30.0 10.8 %collective-permute-start.12 = (bf16[2,16,4096]{2,1,0:T(8,128)(2,1)S(1)}, bf16[2,16,4096]{2,1,0:T(8,128)(2,1)S(1)}, u32[]{:S(2)}, u32[]{:S(2)}) collective-permute-start(bf16[2,16,4096]{2,1,0:T(8,128)(2,1)S(1)} %collective-permute-done.9.refs_9_), channel_id=1, source_target_pairs={{0,2},{1,3},{2,0},{3,1},{4,6},{5,7},{6,4},{7,5},{8,10},{9,11},{10,... | collective-permute-start | bytes 786440 | tf_op jit(solution)/shard_map/ppermute | solution.py:286
  30.9 1.0 %copy-start.2 = (bf16[3,256,256]{2,1,0:T(8,128)(2,1)S(1)}, bf16[3,256,256]{2,1,0:T(8,128)(2,1)}, u32[]{:S(2)}) copy-start(bf16[3,256,256]{2,1,0:T(8,128)(2,1)} %get-tuple-element.16.refs_12_) | copy-start | bytes 1179652
  31.9 8.9 %copy-start.3 = (bf16[3,256,256]{2,1,0:T(8,128)(2,1)S(1)}, bf16[3,256,256]{2,1,0:T(8,128)(2,1)}, u32[]{:S(2)}) copy-start(bf16[3,256,256]{2,1,0:T(8,128)(2,1)} %get-tuple-element.16.refs_12_) | copy-start | bytes 1179652
  45.5 1.0 %copy-start = (f32[64,4096]{1,0:T(8,128)}, f32[64,4096]{1,0:T(8,128)S(1)}, u32[]{:S(2)}) copy-start(f32[64,4096]{1,0:T(8,128)S(1)} %get-tuple-element.18.keep_ref) | copy-start | bytes 3145732
  46.5 1.9 %collective-permute-start.14 = (bf16[64,4096]{1,0:T(8,128)(2,1)S(1)}, bf16[64,4096]{1,0:T(8,128)(2,1)S(1)}, u32[]{:S(2)}, u32[]{:S(2)}) collective-permute-start(bf16[64,4096]{1,0:T(8,128)(2,1)S(1)} %get-tuple-element.19), channel_id=1, source_target_pairs={{0,1},{1,0},{2,3},{3,2},{4,5},{5,4},{6,7},{7,6},{8,9},{9,8},{10,11... | collective-permute-start | bytes 1572872 | tf_op jit(solution)/shard_map/ppermute | solution.py:286
  48.4 0.8 copy-start.4

commit v5 on v4

--- a/solution.py
+++ b/solution.py
@@ -22,6 +22,7 @@
 SMEM = pl.BlockSpec(memory_space=pltpu.SMEM)
 LANES = 128
 ROW_PAD = 1
+SMALL_VMEM = 10 * 1024 * 1024
 QUAD = 4
 PANEL = 8
 
@@ -82,6 +83,7 @@
             jax.ShapeDtypeStruct((NX * NY, LANES), F32),
         ),
         out_specs=(VMEM, VMEM),
+        compiler_params=pltpu.CompilerParams(vmem_limit_bytes=SMALL_VMEM),
         cost_estimate=pl.CostEstimate(flops=1 << 28, bytes_accessed=3 << 20, transcendentals=0),
     )()
 
@@ -333,6 +335,7 @@
         out_shape=jax.ShapeDtypeStruct(shape, BF),
         in_specs=[VMEM, VMEM],
         out_specs=VMEM,
+        compiler_params=pltpu.CompilerParams(vmem_limit_bytes=SMALL_VMEM),
     )(mine, other)
     if chunk % LANES:
         updated = updated.reshape(slabs, slab_rows, blocks, chunk).transpose(2, 0, 1, 3)
@@ -347,6 +350,7 @@
             out_shape=jax.ShapeDtypeStruct((devices, devices * devices // LANES, LANES), F32),
             in_specs=[VMEM],
             out_specs=VMEM,
+            compiler_params=pltpu.CompilerParams(vmem_limit_bytes=SMALL_VMEM),
         )(cellwise)
         parts = lax.all_to_all(local, ("blk", "grid"), 0, 0, tiled=True)
         return pl.pallas_call(
@@ -357,6 +361,7 @@
             ),
             in_specs=[VMEM, VMEM],
             out_specs=(VMEM, VMEM),
+            compiler_params=pltpu.CompilerParams(vmem_limit_bytes=SMALL_VMEM),
         )(parts, cellwise)
     flat = cellwise.reshape(devices, slab_rows * chunk)
     local = jnp.dot(flat, flat.T, preferred_element_type=F32)

time: 90.2 us -> 82.4 us (0.914)
  Pallas kernels: 19.2 us -> 12.9 us
  local copies, waits for them, and re-layouts: 3.85 us -> 1.07 us
  waiting for transfers between devices: 12.9 us -> 15.2 us
    unnamed x10 -> x0, local copies, waits for them, and re-layouts: 2.78 us -> none
    ppermute x12, waiting for transfers between devices: 6.92 us -> 9.24 us  [exchanged(): lax.ppermute(x, axis, [(i, i ^ by) for i in range(lax.axis_size(axis)) if...]
    pallas_call x1, Pallas kernels: 2.24 us -> 0.09 us  [body(): pl.pallas_call(functools.partial(combine_kernel, slabs), out_shape=jax.Sh...]
    pallas_call x1, Pallas kernels: 2.41 us -> 0.71 us  [body(): pl.pallas_call(gram_kernel, out_shape=jax.ShapeDtypeStruct((devices, devi...]
    pallas_call x1, Pallas kernels: 2.11 us -> 0.79 us  [make_tables(): pl.pallas_call(functools.partial(table_kernel, slab_rows), out_shape=(jax...]
    pallas_call x1, Pallas kernels: 3.49 us -> 2.37 us  [body(): pl.pallas_call(functools.partial(rotate_kernel, 1.0 / cell_count), out_sh...]
  transfers between devices with their start and end apart: 15 -> 15, of which waited for: 6 -> 6; matrix products, arithmetic and copies ran while one was open for 0% -> 0% of each run, Pallas kernels for 7% -> 6%
where the time goes in v5:
time: 82.4 us; the launch traced here: 82.2 us
  blocking collectives  31.6 us (38%)
  starting transfers between devices  20.6 us (25%)
  waiting for transfers between devices  15.2 us (18%)
  Pallas kernels  12.9 us (16%)
  local copies, waits for them, and re-layouts  1.07 us (1%)
    all_to_all x1, blocking collectives, body(): cellwise = lax.all_to_all(updated, ('blk', 'grid'), 0, 0, tiled=True)  20.6 us
    ppermute x12, starting transfers between devices, exchanged(): lax.ppermute(x, axis, [(i, i ^ by) for i in range(lax.axis_size(axis)) if...  15.6 us
    all_to_all x1, blocking collectives, body(): parts = lax.all_to_all(local, ('blk', 'grid'), 0, 0, tiled=True)  11 us
    ppermute x12, waiting for transfers between devices, exchanged(): lax.ppermute(x, axis, [(i, i ^ by) for i in range(lax.axis_size(axis)) if...  9.24 us
    pallas_call x2, Pallas kernels, add_block(): pl.pallas_call(lambda *refs: block_kernel(slabs, final, refs), out_shape=...  8.96 us
    ppermute x3, waiting for transfers between devices, shifted(): lax.ppermute(x, 'blk', [(i, (i + 2) % blocks) for i in range(blocks)])  5.94 us
    ppermute x3, starting transfers between devices, shifted(): lax.ppermute(x, 'blk', [(i, (i + 2) % blocks) for i in range(blocks)])  4.98 us
    pallas_call x1, Pallas kernels, body(): pl.pallas_call(functools.partial(rotate_kernel, 1.0 / cell_count), out_sh...  2.37 us
  transfers between devices with their start and end apart: 15, of which 6 were waited for; matrix products, arithmetic and copies ran while one was open for 0% of the time, Pallas kernels for 6%

profile of v5, /device:TPU:0, one launch (start us, length us, event | category | flops | bytes accessed | tf_op | source)
XLA Modules:
  0.0 82.2 jit_solution(3487974285808798839)
XLA Ops:
  0.6 1.1 %constant_dynamic-slice_fusion = (bf16[2,16,4096]{2,1,0:T(8,128)(2,1)S(1)}, bf16[2,16,4096]{2,1,0:T(8,128)(2,1)S(1)}) fusion(bf16[4,16,4096]{2,1,0:T(8,128)(2,1)} %param.1, s32[]{:T(128)S(6)} %select_n.35, s32[]{:T(128)S(6)} %select_n.34), kind=kLoop, calls=%fused_computation.3 | loop fusion | bytes 1048584 | tf_op jit(solution)/shard_map/dynamic_slice | solution.py:313
  1.7 3.0 %collective-permute-start.1 = (bf16[2,16,4096]{2,1,0:T(8,128)(2,1)S(1)}, bf16[2,16,4096]{2,1,0:T(8,128)(2,1)S(1)}, u32[]{:S(2)}, u32[]{:S(2)}) collective-permute-start(bf16[2,16,4096]{2,1,0:T(8,128)(2,1)S(1)} %get-tuple-element.11.refs_0_), channel_id=1, source_target_pairs={{0,2},{1,3},{2,0},{3,1},{4,6},{5,7},{6,4},{7,5},{8,10},{9,11},{10,... | collective-permute-start | bytes 786440 | tf_op jit(solution)/shard_map/ppermute | solution.py:288
  4.8 0.0 collective-permute-start
  4.8 1.6 %collective-permute-start.6 = (bf16[2,16,4096]{2,1,0:T(8,128)(2,1)S(1)}, bf16[2,16,4096]{2,1,0:T(8,128)(2,1)S(1)}, u32[]{:S(2)}, u32[]{:S(2)}) collective-permute-start(bf16[2,16,4096]{2,1,0:T(8,128)(2,1)S(1)} %get-tuple-element.11.refs_0_), channel_id=1, source_target_pairs={{0,8},{4,12},{8,16},{12,20},{16,24},{20,28},{24,0},{28,4},{1,9},{5... | collective-permute-start | bytes 786440 | tf_op jit(solution)/shard_map/ppermute | solution.py:304
  6.3 2.1 %collective-permute-start.3 = (bf16[2,16,4096]{2,1,0:T(8,128)(2,1)S(1)}, bf16[2,16,4096]{2,1,0:T(8,128)(2,1)S(1)}, u32[]{:S(2)}, u32[]{:S(2)}) collective-permute-start(bf16[2,16,4096]{2,1,0:T(8,128)(2,1)S(1)} %get-tuple-element.11.refs_0_), channel_id=1, source_target_pairs={{0,1},{3,2},{4,5},{7,6},{8,9},{11,10},{12,13},{15,14},{16,17},{19,... | collective-permute-start | bytes 786440 | tf_op jit(solution)/shard_map/ppermute | solution.py:288
  8.5 0.8 shard_map.30
  9.3 1.8 %collective-permute-done.1.refs_2_ = bf16[2,16,4096]{2,1,0:T(8,128)(2,1)S(1)} collective-permute-done((bf16[2,16,4096]{2,1,0:T(8,128)(2,1)S(1)}, bf16[2,16,4096]{2,1,0:T(8,128)(2,1)S(1)}, u32[]{:S(2)}, u32[]{:S(2)}) %collective-permute-start.1) | collective-permute-done | bytes 262176 | tf_op jit(solution)/shard_map/ppermute | solution.py:288
  11.1 0.0 collective-permute-done.refs_1_
  11.1 1.8 %collective-permute-start.8 = (bf16[2,16,4096]{2,1,0:T(8,128)(2,1)S(1)}, bf16[2,16,4096]{2,1,0:T(8,128)(2,1)S(1)}, u32[]{:S(2)}, u32[]{:S(2)}) collective-permute-start(bf16[2,16,4096]{2,1,0:T(8,128)(2,1)S(1)} %collective-permute-done.refs_1_), channel_id=1, source_target_pairs={{0,8},{4,12},{8,16},{12,20},{16,24},{20,28},{24,0},{28,4},{1,9},{5... | collective-permute-start | bytes 786440 | tf_op jit(solution)/shard_map/ppermute | solution.py:304
  12.9 1.5 %collective-permute-start.2 = (bf16[2,16,4096]{2,1,0:T(8,128)(2,1)S(1)}, bf16[2,16,4096]{2,1,0:T(8,128)(2,1)S(1)}, u32[]{:S(2)}, u32[]{:S(2)}) collective-permute-start(bf16[2,16,4096]{2,1,0:T(8,128)(2,1)S(1)} %collective-permute-done.refs_1_), channel_id=1, source_target_pairs={{0,2},{1,3},{2,0},{3,1},{4,6},{5,7},{6,4},{7,5},{8,10},{9,11},{10,... | collective-permute-start | bytes 786440 | tf_op jit(solution)/shard_map/ppermute | solution.py:288
  14.4 1.6 %collective-permute-start.10 = (bf16[2,16,4096]{2,1,0:T(8,128)(2,1)S(1)}, bf16[2,16,4096]{2,1,0:T(8,128)(2,1)S(1)}, u32[]{:S(2)}, u32[]{:S(2)}) collective-permute-start(bf16[2,16,4096]{2,1,0:T(8,128)(2,1)S(1)} %collective-permute-done.1.refs_2_), channel_id=1, source_target_pairs={{0,8},{4,12},{8,16},{12,20},{16,24},{20,28},{24,0},{28,4},{1,9},{5... | collective-permute-start | bytes 786440 | tf_op jit(solution)/shard_map/ppermute | solution.py:304
  16.0 0.0 collective-permute-done.6.refs_8_
  16.0 1.3 %collective-permute-start.5 = (bf16[2,16,4096]{2,1,0:T(8,128)(2,1)S(1)}, bf16[2,16,4096]{2,1,0:T(8,128)(2,1)S(1)}, u32[]{:S(2)}, u32[]{:S(2)}) collective-permute-start(bf16[2,16,4096]{2,1,0:T(8,128)(2,1)S(1)} %collective-permute-done.1.refs_2_), channel_id=1, source_target_pairs={{0,1},{3,2},{4,5},{7,6},{8,9},{11,10},{12,13},{15,14},{16,17},{19,... | collective-permute-start | bytes 786440 | tf_op jit(solution)/shard_map/ppermute | solution.py:288
  17.3 4.8 %collective-permute-done.8.refs_9_ = bf16[2,16,4096]{2,1,0:T(8,128)(2,1)S(1)} collective-permute-done((bf16[2,16,4096]{2,1,0:T(8,128)(2,1)S(1)}, bf16[2,16,4096]{2,1,0:T(8,128)(2,1)S(1)}, u32[]{:S(2)}, u32[]{:S(2)}) %collective-permute-start.8) | collective-permute-done | bytes 262176 | tf_op jit(solution)/shard_map/ppermute | solution.py:304
  22.1 1.8 %collective-permute-start.9 = (bf16[2,16,4096]{2,1,0:T(8,128)(2,1)S(1)}, bf16[2,16,4096]{2,1,0:T(8,128)(2,1)S(1)}, u32[]{:S(2)}, u32[]{:S(2)}) collective-permute-start(bf16[2,16,4096]{2,1,0:T(8,128)(2,1)S(1)} %broadcast_select_fusion.1), channel_id=1, source_target_pairs={{0,4},{4,0},{8,12},{12,8},{16,20},{20,16},{24,28},{28,24},{1,5},{5... | collective-permute-start | bytes 786440 | tf_op jit(solution)/shard_map/ppermute | solution.py:288
  23.9 0.0 collective-permute-done.2.refs_3_
  23.9 1.5 %collective-permute-start.13 = (bf16[2,16,4096]{2,1,0:T(8,128)(2,1)S(1)}, bf16[2,16,4096]{2,1,0:T(8,128)(2,1)S(1)}, u32[]{:S(2)}, u32[]{:S(2)}) collective-permute-start(bf16[2,16,4096]{2,1,0:T(8,128)(2,1)S(1)} %collective-permute-done.8.refs_9_), channel_id=1, source_target_pairs={{0,2},{1,3},{2,0},{3,1},{4,6},{5,7},{6,4},{7,5},{8,10},{9,11},{10,... | collective-permute-start | bytes 786440 | tf_op jit(solution)/shard_map/ppermute | solution.py:288
  25.4 1.2 %collective-permute-done.10.refs_10_ = bf16[2,16,4096]{2,1,0:T(8,128)(2,1)S(1)} collective-permute-done((bf16[2,16,4096]{2,1,0:T(8,128)(2,1)S(1)}, bf16[2,16,4096]{2,1,0:T(8,128)(2,1)S(1)}, u32[]{:S(2)}, u32[]{:S(2)}) %collective-permute-start.10) | collective-permute-done | bytes 262176 | tf_op jit(solution)/shard_map/ppermute | solution.py:304
  26.6 1.3 %collective-permute-start.4 = (bf16[2,16,4096]{2,1,0:T(8,128)(2,1)S(1)}, bf16[2,16,4096]{2,1,0:T(8,128)(2,1)S(1)}, u32[]{:S(2)}, u32[]{:S(2)}) collective-permute-start(bf16[2,16,4096]{2,1,0:T(8,128)(2,1)S(1)} %collective-permute-done.2.refs_3_), channel_id=1, source_target_pairs={{0,1},{3,2},{4,5},{7,6},{8,9},{11,10},{12,13},{15,14},{16,17},{19,... | collective-permute-start | bytes 786440 | tf_op jit(solution)/shard_map/ppermute | solution.py:288
  27.9 0.0 collective-permute-done.3.refs_5_
  27.9 1.6 %collective-permute-start.7 = (bf16[2,16,4096]{2,1,0:T(8,128)(2,1)S(1)}, bf16[2,16,4096]{2,1,0:T(8,128)(2,1)S(1)}, u32[]{:S(2)}, u32[]{:S(2)}) collective-permute-start(bf16[2,16,4096]{2,1,0:T(8,128)(2,1)S(1)} %broadcast_select_fusion.2), channel_id=1, source_target_pairs={{0,4},{4,0},{8,12},{12,8},{16,20},{20,16},{24,28},{28,24},{1,5},{5... | collective-permute-start | bytes 786440 | tf_op jit(solution)/shard_map/ppermute | solution.py:288
  29.5 0.0 collective-permute-done.5.refs_7_
  29.5 0.5 collective-permute-start.11
  30.0 0.0 collective-permute-done.9.refs_9_
  30.0 0.9 %collective-permute-start.12 = (bf16[2,16,4096]{2,1,0:T(8,128)(2,1)S(1)}, bf16[2,16,4096]{2,1,0:T(8,128)(2,1)S(1)}, u32[]{:S(2)}, u32[]{:S(2)}) collective-permute-start(bf16[2,16,4096]{2,1,0:T(8,128)(2,1)S(1)} %collective-permute-done.9.refs_9_), channel_id=1, source_target_pairs={{0,2},{1,3},{2,0},{3,1},{4,6},{5,7},{6,4},{7,5},{8,10},{9,11},{10,... | collective-permute-start | bytes 786440 | tf_op jit(solution)/shard_map/ppermute | solution.py:288
  30.9 0.0 collective-permute-done.13.refs_11_
  30.9 0.0 collective-permute-done.4.refs_6_
  30.9 4.3 %shard_map.31.refs_14_ = f32[2,64,4096]{2,1,0:T(8,128)S(1)} custom-call(bf16[2,16,4096]{2,1,0:T(8,128)(2,1)S(1)} %get-tuple-element.11.refs_0_, bf16[2,16,4096]{2,1,0:T(8,128)(2,1)S(1)} %collective-permute-done.refs_1_, bf16[2,16,4096]{2,1,0:T(8,128)(2,1)S(1)} %collective-permute-done.1.refs_2_, bf16[2,16,4096]{2,1,0:T(8,128)(2,1)S(1)} %collective-permute-done.2.refs_3_, ...), custom_call_target="tpu_custom_call" | custom-call | flops 3221225472 | bytes 8388608 | tf_op jit(solution)/shard_map/pallas_call | solution.py:201
  35.2 1.9 %collective-permute-done.7.refs_8_ = bf16[2,16,4096]{2,1,0:T(8,128)(2,1)S(1)} collective-permute-done((bf16[2,16,4096]{2,1,0:T(8,128)(2,1)S(1)}, bf16[2,16,4096]{2,1,0:T(8,128)(2,1)S(1)}, u32[]{:S(2)}, u32[]{:S(2)}) %collective-permute-start.7) | collective-permute-done | bytes 262176 | tf_op jit(solution)/shard_map/ppermute | solution.py:288
  37.2 3.6 %collective-permute-done.11.refs_10_ = bf16[2,16,4096]{2,1,0:T(8,128)(2,1)S(1)} collective-permute-done((bf16[2,16,4096]{2,1,0:T(8,128)(2,1)S(1)}, bf16[2,16,4096]{2,1,0:T(8,128)(2,1)S(1)}, u32[]{:S(2)}, u32[]{:S(2)}) %collective-permute-start.11) | collective-permute-done | bytes 262176 | tf_op jit(solution)/shard_map/ppermute | solution.py:288
  40.8 0.0 collective-permute-done.12.refs_11_
  40.8 4.6 %shard_map.32 = (f32[64,4096]{1,0:T(8,128)S(1)}, bf16[64,4096]{1,0:T(8,128)(2,1)S(1)}) custom-call(bf16[2,16,4096]{2,1,0:T(8,128)(2,1)S(1)} %get-tuple-element.11.refs_0_, bf16[2,16,4096]{2,1,0:T(8,128)(2,1)S(1)} %collective-permute-done.refs_1_, bf16[2,16,4096]{2,1,0:T(8,128)(2,1)S(1)} %collective-permute-done.1.refs_2_, ...), custom_call_target="tpu_custom_call" | custom-call | flops 3221225472 | bytes 8388608 | tf_op jit(solution)/shard_map/pallas_call | solution.py:201
  45.4 0.1 collective-permute-start.14
  45.5 1.9 %collective-permute-done.14.part_ref = bf16[64,4096]{1,0:T(8,128)(2,1)S(1)} collective-permute-done((bf16[64,4096]{1,0:T(8,128)(2,1)S(1)}, bf16[64,4096]{1,0:T(8,128)(2,1)S(1)}, u32[]{:S(2)}, u32[]{:S(2)}) %collective-permute-start.14) | collective-permute-done | bytes 524320 | tf_op jit(solution)/shard_map/ppermute | solution.py:288
  47.4 0.1 shard_map.33
  47.5 20.6 %all_to_all.10.x_ref = bf16[32,16,512]{2,1,0:T(8,128)(2,1)S(1)} all-to-all(bf16[32,16,512]{2,1,0:T(8,128)(2,1)S(1)} %bitcast.1), channel_id=1, replica_groups=mesh['blk'=8,'grid'=4] {'blk','grid'}, dimensions={0} | all-to-all | bytes 1048576 | tf_op jit(solution)/shard_map/all_to_all | solution.py:343
  68.1 0.7 shard_map.34
  68.9 11.0 %all_to_all.11.parts_ref = f32[32,8,128]{2,1,0:T(8,128)S(1)} all-to-all(f32[32,8,128]{2,1,0:T(8,128)S(1)} %shard_map.34), channel_id=1, replica_groups=mesh['blk'=8,'grid'=4] {'blk','grid'}, dimensions={0} | all-to-all | bytes 262144 | tf_op jit(solution)/shard_map/all_to_all | solution.py:355
  79.8 2.4 %shard_map.35 = (bf16[32,16,512]{2,1,0:T(8,128)(2,1)}, f32[32,32]{1,0:T(8,128)}) custom-call(f32[32,8,128]{2,1,0:T(8,128)S(1)} %all_to_all.11.parts_ref, bf16[32,16,512]{2,1,0:T(8,128)(2,1)S(1)} %all_to_all.10.x_ref), custom_call_target="tpu_custom_call" | custom-call | tf_op jit(solution)/shard_map/pallas_call | solution.py:356
  (3 shorter events, 0.1 us)
Async XLA Ops:
  1.7 9.3 %collective-permute-start.1 = (bf16[2,16,4096]{2,1,0:T(8,128)(2,1)S(1)}, bf16[2,16,4096]{2,1,0:T(8,128)(2,1)S(1)}, u32[]{:S(2)}, u32[]{:S(2)}) collective-permute-start(bf16[2,16,4096]{2,1,0:T(8,128)(2,1)S(1)} %get-tuple-element.11.refs_0_), channel_id=1, source_target_pairs={{0,2},{1,3},{2,0},{3,1},{4,6},{5,7},{6,4},{7,5},{8,10},{9,11},{10,... | collective-permute-start | bytes 786440 | tf_op jit(solution)/shard_map/ppermute | solution.py:288
  4.8 6.3 %collective-permute-start = (bf16[2,16,4096]{2,1,0:T(8,128)(2,1)S(1)}, bf16[2,16,4096]{2,1,0:T(8,128)(2,1)S(1)}, u32[]{:S(2)}, u32[]{:S(2)}) collective-permute-start(bf16[2,16,4096]{2,1,0:T(8,128)(2,1)S(1)} %get-tuple-element.12.refs_4_), channel_id=1, source_target_pairs={{0,1},{1,0},{2,3},{3,2},{4,5},{5,4},{6,7},{7,6},{8,9},{9,8},{10,11... | collective-permute-start | bytes 786440 | tf_op jit(solution)/shard_map/ppermute | solution.py:288
  4.8 11.2 %collective-permute-start.6 = (bf16[2,16,4096]{2,1,0:T(8,128)(2,1)S(1)}, bf16[2,16,4096]{2,1,0:T(8,128)(2,1)S(1)}, u32[]{:S(2)}, u32[]{:S(2)}) collective-permute-start(bf16[2,16,4096]{2,1,0:T(8,128)(2,1)S(1)} %get-tuple-element.11.refs_0_), channel_id=1, source_target_pairs={{0,8},{4,12},{8,16},{12,20},{16,24},{20,28},{24,0},{28,4},{1,9},{5... | collective-permute-start | bytes 786440 | tf_op jit(solution)/shard_map/ppermute | solution.py:304
  6.3 21.6 %collective-permute-start.3 = (bf16[2,16,4096]{2,1,0:T(8,128)(2,1)S(1)}, bf16[2,16,4096]{2,1,0:T(8,128)(2,1)S(1)}, u32[]{:S(2)}, u32[]{:S(2)}) collective-permute-start(bf16[2,16,4096]{2,1,0:T(8,128)(2,1)S(1)} %get-tuple-element.11.refs_0_), channel_id=1, source_target_pairs={{0,1},{3,2},{4,5},{7,6},{8,9},{11,10},{12,13},{15,14},{16,17},{19,... | collective-permute-start | bytes 786440 | tf_op jit(solution)/shard_map/ppermute | solution.py:288
  11.1 11.0 %collective-permute-start.8 = (bf16[2,16,4096]{2,1,0:T(8,128)(2,1)S(1)}, bf16[2,16,4096]{2,1,0:T(8,128)(2,1)S(1)}, u32[]{:S(2)}, u32[]{:S(2)}) collective-permute-start(bf16[2,16,4096]{2,1,0:T(8,128)(2,1)S(1)} %collective-permute-done.refs_1_), channel_id=1, source_target_pairs={{0,8},{4,12},{8,16},{12,20},{16,24},{20,28},{24,0},{28,4},{1,9},{5... | collective-permute-start | bytes 786440 | tf_op jit(solution)/shard_map/ppermute | solution.py:304
  12.9 11.0 %collective-permute-start.2 = (bf16[2,16,4096]{2,1,0:T(8,128)(2,1)S(1)}, bf16[2,16,4096]{2,1,0:T(8,128)(2,1)S(1)}, u32[]{:S(2)}, u32[]{:S(2)}) collective-permute-start(bf16[2,16,4096]{2,1,0:T(8,128)(2,1)S(1)} %collective-permute-done.refs_1_), channel_id=1, source_target_pairs={{0,2},{1,3},{2,0},{3,1},{4,6},{5,7},{6,4},{7,5},{8,10},{9,11},{10,... | collective-permute-start | bytes 786440 | tf_op jit(solution)/shard_map/ppermute | solution.py:288
  14.4 12.2 %collective-permute-start.10 = (bf16[2,16,4096]{2,1,0:T(8,128)(2,1)S(1)}, bf16[2,16,4096]{2,1,0:T(8,128)(2,1)S(1)}, u32[]{:S(2)}, u32[]{:S(2)}) collective-permute-start(bf16[2,16,4096]{2,1,0:T(8,128)(2,1)S(1)} %collective-permute-done.1.refs_2_), channel_id=1, source_target_pairs={{0,8},{4,12},{8,16},{12,20},{16,24},{20,28},{24,0},{28,4},{1,9},{5... | collective-permute-start | bytes 786440 | tf_op jit(solution)/shard_map/ppermute | solution.py:304
  16.0 13.5 %collective-permute-start.5 = (bf16[2,16,4096]{2,1,0:T(8,128)(2,1)S(1)}, bf16[2,16,4096]{2,1,0:T(8,128)(2,1)S(1)}, u32[]{:S(2)}, u32[]{:S(2)}) collective-permute-start(bf16[2,16,4096]{2,1,0:T(8,128)(2,1)S(1)} %collective-permute-done.1.refs_2_), channel_id=1, source_target_pairs={{0,1},{3,2},{4,5},{7,6},{8,9},{11,10},{12,13},{15,14},{16,17},{19,... | collective-permute-start | bytes 786440 | tf_op jit(solution)/shard_map/ppermute | solution.py:288
  22.1 7.9 %collective-permute-start.9 = (bf16[2,16,4096]{2,1,0:T(8,128)(2,1)S(1)}, bf16[2,16,4096]{2,1,0:T(8,128)(2,1)S(1)}, u32[]{:S(2)}, u32[]{:S(2)}) collective-permute-start(bf16[2,16,4096]{2,1,0:T(8,128)(2,1)S(1)} %broadcast_select_fusion.1), channel_id=1, source_target_pairs={{0,4},{4,0},{8,12},{12,8},{16,20},{20,16},{24,28},{28,24},{1,5},{5... | collective-permute-start | bytes 786440 | tf_op jit(solution)/shard_map/ppermute | solution.py:288
  23.9 7.0 %collective-permute-start.13 = (bf16[2,16,4096]{2,1,0:T(8,128)(2,1)S(1)}, bf16[2,16,4096]{2,1,0:T(8,128)(2,1)S(1)}, u32[]{:S(2)}, u32[]{:S(2)}) collective-permute-start(bf16[2,16,4096]{2,1,0:T(8,128)(2,1)S(1)} %collective-permute-done.8.refs_9_), channel_id=1, source_target_pairs={{0,2},{1,3},{2,0},{3,1},{4,6},{5,7},{6,4},{7,5},{8,10},{9,11},{10,... | collective-permute-start | bytes 786440 | tf_op jit(solution)/shard_map/ppermute | solution.py:288
  26.6 4.3 %collective-permute-start.4 = (bf16[2,16,4096]{2,1,0:T(8,128)(2,1)S(1)}, bf16[2,16,4096]{2,1,0:T(8,128)(2,1)S(1)}, u32[]{:S(2)}, u32[]{:S(2)}) collective-permute-start(bf16[2,16,4096]{2,1,0:T(8,128)(2,1)S(1)} %collective-permute-done.2.refs_3_), channel_id=1, source_target_pairs={{0,1},{3,2},{4,5},{7,6},{8,9},{11,10},{12,13},{15,14},{16,17},{19,... | collective-permute-start | bytes 786440 | tf_op jit(solution)/shard_map/ppermute | solution.py:288
  27.9 9.2 %collective-permute-start.7 = (bf16[2,16,4096]{2,1,0:T(8,128)(2,1)S(1)}, bf16[2,16,4096]{2,1,0:T(8,128)(2,1)S(1)}, u32[]{:S(2)}, u32[]{:S(2)}) collective-permute-start(bf16[2,16,4096]{2,1,0:T(8,128)(2,1)S(1)} %broadcast_select_fusion.2), channel_id=1, source_target_pairs={{0,4},{4,0},{8,12},{12,8},{16,20},{20,16},{24,28},{28,24},{1,5},{5... | collective-permute-start | bytes 786440 | tf_op jit(solution)/shard_map/ppermute | solution.py:288
  29.5 11.3 %collective-permute-start.11 = (bf16[2,16,4096]{2,1,0:T(8,128)(2,1)S(1)}, bf16[2,16,4096]{2,1,0:T(8,128)(2,1)S(1)}, u32[]{:S(2)}, u32[]{:S(2)}) collective-permute-start(bf16[2,16,4096]{2,1,0:T(8,128)(2,1)S(1)} %broadcast_select_fusion), channel_id=1, source_target_pairs={{0,4},{4,0},{8,12},{12,8},{16,20},{20,16},{24,28},{28,24},{1,5},{5... | collective-permute-start | bytes 786440 | tf_op jit(solution)/shard_map/ppermute | solution.py:288
  30.0 10.8 %collective-permute-start.12 = (bf16[2,16,4096]{2,1,0:T(8,128)(2,1)S(1)}, bf16[2,16,4096]{2,1,0:T(8,128)(2,1)S(1)}, u32[]{:S(2)}, u32[]{:S(2)}) collective-permute-start(bf16[2,16,4096]{2,1,0:T(8,128)(2,1)S(1)} %collective-permute-done.9.refs_9_), channel_id=1, source_target_pairs={{0,2},{1,3},{2,0},{3,1},{4,6},{5,7},{6,4},{7,5},{8,10},{9,11},{10,... | collective-permute-start | bytes 786440 | tf_op jit(solution)/shard_map/ppermute | solution.py:288
  45.4 2.0 %collective-permute-start.14 = (bf16[64,4096]{1,0:T(8,128)(2,1)S(1)}, bf16[64,4096]{1,0:T(8,128)(2,1)S(1)}, u32[]{:S(2)}, u32[]{:S(2)}) collective-permute-start(bf16[64,4096]{1,0:T(8,128)(2,1)S(1)} %get-tuple-element.19), channel_id=1, source_target_pairs={{0,1},{1,0},{2,3},{3,2},{4,5},{5,4},{6,7},{7,6},{8,9},{9,8},{10,11... | collective-permute-start | bytes 1572872 | tf_op jit(solution)/shard_map/ppermute | solution.py:288

commit v6 on v5

--- a/solution.py
+++ b/solution.py
@@ -67,7 +67,11 @@
         table = sines(row.astype(F32), column.astype(F32), NX)
         table = jnp.concatenate([table] * (size // LANES), 1)
         for c in range(copies):
-            diag_ref[i, c * NX:(c + 1) * NX, :] = jnp.where(same == c, table, 0.0).astype(BF)
+            block = jnp.where(same == c, table, 0.0).astype(BF)
+            diag_ref[i, c * NX:(c + 1) * NX, :] = block
+            if i == 0:
+                block = (block.astype(F32) * exchange_fraction).astype(BF)
+                diag_ref[len(pairs), c * NX:(c + 1) * NX, :] = block
     lam = eigen_values(down.astype(F32), NX)
     plane = screening + lam + eigen_values(along.astype(F32), NZ)
     for k in range(NX):
@@ -79,7 +83,7 @@
     return pl.pallas_call(
         functools.partial(table_kernel, slab_rows),
         out_shape=(
-            jax.ShapeDtypeStruct((3, size, size), BF),
+            jax.ShapeDtypeStruct((4, size, size), BF),
             jax.ShapeDtypeStruct((NX * NY, LANES), F32),
         ),
         out_specs=(VMEM, VMEM),
@@ -103,27 +107,39 @@
     owns = local[0].shape[0]
     count = src[0].shape[0]
     halves = owns * count * NZ // LANES
-    width = QUAD * NZ
     pitch = work_ref.shape[1] // NY
 
-    def tile(refs, j, off, size):
-        return jnp.concatenate([r[j, :, pl.ds(off, size)] for r in refs], 0)
-
-    def own_tile(o, off, size):
-        return jnp.where(core == chip, tile(local, o, off, size), tile(passed, o, off, size))
+    low = lax.broadcasted_iota(jnp.int32, (NX, LANES), 1) < NZ
+    low16 = lax.broadcasted_iota(jnp.int16, (NX, LANES), 1) < NZ
+
+    def swapped(x):
+        return jnp.concatenate([x[:, NZ:], x[:, :NZ]], 1)
+
+    def tile(refs, j, off):
+        return jnp.concatenate([r[j, :, pl.ds(off, LANES)] for r in refs], 0)
+
+    def own_tile(o, off):
+        j = (core + o) % owns
+        return jnp.where(core == chip, tile(local, j, off), tile(passed, j, off))
 
     def forward(t):
-        off = t * width
         at = t * QUAD * NX
-        mine = [own_tile(o, off, width) for o in range(owns)]
-        others = [tile(src, j, off, width) for j in range(count)]
-        pairs = [m * other for m in mine for other in others]
-        cut = [slice(q * NZ, (q + 1) * NZ) for q in range(QUAD)]
-        density = jnp.concatenate(
-            [jnp.concatenate([p[:, c] for p in pairs], 1) for c in cut], 0)
-        grouped_ref[pl.ds(at, QUAD * NX), :] = jnp.concatenate(
-            [jnp.concatenate([o[:, c] for o in others], 1) for c in cut], 0)
-        first = product(density, tab_ref[0]).astype(BF)
+        rows_d, rows_s = [], []
+        for q in range(0, QUAD, LANES // NZ):
+            off = (t * QUAD + q) * NZ
+            a, b = tile(src, 0, off), tile(src, 1, off)
+            mixed = swapped(jnp.where(low16, b, a))
+            pair = [jnp.where(low16, a, mixed), jnp.where(low16, mixed, b)]
+            rows_s += pair
+            wide = []
+            for o in range(owns):
+                mine = own_tile(o, off)
+                turned = swapped(mine)
+                wide.append([jnp.where(low16, mine, turned), jnp.where(low16, turned, mine)])
+            for y in range(2):
+                rows_d.append(jnp.concatenate([w[y] * pair[y] for w in wide], 1))
+        grouped_ref[pl.ds(at, QUAD * NX), :] = jnp.concatenate(rows_s, 0)
+        first = product(jnp.concatenate(rows_d, 0), tab_ref[0]).astype(BF)
         modes = product(tab_ref[1], first)
         for q in range(QUAD):
             to = (t * QUAD + q) * pitch
@@ -144,8 +160,6 @@
                 work_ref[h, pl.ds(t * QUAD + q, NY, stride=pitch), :] = (
                     back[q * NY:(q + 1) * NY, h * LANES:(h + 1) * LANES])
 
-    lane = lax.broadcasted_iota(jnp.int32, (NX, LANES), 1)
-
     def backward(t):
         at = t * QUAD * NX
         modes = jnp.concatenate([
@@ -153,32 +167,26 @@
                 [work_ref[h, pl.ds((t * QUAD + q) * pitch, NX), :] for h in range(halves)], 1)
             for q in range(QUAD)], 0).astype(BF)
         third = product(tab_ref[2], modes).astype(BF)
-        potential = product(third, tab_ref[0])
-        factor = grouped_ref[pl.ds(at, QUAD * NX), :].astype(F32)
-        totals = []
-        for o in range(owns):
-            terms = potential[:, o * LANES:(o + 1) * LANES] * factor
-            totals.append(terms + pltpu.roll(terms, NZ, 1))
+        potential = product(third, tab_ref[3])
         for q in range(0, QUAD, LANES // NZ):
             off = (t * QUAD + q) * NZ
-            exchange = [
-                jnp.where(lane < NZ, x[q * NX:(q + 1) * NX], x[(q + 1) * NX:(q + 2) * NX])
-                for x in totals
+            factor = [
+                grouped_ref[pl.ds(at + (q + y) * NX, NX), :].astype(F32) for y in range(2)
             ]
-            if not final:
-                for o in range(owns):
-                    out_ref[o, :, pl.ds(off, LANES)] = exchange[o]
-                continue
-            exchange = [
-                exchange_fraction * (x + acc_ref[o, :, pl.ds(off, LANES)])
-                for o, x in enumerate(exchange)
-            ]
-            own = [own_tile(o, off, LANES) for o in range(owns)]
-            first = core == 0
-            own = jnp.where(first, own[0], own[1]).astype(F32)
-            keep_ref[:, pl.ds(off, LANES)] = own - jnp.where(first, exchange[0], exchange[1])
-            send_ref[:, pl.ds(off, LANES)] = (
-                jnp.where(first, exchange[1], exchange[0]).astype(send_ref.dtype))
+            for o in range(owns):
+                a, b = [
+                    potential[(q + y) * NX:(q + y + 1) * NX, o * LANES:(o + 1) * LANES] * factor[y]
+                    for y in range(2)
+                ]
+                exchange = jnp.where(low, a, b) + pltpu.roll(jnp.where(low, b, a), NZ, 1)
+                if not final:
+                    out_ref[o, :, pl.ds(off, LANES)] = exchange
+                    continue
+                exchange = exchange + acc_ref[o, :, pl.ds(off, LANES)]
+                if o == 0:
+                    keep_ref[:, pl.ds(off, LANES)] = own_tile(0, off).astype(F32) - exchange
+                else:
+                    send_ref[:, pl.ds(off, LANES)] = exchange.astype(send_ref.dtype)
 
     for step, trips in ((forward, NY // QUAD), (solve, NX // QUAD), (backward, NY // QUAD)):
         for t in range(trips):

time: 82.4 us -> 82.2 us (level)
  no operation moved by 1% of the time
where the time goes in v6:
time: 82.2 us; the launch traced here: 82 us
  blocking collectives  31.6 us (38%)
  starting transfers between devices  20.6 us (25%)
  waiting for transfers between devices  15.1 us (18%)
  Pallas kernels  12.8 us (16%)
  local copies, waits for them, and re-layouts  1.07 us (1%)
    all_to_all x1, blocking collectives, body(): cellwise = lax.all_to_all(updated, ('blk', 'grid'), 0, 0, tiled=True)  20.6 us
    ppermute x12, starting transfers between devices, exchanged(): lax.ppermute(x, axis, [(i, i ^ by) for i in range(lax.axis_size(axis)) if...  15.6 us
    all_to_all x1, blocking collectives, body(): parts = lax.all_to_all(local, ('blk', 'grid'), 0, 0, tiled=True)  11 us
    ppermute x12, waiting for transfers between devices, exchanged(): lax.ppermute(x, axis, [(i, i ^ by) for i in range(lax.axis_size(axis)) if...  9.16 us
    pallas_call x2, Pallas kernels, add_block(): pl.pallas_call(lambda *refs: block_kernel(slabs, final, refs), out_shape=...  8.8 us
    ppermute x3, waiting for transfers between devices, shifted(): lax.ppermute(x, 'blk', [(i, (i + 2) % blocks) for i in range(blocks)])  5.94 us
    ppermute x3, starting transfers between devices, shifted(): lax.ppermute(x, 'blk', [(i, (i + 2) % blocks) for i in range(blocks)])  4.98 us
    pallas_call x1, Pallas kernels, body(): pl.pallas_call(functools.partial(rotate_kernel, 1.0 / cell_count), out_sh...  2.37 us
  transfers between devices with their start and end apart: 15, of which 6 were waited for; matrix products, arithmetic and copies ran while one was open for 0% of the time, Pallas kernels for 6%

profile of v6, /device:TPU:0, one launch (start us, length us, event | category | flops | bytes accessed | tf_op | source)
XLA Modules:
  0.0 82.0 jit_solution(6356370691250640067)
XLA Ops:
  0.6 1.1 %constant_dynamic-slice_fusion = (bf16[2,16,4096]{2,1,0:T(8,128)(2,1)S(1)}, bf16[2,16,4096]{2,1,0:T(8,128)(2,1)S(1)}) fusion(bf16[4,16,4096]{2,1,0:T(8,128)(2,1)} %param.1, s32[]{:T(128)S(6)} %select_n.35, s32[]{:T(128)S(6)} %select_n.34), kind=kLoop, calls=%fused_computation.3 | loop fusion | bytes 1048584 | tf_op jit(solution)/shard_map/dynamic_slice | solution.py:321
  1.7 3.0 %collective-permute-start.1 = (bf16[2,16,4096]{2,1,0:T(8,128)(2,1)S(1)}, bf16[2,16,4096]{2,1,0:T(8,128)(2,1)S(1)}, u32[]{:S(2)}, u32[]{:S(2)}) collective-permute-start(bf16[2,16,4096]{2,1,0:T(8,128)(2,1)S(1)} %get-tuple-element.11.refs_0_), channel_id=1, source_target_pairs={{0,2},{1,3},{2,0},{3,1},{4,6},{5,7},{6,4},{7,5},{8,10},{9,11},{10,... | collective-permute-start | bytes 786440 | tf_op jit(solution)/shard_map/ppermute | solution.py:296
  4.8 0.0 collective-permute-start
  4.8 1.6 %collective-permute-start.6 = (bf16[2,16,4096]{2,1,0:T(8,128)(2,1)S(1)}, bf16[2,16,4096]{2,1,0:T(8,128)(2,1)S(1)}, u32[]{:S(2)}, u32[]{:S(2)}) collective-permute-start(bf16[2,16,4096]{2,1,0:T(8,128)(2,1)S(1)} %get-tuple-element.11.refs_0_), channel_id=1, source_target_pairs={{0,8},{4,12},{8,16},{12,20},{16,24},{20,28},{24,0},{28,4},{1,9},{5... | collective-permute-start | bytes 786440 | tf_op jit(solution)/shard_map/ppermute | solution.py:312
  6.3 2.1 %collective-permute-start.3 = (bf16[2,16,4096]{2,1,0:T(8,128)(2,1)S(1)}, bf16[2,16,4096]{2,1,0:T(8,128)(2,1)S(1)}, u32[]{:S(2)}, u32[]{:S(2)}) collective-permute-start(bf16[2,16,4096]{2,1,0:T(8,128)(2,1)S(1)} %get-tuple-element.11.refs_0_), channel_id=1, source_target_pairs={{0,1},{3,2},{4,5},{7,6},{8,9},{11,10},{12,13},{15,14},{16,17},{19,... | collective-permute-start | bytes 786440 | tf_op jit(solution)/shard_map/ppermute | solution.py:296
  8.5 0.8 shard_map.30
  9.3 1.8 %collective-permute-done.1.refs_2_ = bf16[2,16,4096]{2,1,0:T(8,128)(2,1)S(1)} collective-permute-done((bf16[2,16,4096]{2,1,0:T(8,128)(2,1)S(1)}, bf16[2,16,4096]{2,1,0:T(8,128)(2,1)S(1)}, u32[]{:S(2)}, u32[]{:S(2)}) %collective-permute-start.1) | collective-permute-done | bytes 262176 | tf_op jit(solution)/shard_map/ppermute | solution.py:296
  11.1 0.0 collective-permute-done.refs_1_
  11.1 1.8 %collective-permute-start.8 = (bf16[2,16,4096]{2,1,0:T(8,128)(2,1)S(1)}, bf16[2,16,4096]{2,1,0:T(8,128)(2,1)S(1)}, u32[]{:S(2)}, u32[]{:S(2)}) collective-permute-start(bf16[2,16,4096]{2,1,0:T(8,128)(2,1)S(1)} %collective-permute-done.refs_1_), channel_id=1, source_target_pairs={{0,8},{4,12},{8,16},{12,20},{16,24},{20,28},{24,0},{28,4},{1,9},{5... | collective-permute-start | bytes 786440 | tf_op jit(solution)/shard_map/ppermute | solution.py:312
  12.9 1.5 %collective-permute-start.2 = (bf16[2,16,4096]{2,1,0:T(8,128)(2,1)S(1)}, bf16[2,16,4096]{2,1,0:T(8,128)(2,1)S(1)}, u32[]{:S(2)}, u32[]{:S(2)}) collective-permute-start(bf16[2,16,4096]{2,1,0:T(8,128)(2,1)S(1)} %collective-permute-done.refs_1_), channel_id=1, source_target_pairs={{0,2},{1,3},{2,0},{3,1},{4,6},{5,7},{6,4},{7,5},{8,10},{9,11},{10,... | collective-permute-start | bytes 786440 | tf_op jit(solution)/shard_map/ppermute | solution.py:296
  14.4 1.6 %collective-permute-start.10 = (bf16[2,16,4096]{2,1,0:T(8,128)(2,1)S(1)}, bf16[2,16,4096]{2,1,0:T(8,128)(2,1)S(1)}, u32[]{:S(2)}, u32[]{:S(2)}) collective-permute-start(bf16[2,16,4096]{2,1,0:T(8,128)(2,1)S(1)} %collective-permute-done.1.refs_2_), channel_id=1, source_target_pairs={{0,8},{4,12},{8,16},{12,20},{16,24},{20,28},{24,0},{28,4},{1,9},{5... | collective-permute-start | bytes 786440 | tf_op jit(solution)/shard_map/ppermute | solution.py:312
  16.0 0.0 collective-permute-done.6.refs_8_
  16.0 1.3 %collective-permute-start.5 = (bf16[2,16,4096]{2,1,0:T(8,128)(2,1)S(1)}, bf16[2,16,4096]{2,1,0:T(8,128)(2,1)S(1)}, u32[]{:S(2)}, u32[]{:S(2)}) collective-permute-start(bf16[2,16,4096]{2,1,0:T(8,128)(2,1)S(1)} %collective-permute-done.1.refs_2_), channel_id=1, source_target_pairs={{0,1},{3,2},{4,5},{7,6},{8,9},{11,10},{12,13},{15,14},{16,17},{19,... | collective-permute-start | bytes 786440 | tf_op jit(solution)/shard_map/ppermute | solution.py:296
  17.3 4.8 %collective-permute-done.8.refs_9_ = bf16[2,16,4096]{2,1,0:T(8,128)(2,1)S(1)} collective-permute-done((bf16[2,16,4096]{2,1,0:T(8,128)(2,1)S(1)}, bf16[2,16,4096]{2,1,0:T(8,128)(2,1)S(1)}, u32[]{:S(2)}, u32[]{:S(2)}) %collective-permute-start.8) | collective-permute-done | bytes 262176 | tf_op jit(solution)/shard_map/ppermute | solution.py:312
  22.1 1.8 %collective-permute-start.9 = (bf16[2,16,4096]{2,1,0:T(8,128)(2,1)S(1)}, bf16[2,16,4096]{2,1,0:T(8,128)(2,1)S(1)}, u32[]{:S(2)}, u32[]{:S(2)}) collective-permute-start(bf16[2,16,4096]{2,1,0:T(8,128)(2,1)S(1)} %broadcast_select_fusion.1), channel_id=1, source_target_pairs={{0,4},{4,0},{8,12},{12,8},{16,20},{20,16},{24,28},{28,24},{1,5},{5... | collective-permute-start | bytes 786440 | tf_op jit(solution)/shard_map/ppermute | solution.py:296
  23.9 0.0 collective-permute-done.2.refs_3_
  23.9 1.5 %collective-permute-start.13 = (bf16[2,16,4096]{2,1,0:T(8,128)(2,1)S(1)}, bf16[2,16,4096]{2,1,0:T(8,128)(2,1)S(1)}, u32[]{:S(2)}, u32[]{:S(2)}) collective-permute-start(bf16[2,16,4096]{2,1,0:T(8,128)(2,1)S(1)} %collective-permute-done.8.refs_9_), channel_id=1, source_target_pairs={{0,2},{1,3},{2,0},{3,1},{4,6},{5,7},{6,4},{7,5},{8,10},{9,11},{10,... | collective-permute-start | bytes 786440 | tf_op jit(solution)/shard_map/ppermute | solution.py:296
  25.4 1.2 %collective-permute-done.10.refs_10_ = bf16[2,16,4096]{2,1,0:T(8,128)(2,1)S(1)} collective-permute-done((bf16[2,16,4096]{2,1,0:T(8,128)(2,1)S(1)}, bf16[2,16,4096]{2,1,0:T(8,128)(2,1)S(1)}, u32[]{:S(2)}, u32[]{:S(2)}) %collective-permute-start.10) | collective-permute-done | bytes 262176 | tf_op jit(solution)/shard_map/ppermute | solution.py:312
  26.6 1.3 %collective-permute-start.4 = (bf16[2,16,4096]{2,1,0:T(8,128)(2,1)S(1)}, bf16[2,16,4096]{2,1,0:T(8,128)(2,1)S(1)}, u32[]{:S(2)}, u32[]{:S(2)}) collective-permute-start(bf16[2,16,4096]{2,1,0:T(8,128)(2,1)S(1)} %collective-permute-done.2.refs_3_), channel_id=1, source_target_pairs={{0,1},{3,2},{4,5},{7,6},{8,9},{11,10},{12,13},{15,14},{16,17},{19,... | collective-permute-start | bytes 786440 | tf_op jit(solution)/shard_map/ppermute | solution.py:296
  27.9 0.0 collective-permute-done.3.refs_5_
  27.9 1.6 %collective-permute-start.7 = (bf16[2,16,4096]{2,1,0:T(8,128)(2,1)S(1)}, bf16[2,16,4096]{2,1,0:T(8,128)(2,1)S(1)}, u32[]{:S(2)}, u32[]{:S(2)}) collective-permute-start(bf16[2,16,4096]{2,1,0:T(8,128)(2,1)S(1)} %broadcast_select_fusion.2), channel_id=1, source_target_pairs={{0,4},{4,0},{8,12},{12,8},{16,20},{20,16},{24,28},{28,24},{1,5},{5... | collective-permute-start | bytes 786440 | tf_op jit(solution)/shard_map/ppermute | solution.py:296
  29.5 0.0 collective-permute-done.5.refs_7_
  29.5 0.5 collective-permute-start.11
  30.0 0.0 collective-permute-done.9.refs_9_
  30.0 0.9 %collective-permute-start.12 = (bf16[2,16,4096]{2,1,0:T(8,128)(2,1)S(1)}, bf16[2,16,4096]{2,1,0:T(8,128)(2,1)S(1)}, u32[]{:S(2)}, u32[]{:S(2)}) collective-permute-start(bf16[2,16,4096]{2,1,0:T(8,128)(2,1)S(1)} %collective-permute-done.9.refs_9_), channel_id=1, source_target_pairs={{0,2},{1,3},{2,0},{3,1},{4,6},{5,7},{6,4},{7,5},{8,10},{9,11},{10,... | collective-permute-start | bytes 786440 | tf_op jit(solution)/shard_map/ppermute | solution.py:296
  30.9 0.0 collective-permute-done.13.refs_11_
  30.9 0.0 collective-permute-done.4.refs_6_
  30.9 4.4 %shard_map.31.refs_14_ = f32[2,64,4096]{2,1,0:T(8,128)S(1)} custom-call(bf16[2,16,4096]{2,1,0:T(8,128)(2,1)S(1)} %get-tuple-element.11.refs_0_, bf16[2,16,4096]{2,1,0:T(8,128)(2,1)S(1)} %collective-permute-done.refs_1_, bf16[2,16,4096]{2,1,0:T(8,128)(2,1)S(1)} %collective-permute-done.1.refs_2_, bf16[2,16,4096]{2,1,0:T(8,128)(2,1)S(1)} %collective-permute-done.2.refs_3_, ...), custom_call_target="tpu_custom_call" | custom-call | flops 3221225472 | bytes 8388608 | tf_op jit(solution)/shard_map/pallas_call | solution.py:209
  35.3 1.9 %collective-permute-done.7.refs_8_ = bf16[2,16,4096]{2,1,0:T(8,128)(2,1)S(1)} collective-permute-done((bf16[2,16,4096]{2,1,0:T(8,128)(2,1)S(1)}, bf16[2,16,4096]{2,1,0:T(8,128)(2,1)S(1)}, u32[]{:S(2)}, u32[]{:S(2)}) %collective-permute-start.7) | collective-permute-done | bytes 262176 | tf_op jit(solution)/shard_map/ppermute | solution.py:296
  37.2 3.6 %collective-permute-done.11.refs_10_ = bf16[2,16,4096]{2,1,0:T(8,128)(2,1)S(1)} collective-permute-done((bf16[2,16,4096]{2,1,0:T(8,128)(2,1)S(1)}, bf16[2,16,4096]{2,1,0:T(8,128)(2,1)S(1)}, u32[]{:S(2)}, u32[]{:S(2)}) %collective-permute-start.11) | collective-permute-done | bytes 262176 | tf_op jit(solution)/shard_map/ppermute | solution.py:296
  40.8 0.0 collective-permute-done.12.refs_11_
  40.8 4.4 %shard_map.32 = (f32[64,4096]{1,0:T(8,128)S(1)}, bf16[64,4096]{1,0:T(8,128)(2,1)S(1)}) custom-call(bf16[2,16,4096]{2,1,0:T(8,128)(2,1)S(1)} %get-tuple-element.11.refs_0_, bf16[2,16,4096]{2,1,0:T(8,128)(2,1)S(1)} %collective-permute-done.refs_1_, bf16[2,16,4096]{2,1,0:T(8,128)(2,1)S(1)} %collective-permute-done.1.refs_2_, ...), custom_call_target="tpu_custom_call" | custom-call | flops 3221225472 | bytes 8388608 | tf_op jit(solution)/shard_map/pallas_call | solution.py:209
  45.2 0.1 collective-permute-start.14
  45.3 1.9 %collective-permute-done.14.part_ref = bf16[64,4096]{1,0:T(8,128)(2,1)S(1)} collective-permute-done((bf16[64,4096]{1,0:T(8,128)(2,1)S(1)}, bf16[64,4096]{1,0:T(8,128)(2,1)S(1)}, u32[]{:S(2)}, u32[]{:S(2)}) %collective-permute-start.14) | collective-permute-done | bytes 524320 | tf_op jit(solution)/shard_map/ppermute | solution.py:296
  47.2 0.1 shard_map.33
  47.3 20.6 %all_to_all.10.x_ref = bf16[32,16,512]{2,1,0:T(8,128)(2,1)S(1)} all-to-all(bf16[32,16,512]{2,1,0:T(8,128)(2,1)S(1)} %bitcast.1), channel_id=1, replica_groups=mesh['blk'=8,'grid'=4] {'blk','grid'}, dimensions={0} | all-to-all | bytes 1048576 | tf_op jit(solution)/shard_map/all_to_all | solution.py:351
  67.9 0.7 shard_map.34
  68.6 11.0 %all_to_all.11.parts_ref = f32[32,8,128]{2,1,0:T(8,128)S(1)} all-to-all(f32[32,8,128]{2,1,0:T(8,128)S(1)} %shard_map.34), channel_id=1, replica_groups=mesh['blk'=8,'grid'=4] {'blk','grid'}, dimensions={0} | all-to-all | bytes 262144 | tf_op jit(solution)/shard_map/all_to_all | solution.py:363
  79.6 2.4 %shard_map.35 = (bf16[32,16,512]{2,1,0:T(8,128)(2,1)}, f32[32,32]{1,0:T(8,128)}) custom-call(f32[32,8,128]{2,1,0:T(8,128)S(1)} %all_to_all.11.parts_ref, bf16[32,16,512]{2,1,0:T(8,128)(2,1)S(1)} %all_to_all.10.x_ref), custom_call_target="tpu_custom_call" | custom-call | tf_op jit(solution)/shard_map/pallas_call | solution.py:364
  (3 shorter events, 0.1 us)
Async XLA Ops:
  1.7 9.3 %collective-permute-start.1 = (bf16[2,16,4096]{2,1,0:T(8,128)(2,1)S(1)}, bf16[2,16,4096]{2,1,0:T(8,128)(2,1)S(1)}, u32[]{:S(2)}, u32[]{:S(2)}) collective-permute-start(bf16[2,16,4096]{2,1,0:T(8,128)(2,1)S(1)} %get-tuple-element.11.refs_0_), channel_id=1, source_target_pairs={{0,2},{1,3},{2,0},{3,1},{4,6},{5,7},{6,4},{7,5},{8,10},{9,11},{10,... | collective-permute-start | bytes 786440 | tf_op jit(solution)/shard_map/ppermute | solution.py:296
  4.8 6.3 %collective-permute-start = (bf16[2,16,4096]{2,1,0:T(8,128)(2,1)S(1)}, bf16[2,16,4096]{2,1,0:T(8,128)(2,1)S(1)}, u32[]{:S(2)}, u32[]{:S(2)}) collective-permute-start(bf16[2,16,4096]{2,1,0:T(8,128)(2,1)S(1)} %get-tuple-element.12.refs_4_), channel_id=1, source_target_pairs={{0,1},{1,0},{2,3},{3,2},{4,5},{5,4},{6,7},{7,6},{8,9},{9,8},{10,11... | collective-permute-start | bytes 786440 | tf_op jit(solution)/shard_map/ppermute | solution.py:296
  4.8 11.2 %collective-permute-start.6 = (bf16[2,16,4096]{2,1,0:T(8,128)(2,1)S(1)}, bf16[2,16,4096]{2,1,0:T(8,128)(2,1)S(1)}, u32[]{:S(2)}, u32[]{:S(2)}) collective-permute-start(bf16[2,16,4096]{2,1,0:T(8,128)(2,1)S(1)} %get-tuple-element.11.refs_0_), channel_id=1, source_target_pairs={{0,8},{4,12},{8,16},{12,20},{16,24},{20,28},{24,0},{28,4},{1,9},{5... | collective-permute-start | bytes 786440 | tf_op jit(solution)/shard_map/ppermute | solution.py:312
  6.3 21.6 %collective-permute-start.3 = (bf16[2,16,4096]{2,1,0:T(8,128)(2,1)S(1)}, bf16[2,16,4096]{2,1,0:T(8,128)(2,1)S(1)}, u32[]{:S(2)}, u32[]{:S(2)}) collective-permute-start(bf16[2,16,4096]{2,1,0:T(8,128)(2,1)S(1)} %get-tuple-element.11.refs_0_), channel_id=1, source_target_pairs={{0,1},{3,2},{4,5},{7,6},{8,9},{11,10},{12,13},{15,14},{16,17},{19,... | collective-permute-start | bytes 786440 | tf_op jit(solution)/shard_map/ppermute | solution.py:296
  11.1 11.0 %collective-permute-start.8 = (bf16[2,16,4096]{2,1,0:T(8,128)(2,1)S(1)}, bf16[2,16,4096]{2,1,0:T(8,128)(2,1)S(1)}, u32[]{:S(2)}, u32[]{:S(2)}) collective-permute-start(bf16[2,16,4096]{2,1,0:T(8,128)(2,1)S(1)} %collective-permute-done.refs_1_), channel_id=1, source_target_pairs={{0,8},{4,12},{8,16},{12,20},{16,24},{20,28},{24,0},{28,4},{1,9},{5... | collective-permute-start | bytes 786440 | tf_op jit(solution)/shard_map/ppermute | solution.py:312
  12.9 11.0 %collective-permute-start.2 = (bf16[2,16,4096]{2,1,0:T(8,128)(2,1)S(1)}, bf16[2,16,4096]{2,1,0:T(8,128)(2,1)S(1)}, u32[]{:S(2)}, u32[]{:S(2)}) collective-permute-start(bf16[2,16,4096]{2,1,0:T(8,128)(2,1)S(1)} %collective-permute-done.refs_1_), channel_id=1, source_target_pairs={{0,2},{1,3},{2,0},{3,1},{4,6},{5,7},{6,4},{7,5},{8,10},{9,11},{10,... | collective-permute-start | bytes 786440 | tf_op jit(solution)/shard_map/ppermute | solution.py:296
  14.4 12.2 %collective-permute-start.10 = (bf16[2,16,4096]{2,1,0:T(8,128)(2,1)S(1)}, bf16[2,16,4096]{2,1,0:T(8,128)(2,1)S(1)}, u32[]{:S(2)}, u32[]{:S(2)}) collective-permute-start(bf16[2,16,4096]{2,1,0:T(8,128)(2,1)S(1)} %collective-permute-done.1.refs_2_), channel_id=1, source_target_pairs={{0,8},{4,12},{8,16},{12,20},{16,24},{20,28},{24,0},{28,4},{1,9},{5... | collective-permute-start | bytes 786440 | tf_op jit(solution)/shard_map/ppermute | solution.py:312
  16.0 13.5 %collective-permute-start.5 = (bf16[2,16,4096]{2,1,0:T(8,128)(2,1)S(1)}, bf16[2,16,4096]{2,1,0:T(8,128)(2,1)S(1)}, u32[]{:S(2)}, u32[]{:S(2)}) collective-permute-start(bf16[2,16,4096]{2,1,0:T(8,128)(2,1)S(1)} %collective-permute-done.1.refs_2_), channel_id=1, source_target_pairs={{0,1},{3,2},{4,5},{7,6},{8,9},{11,10},{12,13},{15,14},{16,17},{19,... | collective-permute-start | bytes 786440 | tf_op jit(solution)/shard_map/ppermute | solution.py:296
  22.1 7.9 %collective-permute-start.9 = (bf16[2,16,4096]{2,1,0:T(8,128)(2,1)S(1)}, bf16[2,16,4096]{2,1,0:T(8,128)(2,1)S(1)}, u32[]{:S(2)}, u32[]{:S(2)}) collective-permute-start(bf16[2,16,4096]{2,1,0:T(8,128)(2,1)S(1)} %broadcast_select_fusion.1), channel_id=1, source_target_pairs={{0,4},{4,0},{8,12},{12,8},{16,20},{20,16},{24,28},{28,24},{1,5},{5... | collective-permute-start | bytes 786440 | tf_op jit(solution)/shard_map/ppermute | solution.py:296
  23.9 7.0 %collective-permute-start.13 = (bf16[2,16,4096]{2,1,0:T(8,128)(2,1)S(1)}, bf16[2,16,4096]{2,1,0:T(8,128)(2,1)S(1)}, u32[]{:S(2)}, u32[]{:S(2)}) collective-permute-start(bf16[2,16,4096]{2,1,0:T(8,128)(2,1)S(1)} %collective-permute-done.8.refs_9_), channel_id=1, source_target_pairs={{0,2},{1,3},{2,0},{3,1},{4,6},{5,7},{6,4},{7,5},{8,10},{9,11},{10,... | collective-permute-start | bytes 786440 | tf_op jit(solution)/shard_map/ppermute | solution.py:296
  26.6 4.3 %collective-permute-start.4 = (bf16[2,16,4096]{2,1,0:T(8,128)(2,1)S(1)}, bf16[2,16,4096]{2,1,0:T(8,128)(2,1)S(1)}, u32[]{:S(2)}, u32[]{:S(2)}) collective-permute-start(bf16[2,16,4096]{2,1,0:T(8,128)(2,1)S(1)} %collective-permute-done.2.refs_3_), channel_id=1, source_target_pairs={{0,1},{3,2},{4,5},{7,6},{8,9},{11,10},{12,13},{15,14},{16,17},{19,... | collective-permute-start | bytes 786440 | tf_op jit(solution)/shard_map/ppermute | solution.py:296
  27.9 9.2 %collective-permute-start.7 = (bf16[2,16,4096]{2,1,0:T(8,128)(2,1)S(1)}, bf16[2,16,4096]{2,1,0:T(8,128)(2,1)S(1)}, u32[]{:S(2)}, u32[]{:S(2)}) collective-permute-start(bf16[2,16,4096]{2,1,0:T(8,128)(2,1)S(1)} %broadcast_select_fusion.2), channel_id=1, source_target_pairs={{0,4},{4,0},{8,12},{12,8},{16,20},{20,16},{24,28},{28,24},{1,5},{5... | collective-permute-start | bytes 786440 | tf_op jit(solution)/shard_map/ppermute | solution.py:296
  29.5 11.3 %collective-permute-start.11 = (bf16[2,16,4096]{2,1,0:T(8,128)(2,1)S(1)}, bf16[2,16,4096]{2,1,0:T(8,128)(2,1)S(1)}, u32[]{:S(2)}, u32[]{:S(2)}) collective-permute-start(bf16[2,16,4096]{2,1,0:T(8,128)(2,1)S(1)} %broadcast_select_fusion), channel_id=1, source_target_pairs={{0,4},{4,0},{8,12},{12,8},{16,20},{20,16},{24,28},{28,24},{1,5},{5... | collective-permute-start | bytes 786440 | tf_op jit(solution)/shard_map/ppermute | solution.py:296
  30.0 10.8 %collective-permute-start.12 = (bf16[2,16,4096]{2,1,0:T(8,128)(2,1)S(1)}, bf16[2,16,4096]{2,1,0:T(8,128)(2,1)S(1)}, u32[]{:S(2)}, u32[]{:S(2)}) collective-permute-start(bf16[2,16,4096]{2,1,0:T(8,128)(2,1)S(1)} %collective-permute-done.9.refs_9_), channel_id=1, source_target_pairs={{0,2},{1,3},{2,0},{3,1},{4,6},{5,7},{6,4},{7,5},{8,10},{9,11},{10,... | collective-permute-start | bytes 786440 | tf_op jit(solution)/shard_map/ppermute | solution.py:296
  45.2 2.0 %collective-permute-start.14 = (bf16[64,4096]{1,0:T(8,128)(2,1)S(1)}, bf16[64,4096]{1,0:T(8,128)(2,1)S(1)}, u32[]{:S(2)}, u32[]{:S(2)}) collective-permute-start(bf16[64,4096]{1,0:T(8,128)(2,1)S(1)} %get-tuple-element.19), channel_id=1, source_target_pairs={{0,1},{1,0},{2,3},{3,2},{4,5},{5,4},{6,7},{7,6},{8,9},{9,8},{10,11... | collective-permute-start | bytes 1572872 | tf_op jit(solution)/shard_map/ppermute | solution.py:296
